TPU v7x, 32 devices: a whole 2x2x4 slice. The times are simulated.
32 devices in a mesh: dp: 4 (over z), row: 2 (over y), col: 4 (over x, core).
Axes of the slice: x: 2, y: 2, z: 4, core: 2. Of those that a mesh axis runs over, the one named last changes fastest.
Arguments:
- block_in: bfloat16 [4, 1024, 2048], P('dp', None, ('row', 'col')), may hold values from -6 to 6
- segment_ids: int32 [4, 1024], P('dp'), may hold values from 0 to 3, never falling along the last dimension, each value on 1 to 512 neighbouring positions
- block_cotangent: bfloat16 [4, 1024, 2048], P('dp', None, ('row', 'col')), may hold values from -6 to 6
- query_weight: bfloat16 [2048, 2048], P('row', 'col'), may hold values from -0.125 to 0.125
- key_weight: bfloat16 [2048, 2048], P('row', 'col'), may hold values from -0.125 to 0.125
- value_weight: bfloat16 [2048, 4096], P('row', 'col'), may hold values from -0.125 to 0.125
- swish_weight: bfloat16 [2048, 4096], P('row', 'col'), may hold values from -0.125 to 0.125
- output_weight: bfloat16 [4096, 2048], P('col', 'row'), may hold values from -0.1875 to 0.1875
- gelu_weight: bfloat16 [2048, 4096], P('row', 'col'), may hold values from -0.125 to 0.125
- up_weight: bfloat16 [2048, 4096], P('row', 'col'), may hold values from -0.125 to 0.125
- down_weight: bfloat16 [4096, 2048], P('col', 'row'), may hold values from -0.1875 to 0.1875
- first_gain: float32 [2048], P(('row', 'col')), may hold values from 0.25 to 1.75
- second_gain: float32 [2048], P(('row', 'col')), may hold values from 0.25 to 1.75
Outputs:
- block_out: bfloat16 [4, 1024, 2048], P('dp', None, ('row', 'col'))
- grad_input: bfloat16 [4, 1024, 2048], P('dp', None, ('row', 'col'))
- grad_query: float32 [2048, 2048], P('row', 'col')
- grad_key: float32 [2048, 2048], P('row', 'col')
- grad_value: float32 [2048, 4096], P('row', 'col')
- grad_swish: float32 [2048, 4096], P('row', 'col')
- grad_output: float32 [4096, 2048], P('col', 'row')
- grad_gelu: float32 [2048, 4096], P('row', 'col')
- grad_up: float32 [2048, 4096], P('row', 'col')
- grad_down: float32 [4096, 2048], P('col', 'row')
- grad_first: float32 [2048], P(('row', 'col'))
- grad_second: float32 [2048], P(('row', 'col'))
Inputs may be any that keep to these rules, and one draw needn't show every extreme that they name: `segment_ids`: in each pack the ids never fall; each of the 4 documents has 1 to 512 tokens, and one has exactly 512.
All inputs are finite; a program needn't handle non-finite values.
Results may differ from a plain program's by a relative error of at most 0.017.
Values may be sent and summed in bfloat16 or wider, within the bound.
A program may use at most 192 MiB of HBM per device.

v0:
```python
import jax
import jax.numpy as jnp
from jax import lax
from jax.sharding import PartitionSpec as P

D = 2048
KD = 256
QBLK = 512


epsilon = 1e-06


def rotate_half(values):
    half_cols = values.shape[-1] // 2
    return jnp.concatenate([-values[:, half_cols:], values[:, :half_cols]], axis=-1)


def rotary_tables(length, columns):
    half_cols = columns // 2
    frequency = 10000.0 ** (-jnp.arange(half_cols, dtype=jnp.float32) / half_cols)
    angles = jnp.arange(length, dtype=jnp.float32)[:, None] * frequency[None, :]
    cosine_half = jnp.cos(angles)
    sine_half = jnp.sin(angles)
    return (
        jnp.concatenate([cosine_half, cosine_half], axis=1),
        jnp.concatenate([sine_half, sine_half], axis=1),
    )


def decay_block(segments, row_start, row_count, column_count, log_decay):
    query_pos = row_start + jnp.arange(row_count, dtype=jnp.int32)
    key_pos = jnp.arange(column_count, dtype=jnp.int32)
    distance = query_pos[:, None] - key_pos[None, :]
    same_doc = (
        segments[row_start : row_start + row_count][:, None] == segments[:column_count][None, :]
    )
    keep_mask = (distance >= 0) & same_doc
    return jnp.where(
        keep_mask, jnp.exp(jnp.maximum(distance, 0).astype(jnp.float32) * log_decay), 0.0
    )


def row_total(values):
    return lax.psum(jnp.sum(values, axis=1), ("row", "col"))


def widen_norm(values):
    return lax.all_gather(values, "col", axis=1, tiled=True)


def widen_out(values):
    return lax.all_gather(values, "row", axis=1, tiled=True)


def reduce_out(partial_sum):
    return lax.psum_scatter(partial_sum, "col", scatter_dimension=1, tiled=True)


def widen_grad(values):
    return lax.all_gather(values, "col", axis=1, tiled=True)


def reduce_grad(partial_sum):
    return lax.psum_scatter(partial_sum, "row", scatter_dimension=1, tiled=True)


def reduce_input(partial_sum):
    return lax.psum_scatter(partial_sum, "col", scatter_dimension=1, tiled=True)


def matmul(left, right):
    return jnp.dot(left, right, preferred_element_type=jnp.float32)


def weight_grad(inputs, grads):
    return jnp.einsum("tk,tf->kf", inputs, grads, preferred_element_type=jnp.float32)


def back_product(grads, weights):
    return jnp.einsum("tf,kf->tk", grads, weights, preferred_element_type=jnp.float32)


def norm_back(values, scale, gain, normed_grad):
    gain_grad = jnp.sum(normed_grad * values * scale, axis=0)
    inner = row_total(normed_grad * gain * values)[:, None]
    value_grad = scale * gain * normed_grad - values * scale**3 * inner / D
    return (value_grad, gain_grad)


def group_norm(retained):
    spread = jnp.sqrt(jnp.mean(retained * retained, axis=1, keepdims=True) + epsilon)
    return retained / jnp.maximum(spread, 1.0)


def swish_gate(swish_sum, grouped):
    return jax.nn.silu(swish_sum) * grouped


def gelu_gate(gelu_sum, up_sum):
    return jax.nn.gelu(gelu_sum) * up_sum


def shards(
    block_in,
    segment_ids,
    block_cotangent,
    query_weight,
    key_weight,
    value_weight,
    swish_weight,
    output_weight,
    gelu_weight,
    up_weight,
    down_weight,
    first_gain,
    second_gain,
):
    hidden = block_in[0].astype(jnp.float32)
    segments = segment_ids[0]
    tokens = hidden.shape[0]
    head_index = lax.axis_index("col") * lax.axis_size("row") + lax.axis_index("row")
    log_decay = jnp.log(1.0 - 2.0 ** (-5.0 - head_index.astype(jnp.float32)))
    cosine_table, sine_table = rotary_tables(tokens, KD)
    block_count = tokens // QBLK
    scale_one = lax.rsqrt(row_total(hidden * hidden)[:, None] / D + epsilon)
    normed_one = (hidden * scale_one * first_gain).astype(jnp.bfloat16)
    wide_one = widen_norm(normed_one)
    query_sum, key_sum, value_sum, swish_sum = (
        lax.psum_scatter(matmul(wide_one, query_weight), "row", scatter_dimension=1, tiled=True),
        lax.psum_scatter(matmul(wide_one, key_weight), "row", scatter_dimension=1, tiled=True),
        lax.psum_scatter(matmul(wide_one, value_weight), "row", scatter_dimension=1, tiled=True),
        lax.psum_scatter(matmul(wide_one, swish_weight), "row", scatter_dimension=1, tiled=True),
    )
    query_low = (query_sum * cosine_table + rotate_half(query_sum) * sine_table).astype(
        jnp.bfloat16
    )
    key_low = ((key_sum * cosine_table + rotate_half(key_sum) * sine_table) * KD ** (-0.5)).astype(
        jnp.bfloat16
    )
    value_low = value_sum.astype(jnp.bfloat16)
    outputs = []
    for block_num in range(block_count):
        start = block_num * QBLK
        stop = start + QBLK
        decay = decay_block(segments, start, QBLK, stop, log_decay)
        scores = jnp.einsum(
            "qd,kd->qk", query_low[start:stop], key_low[:stop], preferred_element_type=jnp.float32
        )
        weights_low = (scores * decay).astype(jnp.bfloat16)
        outputs.append(matmul(weights_low, value_low[:stop]))
    retained = jnp.concatenate(outputs, axis=0)
    grouped, group_pull = jax.vjp(group_norm, retained)
    gated_full, swish_pull = jax.vjp(swish_gate, swish_sum, grouped)
    gated = gated_full.astype(jnp.bfloat16)
    wide_gated = widen_out(gated)
    attended = reduce_out(matmul(wide_gated, output_weight))
    middle = hidden + attended
    scale_two = lax.rsqrt(row_total(middle * middle)[:, None] / D + epsilon)
    normed_two = (middle * scale_two * second_gain).astype(jnp.bfloat16)
    wide_two = widen_norm(normed_two)
    gelu_sum, up_sum = (
        lax.psum_scatter(matmul(wide_two, gelu_weight), "row", scatter_dimension=1, tiled=True),
        lax.psum_scatter(matmul(wide_two, up_weight), "row", scatter_dimension=1, tiled=True),
    )
    product_full, gelu_pull = jax.vjp(gelu_gate, gelu_sum, up_sum)
    product = product_full.astype(jnp.bfloat16)
    wide_product = widen_out(product)
    feed = reduce_out(matmul(wide_product, down_weight))
    block_out = (middle + feed).astype(jnp.bfloat16)
    upstream = block_cotangent[0].astype(jnp.float32)
    wide_feed_grad = widen_grad(upstream.astype(jnp.bfloat16))
    grad_down = weight_grad(wide_product, wide_feed_grad)
    product_grad = reduce_grad(back_product(wide_feed_grad, down_weight))
    gelu_grad, up_grad = gelu_pull(product_grad)
    wide_gelu_grad, wide_up_grad = (
        lax.all_gather(gelu_grad.astype(jnp.bfloat16), "row", axis=1, tiled=True),
        lax.all_gather(up_grad.astype(jnp.bfloat16), "row", axis=1, tiled=True),
    )
    grad_gelu = weight_grad(wide_two, wide_gelu_grad)
    grad_up = weight_grad(wide_two, wide_up_grad)
    normed_two_grad = reduce_input(
        back_product(wide_gelu_grad, gelu_weight) + back_product(wide_up_grad, up_weight)
    )
    middle_part, grad_second = norm_back(middle, scale_two, second_gain, normed_two_grad)
    middle_grad = upstream + middle_part
    wide_attended_grad = widen_grad(middle_grad.astype(jnp.bfloat16))
    grad_output = weight_grad(wide_gated, wide_attended_grad)
    gated_grad = reduce_grad(back_product(wide_attended_grad, output_weight))
    swish_grad, grouped_grad = swish_pull(gated_grad)
    (retained_grad,) = group_pull(grouped_grad)
    retained_low = retained_grad.astype(jnp.bfloat16)
    key_accum = jnp.zeros((tokens, key_low.shape[1]), jnp.float32)
    value_accum = jnp.zeros((tokens, value_low.shape[1]), jnp.float32)
    query_parts = []
    for block_num in range(block_count):
        start = block_num * QBLK
        stop = start + QBLK
        decay = decay_block(segments, start, QBLK, stop, log_decay)
        scores = jnp.einsum(
            "qd,kd->qk", query_low[start:stop], key_low[:stop], preferred_element_type=jnp.float32
        )
        weights_low = (scores * decay).astype(jnp.bfloat16)
        weights_grad = jnp.einsum(
            "qv,kv->qk",
            retained_low[start:stop],
            value_low[:stop],
            preferred_element_type=jnp.float32,
        )
        scores_low = (weights_grad * decay).astype(jnp.bfloat16)
        query_parts.append(matmul(scores_low, key_low[:stop]))
        key_accum = key_accum.at[:stop].add(
            jnp.einsum(
                "qk,qd->kd", scores_low, query_low[start:stop], preferred_element_type=jnp.float32
            )
        )
        value_accum = value_accum.at[:stop].add(
            jnp.einsum(
                "qk,qv->kv",
                weights_low,
                retained_low[start:stop],
                preferred_element_type=jnp.float32,
            )
        )
    query_grad = jnp.concatenate(query_parts, axis=0)
    key_scaled = key_accum * KD ** (-0.5)
    query_back = (query_grad * cosine_table - rotate_half(query_grad) * sine_table).astype(
        jnp.bfloat16
    )
    key_back = (key_scaled * cosine_table - rotate_half(key_scaled) * sine_table).astype(
        jnp.bfloat16
    )
    value_back = value_accum.astype(jnp.bfloat16)
    swish_back = swish_grad.astype(jnp.bfloat16)
    wide_query, wide_key, wide_value, wide_swish = (
        lax.all_gather(query_back, "row", axis=1, tiled=True),
        lax.all_gather(key_back, "row", axis=1, tiled=True),
        lax.all_gather(value_back, "row", axis=1, tiled=True),
        lax.all_gather(swish_back, "row", axis=1, tiled=True),
    )
    grad_query = weight_grad(wide_one, wide_query)
    grad_key = weight_grad(wide_one, wide_key)
    grad_value = weight_grad(wide_one, wide_value)
    grad_swish = weight_grad(wide_one, wide_swish)
    normed_one_grad = reduce_input(
        back_product(wide_query, query_weight)
        + back_product(wide_key, key_weight)
        + back_product(wide_value, value_weight)
        + back_product(wide_swish, swish_weight)
    )
    input_part, grad_first = norm_back(hidden, scale_one, first_gain, normed_one_grad)
    grad_input = (middle_grad + input_part).astype(jnp.bfloat16)
    (
        grad_query,
        grad_key,
        grad_value,
        grad_swish,
        grad_output,
        grad_gelu,
        grad_up,
        grad_down,
        grad_first,
        grad_second,
    ) = lax.psum(
        (
            grad_query,
            grad_key,
            grad_value,
            grad_swish,
            grad_output,
            grad_gelu,
            grad_up,
            grad_down,
            grad_first,
            grad_second,
        ),
        "dp",
    )
    return (
        block_out[None],
        grad_input[None],
        grad_query,
        grad_key,
        grad_value,
        grad_swish,
        grad_output,
        grad_gelu,
        grad_up,
        grad_down,
        grad_first,
        grad_second,
    )


def solution(mesh):
    return jax.shard_map(
        shards,
        mesh=mesh,
        in_specs=(
            P("dp", None, ("row", "col")),
            P("dp", None),
            P("dp", None, ("row", "col")),
            P("row", "col"),
            P("row", "col"),
            P("row", "col"),
            P("row", "col"),
            P("col", "row"),
            P("row", "col"),
            P("row", "col"),
            P("col", "row"),
            P(("row", "col")),
            P(("row", "col")),
        ),
        out_specs=(
            P("dp", None, ("row", "col")),
            P("dp", None, ("row", "col")),
            P("row", "col"),
            P("row", "col"),
            P("row", "col"),
            P("row", "col"),
            P("col", "row"),
            P("row", "col"),
            P("row", "col"),
            P("col", "row"),
            P(("row", "col")),
            P(("row", "col")),
        ),
        check_vma=False,
    )
```

profile of v0, /device:TPU:0, one launch (start us, length us, event | category | flops | bytes accessed | tf_op | source)
XLA Modules:
  0.0 2021.4 jit_solution(7381359288320375753)
XLA Ops:
  8.6 15.2 psum.98
  25.9 22.3 %all-gather.14.cloned.1.call-done = bf16[1024,1024]{1,0:T(8,128)(2,1)} async-done(((bf16[1024,256]{1,0:T(8,128)(2,1)}), bf16[1024,1024]{1,0:T(8,128)(2,1)}) %all-gather.14.cloned.1.call-update) | async-done | bytes 2097168 | tf_op jit(solution)/shard_map/all_gather | solution.py:49
  48.2 4.4 fusion.77
  53.9 4.2 fusion.78
  58.1 7.1 fusion.79
  65.3 6.6 fusion.76
  74.5 10.2 reduce-scatter.15.cloned.1.call-done
  84.7 2.2 slice_negate_fusion.2
  87.0 32.5 %reduce-scatter.17.cloned.1.call-done = f32[1024,256]{1,0:T(8,128)} async-done(((f32[1024,512]{1,0:T(8,128)}), f32[1024,256]{1,0:T(8,128)}) %reduce-scatter.17.cloned.1.call-update) | async-done | bytes 1048592 | tf_op jit(solution)/shard_map/reduce_scatter | solution.py:131
  126.3 50.3 %reduce-scatter.19.cloned.1.call-done = f32[1024,512]{1,0:T(8,128)} async-done(((f32[1024,1024]{1,0:T(8,128)}), f32[1024,512]{1,0:T(8,128)}) %reduce-scatter.19.cloned.1.call-update) | async-done | bytes 2097168 | tf_op jit(solution)/shard_map/reduce_scatter | solution.py:132
  180.9 52.9 %reduce-scatter.13.cloned.1.call-done = f32[1024,512]{1,0:T(8,128)} async-done(((f32[1024,1024]{1,0:T(8,128)}), f32[1024,512]{1,0:T(8,128)}) %reduce-scatter.13.cloned.1.call-update) | async-done | bytes 2097168 | tf_op jit(solution)/shard_map/reduce_scatter | solution.py:133
  233.7 3.6 multiply_convert_fusion.3
  237.6 33.0 %all-gather.16.cloned.1.call-done = bf16[1024,1024]{1,0:T(8,128)(2,1)} async-done(((bf16[1024,512]{1,0:T(8,128)(2,1)}), bf16[1024,1024]{1,0:T(8,128)(2,1)}) %all-gather.16.cloned.1.call-update) | async-done | bytes 2097168 | tf_op jit(solution)/shard_map/all_gather | solution.py:53
  270.6 6.6 fusion.81
  278.0 43.7 %reduce-scatter.21.cloned.1.call-done = f32[1024,256]{1,0:T(8,128)} async-done(((f32[1024,1024]{1,0:T(8,128)}), f32[1024,256]{1,0:T(8,128)}) %reduce-scatter.21.cloned.1.call-update) | async-done | bytes 1048592 | tf_op jit(solution)/shard_map/reduce_scatter | solution.py:57
  321.8 2.5 multiply_reduce_fusion.4
  324.2 12.9 psum.99
  337.2 2.2 multiply_convert_fusion.5
  339.5 6.8 all-gather.36.cloned.1.call-done
  346.2 6.6 fusion.13
  352.9 18.3 all-gather.18.cloned.1.call-done
  371.3 5.9 fusion.82
  377.3 6.6 fusion.83
  383.9 44.5 %reduce-scatter.29.cloned.1.call-done = f32[1024,512]{1,0:T(8,128)} async-done(((f32[1024,1024]{1,0:T(8,128)}), f32[1024,512]{1,0:T(8,128)}) %reduce-scatter.29.cloned.1.call-update) | async-done | bytes 2097168 | tf_op jit(solution)/shard_map/reduce_scatter | solution.py:65
  428.4 57.3 %reduce-scatter.23.cloned.1.call-done = f32[1024,512]{1,0:T(8,128)} async-done(((f32[1024,1024]{1,0:T(8,128)}), f32[1024,512]{1,0:T(8,128)}) %reduce-scatter.23.cloned.1.call-update) | async-done | bytes 2097168 | tf_op jit(solution)/shard_map/reduce_scatter | solution.py:163
  485.7 57.1 %reduce-scatter.25.cloned.1.call-done = f32[1024,512]{1,0:T(8,128)} async-done(((f32[1024,1024]{1,0:T(8,128)}), f32[1024,512]{1,0:T(8,128)}) %reduce-scatter.25.cloned.1.call-update) | async-done | bytes 2097168 | tf_op jit(solution)/shard_map/reduce_scatter | solution.py:164
  542.8 5.3 multiply_convert_fusion.1
  549.8 31.6 %all-gather.22.cloned.1.call-done = bf16[1024,1024]{1,0:T(8,128)(2,1)} async-done(((bf16[1024,512]{1,0:T(8,128)(2,1)}), bf16[1024,1024]{1,0:T(8,128)(2,1)}) %all-gather.22.cloned.1.call-update) | async-done | bytes 2097168 | tf_op jit(solution)/shard_map/all_gather | solution.py:177
  581.4 6.0 fusion.85
  587.4 29.1 %all-gather.24.cloned.1.call-done = bf16[1024,1024]{1,0:T(8,128)(2,1)} async-done(((bf16[1024,512]{1,0:T(8,128)(2,1)}), bf16[1024,1024]{1,0:T(8,128)(2,1)}) %all-gather.24.cloned.1.call-update) | async-done | bytes 2097168 | tf_op jit(solution)/shard_map/all_gather | solution.py:178
  616.5 7.8 convolution_add_fusion
  624.4 27.2 %all-gather.20.cloned.1.call-done = bf16[1024,1024]{1,0:T(8,128)(2,1)} async-done(((bf16[1024,512]{1,0:T(8,128)(2,1)}), bf16[1024,1024]{1,0:T(8,128)(2,1)}) %all-gather.20.cloned.1.call-update) | async-done | bytes 2097168 | tf_op jit(solution)/shard_map/all_gather | solution.py:53
  651.6 5.9 fusion.84
  657.6 41.4 %reduce-scatter.31.cloned.1.call-done = f32[1024,256]{1,0:T(8,128)} async-done(((f32[1024,1024]{1,0:T(8,128)}), f32[1024,256]{1,0:T(8,128)}) %reduce-scatter.31.cloned.1.call-update) | async-done | bytes 1048592 | tf_op jit(solution)/shard_map/reduce_scatter | solution.py:69
  700.7 12.6 psum.100
  713.3 33.1 %reduce-scatter.27.cloned.1.call-done = f32[1024,256]{1,0:T(8,128)} async-done(((f32[1024,1024]{1,0:T(8,128)}), f32[1024,256]{1,0:T(8,128)}) %reduce-scatter.27.cloned.1.call-update) | async-done | bytes 1048592 | tf_op jit(solution)/shard_map/reduce_scatter | solution.py:57
  746.4 3.2 fusion.74
  749.6 22.9 %all-gather.26.cloned.1.call-done = bf16[1024,1024]{1,0:T(8,128)(2,1)} async-done(((bf16[1024,256]{1,0:T(8,128)(2,1)}), bf16[1024,1024]{1,0:T(8,128)(2,1)}) %all-gather.26.cloned.1.call-update) | async-done | bytes 2097168 | tf_op jit(solution)/shard_map/all_gather | solution.py:61
  772.6 6.6 fusion.86
  779.4 54.3 %reduce-scatter.33.cloned.1.call-done = f32[1024,512]{1,0:T(8,128)} async-done(((f32[1024,1024]{1,0:T(8,128)}), f32[1024,512]{1,0:T(8,128)}) %reduce-scatter.33.cloned.1.call-update) | async-done | bytes 2097168 | tf_op jit(solution)/shard_map/reduce_scatter | solution.py:65
  833.8 2.9 multiply_reduce_fusion
  836.7 2.7 fusion.7
  850.7 16.6 all-gather.28.cloned.1.call-done
  867.3 4.8 fusion.88
  872.1 30.4 %all-gather.34.cloned.1.call-done = bf16[1024,1024]{1,0:T(8,128)(2,1)} async-done(((bf16[1024,512]{1,0:T(8,128)(2,1)}), bf16[1024,1024]{1,0:T(8,128)(2,1)}) %all-gather.34.cloned.1.call-update) | async-done | bytes 2097168 | tf_op jit(solution)/shard_map/all_gather | solution.py:239
  902.5 6.0 fusion.90
  908.5 29.3 %all-gather.32.cloned.1.call-done = bf16[1024,1024]{1,0:T(8,128)(2,1)} async-done(((bf16[1024,512]{1,0:T(8,128)(2,1)}), bf16[1024,1024]{1,0:T(8,128)(2,1)}) %all-gather.32.cloned.1.call-update) | async-done | bytes 2097168 | tf_op jit(solution)/shard_map/all_gather | solution.py:238
  937.8 6.6 fusion.89
  944.4 16.8 all-gather.30.cloned.1.call-done
  961.2 8.3 add_add_fusion
  971.1 6.1 fusion.96
  977.2 4.4 fusion.97
  981.7 4.4 fusion.11
  986.1 4.4 fusion.95
  990.5 2.6 fusion.91
  993.1 2.6 fusion.92
  995.8 4.7 fusion.93
  1000.5 4.4 fusion.94
  1005.0 9.1 reduce-scatter.35.cloned.1.call-done
  1015.9 12.5 all-reduce.2
  1028.4 12.6 psum.101
  1042.3 944.4 %all-reduce.6.cloned.1.call-done = (f32[1024,512]{1,0:T(8,128)}, f32[1024,512]{1,0:T(8,128)}, f32[1024,1024]{1,0:T(8,128)}, f32[1024,1024]{1,0:T(8,128)}, f32[10...) async-done(((f32[1024,512]{1,0:T(8,128)}, f32[1024,512]{1,0:T(8,128)}, f32[1024,1024]{1,0:T(8,128)}, ...) | async-done | bytes 29360144 | tf_op jit(solution)/shard_map/psum | solution.py:264
  1986.6 3.2 copy.37
  1992.8 2.1 copy.39
  (193 shorter events, 61.8 us)
Async XLA Ops:
  7.2 364.1 %copy-start = (bf16[1024,1024]{1,0:T(8,128)(2,1)S(1)}, bf16[1024,1024]{1,0:T(8,128)(2,1)}, u32[]{:S(2)}) copy-start(bf16[1024,1024]{1,0:T(8,128)(2,1)} %param.33) | copy-start | bytes 6291460
  7.2 41.0 %all-gather.14.cloned.1.call-start = ((), (), s32[]{:S(2)}) async-start(), calls=%async_computation.12 | async-start | bytes 2621440 | tf_op jit(solution)/shard_map/all_gather | solution.py:49
  25.9 58.8 %reduce-scatter.15.cloned.1.call-start = ((), (), s32[]{:S(2)}) async-start(), calls=%async_computation.14 | async-start | bytes 3145728 | tf_op jit(solution)/shard_map/reduce_scatter | solution.py:130
  52.7 66.8 %reduce-scatter.17.cloned.1.call-start = ((), (), s32[]{:S(2)}) async-start(), calls=%async_computation.15 | async-start | bytes 3145728 | tf_op jit(solution)/shard_map/reduce_scatter | solution.py:131
  58.1 118.6 %reduce-scatter.19.cloned.1.call-start = ((), (), s32[]{:S(2)}) async-start(), calls=%async_computation.16 | async-start | bytes 6291456 | tf_op jit(solution)/shard_map/reduce_scatter | solution.py:132
  65.2 168.5 %reduce-scatter.13.cloned.1.call-start = ((), (), s32[]{:S(2)}) async-start(), calls=%async_computation.13 | async-start | bytes 6291456 | tf_op jit(solution)/shard_map/reduce_scatter | solution.py:133
  71.9 198.7 %all-gather.16.cloned.1.call-start = ((), (), s32[]{:S(2)}) async-start(), calls=%async_computation.17 | async-start | bytes 3145728 | tf_op jit(solution)/shard_map/all_gather | solution.py:53
  74.5 46.4 %copy-start.8 = (f32[1024,128]{1,0:T(8,128)}, f32[1024,128]{1,0:T(8,128)S(1)}, u32[]{:S(2)}) copy-start(f32[1024,128]{1,0:T(8,128)S(1)} %get-tuple-element.120) | copy-start | bytes 1572868
  74.5 46.4 %copy-start.10 = (f32[1024,128]{1,0:T(8,128)}, f32[1024,128]{1,0:T(8,128)S(1)}, u32[]{:S(2)}) copy-start(f32[1024,128]{1,0:T(8,128)S(1)} %get-tuple-element.121) | copy-start | bytes 1572868
  119.5 1.9 copy-start.22
  176.6 2.3 copy-start.51
  237.4 84.4 %reduce-scatter.21.cloned.1.call-start = ((), (), s32[]{:S(2)}) async-start(), calls=%async_computation.18 | async-start | bytes 5242880 | tf_op jit(solution)/shard_map/reduce_scatter | solution.py:57
  277.2 60.0 %copy-start.37 = (f32[256]{0:T(256)S(1)}, f32[256]{0:T(256)}, u32[]{:S(2)}) copy-start(f32[256]{0:T(256)} %param.37) | copy-start | bytes 3076
  277.2 69.0 %all-gather.36.cloned.1.call-start = ((), (), s32[]{:S(2)}) async-start(), calls=%async_computation.35 | async-start | bytes 2621440 | tf_op jit(solution)/shard_map/all_gather | solution.py:61
  278.0 93.3 %all-gather.18.cloned.1.call-start = ((), (), s32[]{:S(2)}) async-start(), calls=%async_computation.19 | async-start | bytes 2621440 | tf_op jit(solution)/shard_map/all_gather | solution.py:49
  339.4 89.0 %reduce-scatter.29.cloned.1.call-start = ((), (), s32[]{:S(2)}) async-start(), calls=%async_computation.24 | async-start | bytes 6291456 | tf_op jit(solution)/shard_map/reduce_scatter | solution.py:65
  352.9 132.8 %reduce-scatter.23.cloned.1.call-start = ((), (), s32[]{:S(2)}) async-start(), calls=%async_computation.20 | async-start | bytes 6291456 | tf_op jit(solution)/shard_map/reduce_scatter | solution.py:163
  377.2 165.6 %reduce-scatter.25.cloned.1.call-start = ((), (), s32[]{:S(2)}) async-start(), calls=%async_computation.21 | async-start | bytes 6291456 | tf_op jit(solution)/shard_map/reduce_scatter | solution.py:164
  383.9 197.6 %all-gather.22.cloned.1.call-start = ((), (), s32[]{:S(2)}) async-start(), calls=%async_computation.25 | async-start | bytes 3145728 | tf_op jit(solution)/shard_map/all_gather | solution.py:177
  548.2 68.4 %all-gather.24.cloned.1.call-start = ((), (), s32[]{:S(2)}) async-start(), calls=%async_computation.26 | async-start | bytes 3145728 | tf_op jit(solution)/shard_map/all_gather | solution.py:178
  548.7 102.9 %all-gather.20.cloned.1.call-start = ((), (), s32[]{:S(2)}) async-start(), calls=%async_computation.22 | async-start | bytes 3145728 | tf_op jit(solution)/shard_map/all_gather | solution.py:53
  549.3 149.7 %reduce-scatter.31.cloned.1.call-start = ((), (), s32[]{:S(2)}) async-start(), calls=%async_computation.27 | async-start | bytes 5242880 | tf_op jit(solution)/shard_map/reduce_scatter | solution.py:69
  624.4 27.3 %copy-start.39 = (bf16[1024,1024]{1,0:T(8,128)(2,1)S(1)}, bf16[1024,1024]{1,0:T(8,128)(2,1)}, u32[]{:S(2)}) copy-start(bf16[1024,1024]{1,0:T(8,128)(2,1)} %param.35) | copy-start | bytes 6291460
  624.4 122.0 %reduce-scatter.27.cloned.1.call-start = ((), (), s32[]{:S(2)}) async-start(), calls=%async_computation.23 | async-start | bytes 5242880 | tf_op jit(solution)/shard_map/reduce_scatter | solution.py:57
  657.5 41.5 %copy-start.3 = (f32[1024,256]{1,0:T(8,128)S(1)}, f32[1024,256]{1,0:T(8,128)}, u32[]{:S(2)}) copy-start(f32[1024,256]{1,0:T(8,128)} %get-tuple-element.93) | copy-start | bytes 3145732
  657.6 115.0 %all-gather.26.cloned.1.call-start = ((), (), s32[]{:S(2)}) async-start(), calls=%async_computation.28 | async-start | bytes 2621440 | tf_op jit(solution)/shard_map/all_gather | solution.py:61
  699.0 47.4 %copy-start.20 = (f32[1024,256]{1,0:T(8,128)S(1)}, f32[1024,256]{1,0:T(8,128)}, u32[]{:S(2)}) copy-start(f32[1024,256]{1,0:T(8,128)} %reduce-scatter.31.cloned.1.call-done) | copy-start | bytes 3145732
  749.6 84.1 %reduce-scatter.33.cloned.1.call-start = ((), (), s32[]{:S(2)}) async-start(), calls=%async_computation.29 | async-start | bytes 6291456 | tf_op jit(solution)/shard_map/reduce_scatter | solution.py:65
  779.2 54.6 %copy-start.2 = (f32[1024,512]{1,0:T(8,128)S(1)}, f32[1024,512]{1,0:T(8,128)}, u32[]{:S(2)}) copy-start(f32[1024,512]{1,0:T(8,128)} %reduce-scatter.13.cloned.1.call-done) | copy-start | bytes 6291460
  779.2 88.1 %all-gather.28.cloned.1.call-start = ((), (), s32[]{:S(2)}) async-start(), calls=%async_computation.30 | async-start | bytes 1572864 | tf_op jit(solution)/shard_map/all_gather | solution.py:236
  833.7 2.9 copy-start.5
  833.8 2.9 copy-start.7
  836.7 2.7 copy-start.26
  844.4 2.2 copy-start.28
  845.8 2.3 copy-start.52
  845.8 56.7 %all-gather.34.cloned.1.call-start = ((), (), s32[]{:S(2)}) async-start(), calls=%async_computation.33 | async-start | bytes 3145728 | tf_op jit(solution)/shard_map/all_gather | solution.py:239
  846.6 91.2 %all-gather.32.cloned.1.call-start = ((), (), s32[]{:S(2)}) async-start(), calls=%async_computation.32 | async-start | bytes 3145728 | tf_op jit(solution)/shard_map/all_gather | solution.py:238
  849.9 111.3 %all-gather.30.cloned.1.call-start = ((), (), s32[]{:S(2)}) async-start(), calls=%async_computation.31 | async-start | bytes 1572864 | tf_op jit(solution)/shard_map/all_gather | solution.py:237
  850.6 51.9 %copy-start.40 = (bf16[1024,1024]{1,0:T(8,128)(2,1)S(1)}, bf16[1024,1024]{1,0:T(8,128)(2,1)}, u32[]{:S(2)}) copy-start(bf16[1024,1024]{1,0:T(8,128)(2,1)} %param.31) | copy-start | bytes 6291460
  850.7 163.4 %reduce-scatter.35.cloned.1.call-start = ((), (), s32[]{:S(2)}) async-start(), calls=%async_computation.34 | async-start | bytes 5242880 | tf_op jit(solution)/shard_map/reduce_scatter | solution.py:69
  908.5 52.7 %copy-start.34 = (bf16[1024,512]{1,0:T(8,128)(2,1)S(1)}, bf16[1024,512]{1,0:T(8,128)(2,1)}, u32[]{:S(2)}) copy-start(bf16[1024,512]{1,0:T(8,128)(2,1)} %param.29) | copy-start | bytes 3145732
  969.5 1017.1 %all-reduce.6.cloned.1.call-start = ((), (), s32[]{:S(2)}) async-start(), calls=%async_computation.36 | async-start | bytes 58720256 | tf_op jit(solution)/shard_map/psum | solution.py:264
  971.1 6.1 copy-start.45
  977.2 4.4 copy-start.43
  977.2 4.4 copy-start.46
  981.7 4.4 copy-start.42
  981.7 4.4 copy-start.47
  986.1 4.4 copy-start.41
  986.1 4.4 copy-start.50
  990.5 2.6 copy-start.35
  993.1 2.6 copy-start.49
  995.8 4.7 copy-start.48
  1004.9 9.2 copy-start.6
  1004.9 9.2 copy-start.36
  1004.9 36.1 %copy-start.19 = (f32[1024,256]{1,0:T(8,128)S(1)}, f32[1024,256]{1,0:T(8,128)}, u32[]{:S(2)}) copy-start(f32[1024,256]{1,0:T(8,128)} %get-tuple-element.91) | copy-start | bytes 3145732
  1014.1 26.9 %copy-start.12 = (f32[1024,256]{1,0:T(8,128)S(1)}, f32[1024,256]{1,0:T(8,128)}, u32[]{:S(2)}) copy-start(f32[1024,256]{1,0:T(8,128)} %reduce-scatter.35.cloned.1.call-done) | copy-start | bytes 3145732
  1986.6 3.2 copy-start.29
  1989.8 2.9 copy-start.18
  1992.8 3.7 copy-start.17
  1996.5 3.7 copy-start.16
  2000.2 3.7 copy-start.15
  2003.9 3.7 copy-start.14
  2007.6 3.7 copy-start.13
  2011.3 3.1 copy-start.1
  (14 other events, 17.4 us)
Sparse Core Ops, SparseCore 0:
  26.0 22.1 all-gather.13
  52.8 31.8 reduce-scatter.14
  87.5 31.8 reduce-scatter.16
  122.2 54.3 reduce-scatter.18
  179.3 54.3 reduce-scatter.12
  237.5 33.0 all-gather.15
  277.3 44.3 reduce-scatter.20
  323.3 22.8 all-gather.35
  348.4 22.8 all-gather.17
  374.0 54.3 reduce-scatter.28
  431.3 54.3 reduce-scatter.22
  488.4 54.3 reduce-scatter.24
  548.3 33.0 all-gather.21
  583.4 33.0 all-gather.23
  618.5 33.0 all-gather.19
  654.6 44.3 reduce-scatter.30
  701.9 44.3 reduce-scatter.26
  749.7 22.8 all-gather.25
  779.3 54.3 reduce-scatter.32
  846.0 21.2 all-gather.27
  869.4 33.0 all-gather.33
  904.6 33.0 all-gather.31
  939.9 21.2 all-gather.29
  969.6 44.3 reduce-scatter.34
  1018.7 967.8 all-reduce.5
where the time goes:
time: 2030 us; the launch traced here: 2020 us
  waiting for transfers between devices  1720 us (85%)
  matrix products  145 us (7%)
  blocking collectives  65.7 us (3%)
  other arithmetic  41.6 us (2%)
  local copies, waits for them, and re-layouts  33.8 us (2%)
    psum x1, waiting for transfers between devices, shards(): lax.psum((grad_query, grad_key, grad_value, grad_swish, grad_output, grad...  944 us
    reduce_scatter x2, waiting for transfers between devices, reduce_grad(): return lax.psum_scatter(partial_sum, 'row', scatter_dimension=1, tiled=True)  98.8 us
    reduce_scatter x2, waiting for transfers between devices, reduce_out(): return lax.psum_scatter(partial_sum, 'col', scatter_dimension=1, tiled=True)  76.9 us
    all_gather x2, waiting for transfers between devices, widen_out(): return lax.all_gather(values, 'row', axis=1, tiled=True)  60.2 us
    reduce_scatter x1, waiting for transfers between devices, shards(): lax.psum_scatter(matmul(wide_two, gelu_weight), 'row', scatter_dimension=...  57.3 us
    reduce_scatter x1, waiting for transfers between devices, shards(): lax.psum_scatter(matmul(wide_two, up_weight), 'row', scatter_dimension=1,...  57.1 us
    psum x4, blocking collectives, row_total(): return lax.psum(jnp.sum(values, axis=1), ('row', 'col'))  53.2 us
    reduce_scatter x1, waiting for transfers between devices, shards(): lax.psum_scatter(matmul(wide_one, swish_weight), 'row', scatter_dimension...  52.9 us
  transfers between devices with their start and end apart: 25, of which 25 were waited for; matrix products, arithmetic and copies ran while one was open for 7% of the time, Pallas kernels for 0%

commit v1 on v0

v1 whole, which is shorter than its diff:
```python
import jax
import jax.numpy as jnp
from jax import lax
from jax.experimental import pallas as pl
from jax.experimental.pallas import tpu as pltpu
from jax.sharding import PartitionSpec as P

KD = 256
QBLK = 512
MESH = pl.DeviceIdType.MESH
VM = pltpu.VMEM
F32 = jnp.float32
BF16 = jnp.bfloat16

epsilon = 1e-06


def rotate_half(values):
    half_cols = values.shape[-1] // 2
    return jnp.concatenate([-values[:, half_cols:], values[:, :half_cols]], axis=-1)


def rotary_tables(length, columns):
    half_cols = columns // 2
    frequency = 10000.0 ** (-jnp.arange(half_cols, dtype=jnp.float32) / half_cols)
    angles = jnp.arange(length, dtype=jnp.float32)[:, None] * frequency[None, :]
    cosine_half = jnp.cos(angles)
    sine_half = jnp.sin(angles)
    return (
        jnp.concatenate([cosine_half, cosine_half], axis=1),
        jnp.concatenate([sine_half, sine_half], axis=1),
    )


def decay_block(segments, row_start, row_count, column_count, log_decay):
    query_pos = row_start + jnp.arange(row_count, dtype=jnp.int32)
    key_pos = jnp.arange(column_count, dtype=jnp.int32)
    distance = query_pos[:, None] - key_pos[None, :]
    same_doc = (
        segments[row_start : row_start + row_count][:, None] == segments[:column_count][None, :]
    )
    keep_mask = (distance >= 0) & same_doc
    return jnp.where(
        keep_mask, jnp.exp(jnp.maximum(distance, 0).astype(jnp.float32) * log_decay), 0.0
    )


def neighbours():
    r, c = lax.axis_index("row"), lax.axis_index("col")
    core = c + 1 - 2 * lax.rem(c, 2)
    across = lax.rem(c + 2, 4)
    return r, c, core, across


def enter():
    r, c, core, across = neighbours()
    barrier = pltpu.get_barrier_semaphore()
    for target in ({"col": core}, {"col": across}, {"row": 1 - r}):
        pl.semaphore_signal(barrier, inc=1, device_id=target, device_id_type=MESH)
    pl.semaphore_wait(barrier, 3)


class Sender:
    def __init__(self, send_sem, recv_sem):
        self.send_sem, self.recv_sem, self.started = send_sem, recv_sem, []

    def __call__(self, src, dst, target):
        slot = len(self.started)
        copy = pltpu.make_async_remote_copy(
            src_ref=src,
            dst_ref=dst,
            send_sem=self.send_sem.at[slot],
            recv_sem=self.recv_sem.at[slot],
            device_id=target,
            device_id_type=MESH,
        )
        copy.start()
        self.started.append(copy)
        return copy


def gather_body(own_ref, out_ref, send, local_sem, side):
    rows, width = own_ref.shape
    half = rows // 2
    r, c, core, across = neighbours()
    to_core, to_x, to_y = {"col": core}, {"col": across}, {"row": 1 - r}

    def view(ref, place, part):
        cols = pl.ds(pl.multiple_of(place * width, width), width)
        if part is None:
            return ref.at[:, cols]
        return ref.at[part * half : (part + 1) * half, cols]

    def own(part):
        return own_ref.at[part * half : (part + 1) * half]

    side_start = side(send, to_core, to_x, to_y)
    x0 = send(own(0), view(out_ref, c, 0), to_x)
    y1 = send(own(1), view(out_ref, 4 + c, 1), to_y)
    x1 = send(own(1), view(out_ref, c, 1), to_x)
    y0 = send(own(0), view(out_ref, 4 + c, 0), to_y)
    late = [send(own_ref, view(out_ref, c, None), to_core)]
    keep = pltpu.make_async_copy(own_ref, view(out_ref, c, None), local_sem)
    keep.start()
    next(side_start)
    x0.wait_recv()
    fy = send(view(out_ref, across, 0), view(out_ref, 4 + across, 0), to_y)
    late.append(send(view(out_ref, across, 0), view(out_ref, across, 0), to_core))
    y1.wait_recv()
    fx = send(view(out_ref, 4 + c, 1), view(out_ref, 4 + c, 1), to_x)
    late.append(send(view(out_ref, 4 + c, 1), view(out_ref, 4 + c, 1), to_core))
    next(side_start)
    x1.wait_recv()
    late.append(send(view(out_ref, across, 1), view(out_ref, across, 1), to_core))
    y0.wait_recv()
    late.append(send(view(out_ref, 4 + c, 0), view(out_ref, 4 + c, 0), to_core))
    next(side_start)
    fy.wait_recv()
    late.append(send(view(out_ref, 4 + across, 0), view(out_ref, 4 + across, 0), to_core))
    fx.wait_recv()
    late.append(send(view(out_ref, 4 + across, 1), view(out_ref, 4 + across, 1), to_core))
    keep.wait()
    for copy in late:
        copy.wait_recv()
    for copy in send.started:
        copy.wait_send()


def no_side(send, to_core, to_x, to_y):
    while True:
        yield


def total_side(vec_ref, total_ref, got):
    def steps(send, to_core, to_x, to_y):
        first = send(vec_ref, got.at[0], to_core)

        def rest():
            first.wait_recv()
            got[3] = vec_ref[...] + got[0]
            second = send(got.at[3], got.at[1], to_x)
            yield
            second.wait_recv()
            got[4] = got[3] + got[1]
            third = send(got.at[4], got.at[2], to_y)
            yield
            third.wait_recv()
            total_ref[...] = got[4] + got[2]
            yield

        return rest()

    return steps


def gather_kernel(own_ref, out_ref, send_sem, recv_sem, local_sem):
    enter()
    gather_body(own_ref, out_ref, Sender(send_sem, recv_sem), local_sem, no_side)


def gather_total_kernel(own_ref, vec_ref, out_ref, total_ref, got, send_sem, recv_sem, local_sem):
    enter()
    gather_body(
        own_ref, out_ref, Sender(send_sem, recv_sem), local_sem, total_side(vec_ref, total_ref, got)
    )


def vmem(count):
    return [pl.BlockSpec(memory_space=VM)] * count


def params(number):
    return pltpu.CompilerParams(
        collective_id=number, has_side_effects=True, vmem_limit_bytes=40 << 20
    )


def plane_gather(own):
    rows, width = own.shape
    return pl.pallas_call(
        gather_kernel,
        out_shape=jax.ShapeDtypeStruct((rows, width * 8), own.dtype),
        in_specs=vmem(1),
        out_specs=vmem(1)[0],
        scratch_shapes=[
            pltpu.SemaphoreType.DMA((13,)),
            pltpu.SemaphoreType.DMA((13,)),
            pltpu.SemaphoreType.DMA(()),
        ],
        compiler_params=params(0),
    )(own)


def plane_gather_total(own, vector):
    rows, width = own.shape
    small = (rows // 128, 128)
    wide, total = pl.pallas_call(
        gather_total_kernel,
        out_shape=(
            jax.ShapeDtypeStruct((rows, width * 8), own.dtype),
            jax.ShapeDtypeStruct(small, F32),
        ),
        in_specs=vmem(2),
        out_specs=tuple(vmem(2)),
        scratch_shapes=[
            pltpu.VMEM((5,) + small, F32),
            pltpu.SemaphoreType.DMA((16,)),
            pltpu.SemaphoreType.DMA((16,)),
            pltpu.SemaphoreType.DMA(()),
        ],
        compiler_params=params(1),
    )(own, vector.reshape(small))
    return wide, total.reshape(rows)


def scatter_body(part_ref, out_ref, stage, from_core, from_x, from_y, send, side):
    rows, width = out_ref.shape
    half = rows // 2
    r, c, core, across = neighbours()
    to_core, to_x, to_y = {"col": core}, {"col": across}, {"row": 1 - r}
    places = (4 + across, across, 4 + c, c)
    other = core - c

    def cols(place):
        return pl.ds(pl.multiple_of(place * width, width), width)

    side_start = side(send, to_core, to_x, to_y)
    first = [
        send(part_ref.at[:, cols(places[i] + other)], from_core.at[i], to_core) for i in range(4)
    ]
    lo, hi = slice(0, half), slice(half, 2 * half)

    def summed(i, part):
        return part_ref[part, cols(places[i])].astype(F32) + from_core[i, part].astype(F32)

    first[0].wait_recv()
    next(side_start)
    stage[0, lo] = summed(0, lo).astype(BF16)
    dx = send(stage.at[0, lo], from_x.at[2], to_x)
    stage[0, hi] = summed(0, hi).astype(BF16)
    dy = send(stage.at[0, hi], from_y.at[2], to_y)
    first[1].wait_recv()
    stage[1, lo] = summed(1, lo).astype(BF16)
    x0 = send(stage.at[1, lo], from_x.at[0], to_x)
    first[2].wait_recv()
    stage[2, hi] = summed(2, hi).astype(BF16)
    y1 = send(stage.at[2, hi], from_y.at[1], to_y)
    next(side_start)
    dy.wait_recv()
    stage[1, hi] = (summed(1, hi) + from_y[2].astype(F32)).astype(BF16)
    x1 = send(stage.at[1, hi], from_x.at[1], to_x)
    dx.wait_recv()
    stage[2, lo] = (summed(2, lo) + from_x[2].astype(F32)).astype(BF16)
    y0 = send(stage.at[2, lo], from_y.at[0], to_y)
    next(side_start)
    first[3].wait_recv()
    x0.wait_recv()
    y1.wait_recv()
    out_ref[lo] = summed(3, lo) + from_x[0].astype(F32)
    out_ref[hi] = summed(3, hi) + from_y[1].astype(F32)
    x1.wait_recv()
    out_ref[hi] = out_ref[hi] + from_x[1].astype(F32)
    y0.wait_recv()
    out_ref[lo] = out_ref[lo] + from_y[0].astype(F32)
    for copy in send.started:
        copy.wait_send()


def scatter_kernel(part_ref, out_ref, stage, from_core, from_x, from_y, send_sem, recv_sem):
    enter()
    scatter_body(
        part_ref, out_ref, stage, from_core, from_x, from_y, Sender(send_sem, recv_sem), no_side
    )


def scatter_total_kernel(
    part_ref, vec_ref, out_ref, total_ref, stage, from_core, from_x, from_y, got, send_sem, recv_sem
):
    enter()
    scatter_body(
        part_ref,
        out_ref,
        stage,
        from_core,
        from_x,
        from_y,
        Sender(send_sem, recv_sem),
        total_side(vec_ref, total_ref, got),
    )


def scatter_scratch(rows, width):
    half = rows // 2
    return [
        pltpu.VMEM((3, rows, width), BF16),
        pltpu.VMEM((4, rows, width), BF16),
        pltpu.VMEM((3, half, width), BF16),
        pltpu.VMEM((3, half, width), BF16),
    ]


def plane_scatter(part):
    rows, wide = part.shape
    width = wide // 8
    return pl.pallas_call(
        scatter_kernel,
        out_shape=jax.ShapeDtypeStruct((rows, width), F32),
        in_specs=vmem(1),
        out_specs=vmem(1)[0],
        scratch_shapes=scatter_scratch(rows, width)
        + [pltpu.SemaphoreType.DMA((10,)), pltpu.SemaphoreType.DMA((10,))],
        compiler_params=params(2),
    )(part)


def plane_scatter_total(part, vector):
    rows, wide = part.shape
    width = wide // 8
    small = (rows // 128, 128)
    out, total = pl.pallas_call(
        scatter_total_kernel,
        out_shape=(jax.ShapeDtypeStruct((rows, width), F32), jax.ShapeDtypeStruct(small, F32)),
        in_specs=vmem(2),
        out_specs=tuple(vmem(2)),
        scratch_shapes=scatter_scratch(rows, width)
        + [
            pltpu.VMEM((5,) + small, F32),
            pltpu.SemaphoreType.DMA((13,)),
            pltpu.SemaphoreType.DMA((13,)),
        ],
        compiler_params=params(3),
    )(part, vector.reshape(small))
    return out, total.reshape(rows)


def swap_rows(values):
    return lax.ppermute(values, "row", [(0, 1), (1, 0)])


def halves_of(values, axis, r):
    size = values.shape[axis] // 2
    mine = lax.dynamic_slice_in_dim(values, r * size, size, axis)
    theirs = lax.dynamic_slice_in_dim(values, (1 - r) * size, size, axis)
    return mine, theirs


def whole_weight(values, axis, r):
    mine, theirs = halves_of(values, axis, r)
    return jnp.concatenate([mine, swap_rows(theirs)], axis=1 - axis)


def sum_packs(grad, axis, r):
    size = grad.shape[1 - axis] // 2
    mine = lax.slice_in_dim(grad, 0, size, axis=1 - axis)
    theirs = swap_rows(lax.slice_in_dim(grad, size, 2 * size, axis=1 - axis))
    mine, theirs = lax.psum((mine, theirs), "dp")
    both = jnp.concatenate([mine, theirs, mine], axis=axis)
    width = mine.shape[axis]
    return lax.dynamic_slice_in_dim(both, r * width, 2 * width, axis).astype(F32)


def matmul(left, right):
    return jnp.dot(left, right, preferred_element_type=jnp.float32)


def weight_grad(inputs, grads):
    return jnp.einsum("tk,tf->kf", inputs, grads, preferred_element_type=jnp.float32).astype(BF16)


def back_product(grads, weights):
    return jnp.einsum("tf,kf->tk", grads, weights, preferred_element_type=jnp.float32)


def group_norm(retained):
    spread = jnp.sqrt(jnp.mean(retained * retained, axis=1, keepdims=True) + epsilon)
    return retained / jnp.maximum(spread, 1.0)


def swish_gate(swish_sum, grouped):
    return jax.nn.silu(swish_sum) * grouped


def gelu_gate(gelu_sum, up_sum):
    return jax.nn.gelu(gelu_sum) * up_sum


def retention(query_low, key_low, value_low, segments, log_decay):
    outputs = []
    for start in range(0, query_low.shape[0], QBLK):
        stop = start + QBLK
        decay = decay_block(segments, start, QBLK, stop, log_decay)
        scores = jnp.einsum(
            "qd,kd->qk", query_low[start:stop], key_low[:stop], preferred_element_type=jnp.float32
        )
        weights_low = (scores * decay).astype(jnp.bfloat16)
        outputs.append(matmul(weights_low, value_low[:stop]))
    return jnp.concatenate(outputs, axis=0)


def retention_back(query_low, key_low, value_low, retained_low, segments, log_decay):
    tokens = query_low.shape[0]
    key_accum = jnp.zeros((tokens, key_low.shape[1]), jnp.float32)
    value_accum = jnp.zeros((tokens, value_low.shape[1]), jnp.float32)
    query_parts = []
    for start in range(0, tokens, QBLK):
        stop = start + QBLK
        decay = decay_block(segments, start, QBLK, stop, log_decay)
        scores = jnp.einsum(
            "qd,kd->qk", query_low[start:stop], key_low[:stop], preferred_element_type=jnp.float32
        )
        weights_low = (scores * decay).astype(jnp.bfloat16)
        weights_grad = jnp.einsum(
            "qv,kv->qk",
            retained_low[start:stop],
            value_low[:stop],
            preferred_element_type=jnp.float32,
        )
        scores_low = (weights_grad * decay).astype(jnp.bfloat16)
        query_parts.append(matmul(scores_low, key_low[:stop]))
        key_accum = key_accum.at[:stop].add(
            jnp.einsum(
                "qk,qd->kd", scores_low, query_low[start:stop], preferred_element_type=jnp.float32
            )
        )
        value_accum = value_accum.at[:stop].add(
            jnp.einsum(
                "qk,qv->kv",
                weights_low,
                retained_low[start:stop],
                preferred_element_type=jnp.float32,
            )
        )
    return jnp.concatenate(query_parts, axis=0), key_accum, value_accum


def shards(
    block_in,
    segment_ids,
    block_cotangent,
    query_weight,
    key_weight,
    value_weight,
    swish_weight,
    output_weight,
    gelu_weight,
    up_weight,
    down_weight,
    first_gain,
    second_gain,
):
    r = lax.axis_index("row")
    hidden = block_in[0].astype(jnp.float32)
    segments = segment_ids[0]
    tokens = hidden.shape[0]
    features = hidden.shape[1] * lax.axis_size("row") * lax.axis_size("col")
    head_index = lax.axis_index("col") * lax.axis_size("row") + r
    log_decay = jnp.log(1.0 - 2.0 ** (-5.0 - head_index.astype(jnp.float32)))
    cosine_table, sine_table = rotary_tables(tokens, KD)

    first_weight = jnp.concatenate(
        [
            whole_weight(query_weight, 1, r),
            whole_weight(key_weight, 1, r),
            whole_weight(value_weight, 1, r),
            whole_weight(swish_weight, 1, r),
        ],
        axis=1,
    )
    out_weight = whole_weight(output_weight, 0, r)
    second_weight = jnp.concatenate(
        [whole_weight(gelu_weight, 1, r), whole_weight(up_weight, 1, r)], axis=1
    )
    last_weight = whole_weight(down_weight, 0, r)
    value_cols = out_weight.shape[0]

    wide_one, square_one = plane_gather_total(
        (hidden * first_gain).astype(BF16), jnp.sum(hidden * hidden, axis=1)
    )
    scale_one = lax.rsqrt(square_one / features + epsilon)[:, None]
    sums_one = matmul(wide_one, first_weight) * scale_one
    query_sum = sums_one[:, :KD]
    key_sum = sums_one[:, KD : 2 * KD]
    value_sum = sums_one[:, 2 * KD : 2 * KD + value_cols]
    swish_sum = sums_one[:, 2 * KD + value_cols :]
    query_low = (query_sum * cosine_table + rotate_half(query_sum) * sine_table).astype(
        jnp.bfloat16
    )
    key_low = ((key_sum * cosine_table + rotate_half(key_sum) * sine_table) * KD ** (-0.5)).astype(
        jnp.bfloat16
    )
    value_low = value_sum.astype(jnp.bfloat16)
    retained = retention(query_low, key_low, value_low, segments, log_decay)
    grouped, group_pull = jax.vjp(group_norm, retained)
    gated_full, swish_pull = jax.vjp(swish_gate, swish_sum, grouped)
    gated = gated_full.astype(jnp.bfloat16)
    middle = hidden + plane_scatter(matmul(gated, out_weight).astype(BF16))

    wide_two, square_two = plane_gather_total(
        (middle * second_gain).astype(BF16), jnp.sum(middle * middle, axis=1)
    )
    scale_two = lax.rsqrt(square_two / features + epsilon)[:, None]
    sums_two = matmul(wide_two, second_weight) * scale_two
    hidden_cols = sums_two.shape[1] // 2
    gelu_sum, up_sum = sums_two[:, :hidden_cols], sums_two[:, hidden_cols:]
    product_full, gelu_pull = jax.vjp(gelu_gate, gelu_sum, up_sum)
    product = product_full.astype(jnp.bfloat16)
    block_out = (middle + plane_scatter(matmul(product, last_weight).astype(BF16))).astype(BF16)

    upstream = block_cotangent[0].astype(jnp.float32)
    wide_feed_grad = plane_gather(block_cotangent[0])
    grad_down = weight_grad(product, wide_feed_grad)
    product_grad = back_product(wide_feed_grad, last_weight)
    gelu_grad, up_grad = gelu_pull(product_grad)
    both_grad = jnp.concatenate([gelu_grad, up_grad], axis=1)
    inner_two = jnp.sum(both_grad * sums_two, axis=1)
    both_low = (both_grad * scale_two).astype(BF16)
    grad_both = weight_grad(wide_two, both_low)
    normed_two_grad, inner_two = plane_scatter_total(
        back_product(both_low, second_weight).astype(BF16), inner_two
    )
    grad_second = jnp.sum(normed_two_grad * middle, axis=0)
    middle_grad = (
        upstream
        + second_gain * normed_two_grad
        - middle * (scale_two**2 * inner_two[:, None] / features)
    )
    wide_attended_grad = plane_gather(middle_grad.astype(BF16))
    grad_output = weight_grad(gated, wide_attended_grad)
    gated_grad = back_product(wide_attended_grad, out_weight)
    swish_grad, grouped_grad = swish_pull(gated_grad)
    (retained_grad,) = group_pull(grouped_grad)
    query_grad, key_grad, value_grad = retention_back(
        query_low, key_low, value_low, retained_grad.astype(BF16), segments, log_decay
    )
    key_grad = key_grad * KD ** (-0.5)
    query_back = query_grad * cosine_table - rotate_half(query_grad) * sine_table
    key_back = key_grad * cosine_table - rotate_half(key_grad) * sine_table
    all_grad = jnp.concatenate([query_back, key_back, value_grad, swish_grad], axis=1)
    inner_one = jnp.sum(all_grad * sums_one, axis=1)
    all_low = (all_grad * scale_one).astype(BF16)
    grad_all = weight_grad(wide_one, all_low)
    normed_one_grad, inner_one = plane_scatter_total(
        back_product(all_low, first_weight).astype(BF16), inner_one
    )
    grad_first = jnp.sum(normed_one_grad * hidden, axis=0)
    grad_input = (
        middle_grad
        + first_gain * normed_one_grad
        - hidden * (scale_one**2 * inner_one[:, None] / features)
    ).astype(BF16)

    grad_first, grad_second = lax.psum((grad_first, grad_second), "dp")
    return (
        block_out[None],
        grad_input[None],
        sum_packs(grad_all[:, :KD], 1, r),
        sum_packs(grad_all[:, KD : 2 * KD], 1, r),
        sum_packs(grad_all[:, 2 * KD : 2 * KD + value_cols], 1, r),
        sum_packs(grad_all[:, 2 * KD + value_cols :], 1, r),
        sum_packs(grad_output, 0, r),
        sum_packs(grad_both[:, :hidden_cols], 1, r),
        sum_packs(grad_both[:, hidden_cols:], 1, r),
        sum_packs(grad_down, 0, r),
        grad_first,
        grad_second,
    )


def solution(mesh):
    activations = P("dp", None, ("row", "col"))
    in_weight, out_weight, gain = P("row", "col"), P("col", "row"), P(("row", "col"))
    return jax.shard_map(
        shards,
        mesh=mesh,
        in_specs=(activations, P("dp", None), activations)
        + (in_weight,) * 4
        + (out_weight, in_weight, in_weight, out_weight, gain, gain),
        out_specs=(activations, activations)
        + (in_weight,) * 4
        + (out_weight, in_weight, in_weight, out_weight, gain, gain),
        check_vma=False,
    )
```

time: 2030 us -> 1040 us (0.51)
  waiting for transfers between devices: 1720 us -> 546 us
  Pallas kernels: 0 us -> 270 us
  blocking collectives: 65.7 us -> 13.2 us
  matrix products: 145 us -> 99.7 us
    psum x1, waiting for transfers between devices: 944 us -> 412 us  [sum_packs(): mine, theirs = lax.psum((mine, theirs), 'dp')]
    reduce_scatter x12 -> x0, waiting for transfers between devices: 486 us -> none  [the longest x2 98.8 us: reduce_grad(): return lax.psum_scatter(partial_sum, 'row', scatter_dimension=1, tiled=True)]
    all_gather x12 -> x0, waiting for transfers between devices: 284 us -> none  [the longest x2 60.2 us: widen_out(): return lax.all_gather(values, 'row', axis=1, tiled=True)]
    pallas_call x0 -> x8, Pallas kernels: none -> 270 us  [the longest x2 114 us: plane_gather(): pl.pallas_call(gather_kernel, out_shape=jax.ShapeDtypeStruct((rows, width...]
    ppermute x0 -> x16, waiting for transfers between devices: none -> 134 us  [swap_rows(): return lax.ppermute(values, 'row', [(0, 1), (1, 0)])]
    psum x5 -> x1, blocking collectives: 65.7 us -> 13.2 us  [shards(): grad_first, grad_second = lax.psum((grad_first, grad_second), 'dp')]
    dot_general x8 -> x4, matrix products: 52.8 us -> 30.6 us  [back_product(): jnp.einsum('tf,kf->tk', grads, weights, preferred_element_type=jnp.float32)]
    dot_general x12 -> x8, matrix products: 49.1 us -> 42.2 us  [matmul(): return jnp.dot(left, right, preferred_element_type=jnp.float32)]
  transfers between devices with their start and end apart: 25 -> 17, of which waited for: 25 -> 6; matrix products, arithmetic and copies ran while one was open for 7% -> 9% of each run, Pallas kernels for 0% -> 22%
where the time goes in v1:
time: 1040 us
  waiting for transfers between devices  546 us (52%)
  Pallas kernels  270 us (26%)
  matrix products  99.7 us (10%)
  other arithmetic  41.2 us (4%)
  local copies, waits for them, and re-layouts  34.7 us (3%)
  starting transfers between devices  18 us (2%)
  between operations  15.2 us (1%)
  blocking collectives  13.2 us (1%)
    psum x1, waiting for transfers between devices, sum_packs(): mine, theirs = lax.psum((mine, theirs), 'dp')  412 us
    ppermute x16, waiting for transfers between devices, swap_rows(): return lax.ppermute(values, 'row', [(0, 1), (1, 0)])  134 us
    pallas_call x2, Pallas kernels, plane_gather(): pl.pallas_call(gather_kernel, out_shape=jax.ShapeDtypeStruct((rows, width...  114 us
    pallas_call x2, Pallas kernels, plane_scatter(): pl.pallas_call(scatter_kernel, out_shape=jax.ShapeDtypeStruct((rows, widt...  67.2 us
    pallas_call x2, Pallas kernels, plane_scatter_total(): pl.pallas_call(scatter_total_kernel, out_shape=(jax.ShapeDtypeStruct((row...  44.4 us
    pallas_call x2, Pallas kernels, plane_gather_total(): pl.pallas_call(gather_total_kernel, out_shape=(jax.ShapeDtypeStruct((rows...  43.9 us
    dot_general x8, matrix products, matmul(): return jnp.dot(left, right, preferred_element_type=jnp.float32)  42.2 us
    dot_general x4, matrix products, back_product(): jnp.einsum('tf,kf->tk', grads, weights, preferred_element_type=jnp.float32)  30.6 us
  transfers between devices with their start and end apart: 17, of which 6 were waited for; matrix products, arithmetic and copies ran while one was open for 9% of the time, Pallas kernels for 22%

profile of v1, /device:TPU:0, one launch (start us, length us, event | category | flops | bytes accessed | tf_op | source)
XLA Modules:
  0.0 1037.7 jit_solution(7103928396075077152)
XLA Ops:
  7.2 2.4 constant_dynamic-slice_fusion.15
  9.7 3.0 collective-permute-start
  12.6 2.2 constant_dynamic-slice_fusion.13
  14.9 1.3 constant_dynamic-slice_fusion.11
  16.1 2.0 collective-permute-start.2
  18.2 1.6 constant_dynamic-slice_fusion.9
  20.4 1.5 constant_dynamic-slice_fusion.7
  21.9 1.3 collective-permute-start.4
  23.2 1.6 constant_dynamic-slice_fusion.5
  24.8 1.6 constant_dynamic-slice_fusion.3
  27.2 1.5 constant_dynamic-slice_fusion.1
  29.1 93.0 %shard_map.234 = bf16[1024,2048]{1,0:T(8,128)(2,1)S(1)} custom-call(bf16[1024,256]{1,0:T(8,128)(2,1)S(1)} %bitcast.77), custom_call_target="tpu_custom_call" | custom-call | tf_op jit(solution)/shard_map/pallas_call | solution.py:180
  122.1 23.0 %shard_map.230 = (bf16[1024,2048]{1,0:T(8,128)(2,1)S(1)}, f32[8,128]{1,0:T(8,128)S(1)}) custom-call(bf16[1024,256]{1,0:T(8,128)(2,1)S(1)} %get-tuple-element.166.own_ref, f32[8,128]{1,0:T(8,128)S(1)} %bitcast.78), custom_call_target="tpu_custom_call" | custom-call | tf_op jit(solution)/shard_map/pallas_call | solution.py:197
  145.1 2.0 copy-done.6
  147.1 1.9 fusion.68
  149.7 1.5 collective-permute-start.6
  151.7 25.5 %fusion.102 = (bf16[1024,1536]{1,0:T(8,128)(2,1)}, f32[1024,1536]{1,0:T(8,128)}) fusion(f32[1024]{0:T(1024)S(1)} %rsqrt_bitcast_fusion.1, bf16[1024,2048]{1,0:T(8,128)(2,1)} %copy-done.6, bf16[1024,512]{1,0:T(8,128)(2,1)} %collective-permute-done.3, bf16[1024,512]{1,0:T(8,128)(2,1)S(1)} %copy-done.35, bf16[1024,512]{1,0:T(8,128)(2,1)} %collective-permute-done.2, ...), kind=kOutput, calls=%fused_computation.219 | convolution fusion | flops 6495928320 | bytes 19927040 | tf_op jit(solution)/shard_map/dot_general | solution.py:363
  177.3 1.7 slice_negate_fusion.2
  179.0 2.1 fusion.52
  181.5 2.0 copy-done.60
  186.7 4.4 convolution_convert_fusion.3.part_ref
  191.1 45.7 %shard_map.231 = f32[1024,256]{1,0:T(8,128)S(1)} custom-call(bf16[1024,2048]{1,0:T(8,128)(2,1)S(1)} %convolution_convert_fusion.3.part_ref), custom_call_target="tpu_custom_call" | custom-call | tf_op jit(solution)/shard_map/pallas_call | solution.py:305
  237.1 20.9 %shard_map.232 = (bf16[1024,2048]{1,0:T(8,128)(2,1)S(1)}, f32[8,128]{1,0:T(8,128)S(1)}) custom-call(bf16[1024,256]{1,0:T(8,128)(2,1)S(1)} %get-tuple-element.154.own_ref, f32[8,128]{1,0:T(8,128)S(1)} %bitcast.81), custom_call_target="tpu_custom_call" | custom-call | tf_op jit(solution)/shard_map/pallas_call | solution.py:197
  258.1 6.1 convolution_multiply_fusion.1
  264.3 6.0 fusion.5
  271.6 6.5 convolution_convert_fusion.4
  278.1 7.1 convolution_convert_fusion.5.part_ref
  285.2 22.2 %shard_map.235 = (f32[1024,256]{1,0:T(8,128)S(1)}, f32[8,128]{1,0:T(8,128)S(1)}) custom-call(bf16[1024,2048]{1,0:T(8,128)(2,1)S(1)} %convolution_convert_fusion.5.part_ref, f32[8,128]{1,0:T(8,128)S(1)} %bitcast.80), custom_call_target="tpu_custom_call" | custom-call | tf_op jit(solution)/shard_map/pallas_call | solution.py:320
  307.6 21.3 %shard_map.236 = bf16[1024,2048]{1,0:T(8,128)(2,1)S(1)} custom-call(bf16[1024,256]{1,0:T(8,128)(2,1)S(1)} %fusion.95.own_ref), custom_call_target="tpu_custom_call" | custom-call | tf_op jit(solution)/shard_map/pallas_call | solution.py:180
  329.0 4.1 convolution_convert_fusion.7
  333.1 4.2 multiply_reduce_fusion.2
  337.3 2.1 fusion.6
  340.0 1.2 multiply_convert_fusion.2
  342.5 2.4 convolution_convert_fusion.6
  345.0 2.1 fusion.98
  347.1 1.6 fusion.99
  353.6 1.3 copy-done.14
  355.3 2.5 copy-done.7
  357.9 8.5 convolution_convert_fusion
  366.4 1.1 fusion.97
  369.5 1.2 fusion.100
  370.7 1.6 fusion.96
  372.3 58.8 %collective-permute-done.9 = bf16[1024,256]{1,0:T(8,128)(2,1)S(1)} collective-permute-done((bf16[1024,256]{1,0:T(8,128)(2,1)S(1)}, bf16[1024,256]{1,0:T(8,128)(2,1)S(1)}, u32[]{:S(2)}, u32[]{:S(2)}) %collective-permute-start.9) | collective-permute-done | bytes 524320 | tf_op jit(solution)/shard_map/ppermute | solution.py:337
  432.2 10.1 collective-permute-done.8
  444.4 20.5 %collective-permute-done.12 = bf16[512,1024]{1,0:T(8,128)(2,1)} collective-permute-done((bf16[512,1024]{1,0:T(8,128)(2,1)S(1)}, bf16[512,1024]{1,0:T(8,128)(2,1)}, u32[]{:S(2)}, u32[]{:S(2)}) %collective-permute-start.12) | collective-permute-done | bytes 1048608 | tf_op jit(solution)/shard_map/ppermute | solution.py:337
  464.9 22.5 %collective-permute-done.11 = bf16[1024,512]{1,0:T(8,128)(2,1)} collective-permute-done((bf16[1024,512]{1,0:T(8,128)(2,1)S(1)}, bf16[1024,512]{1,0:T(8,128)(2,1)}, u32[]{:S(2)}, u32[]{:S(2)}) %collective-permute-start.11) | collective-permute-done | bytes 1048608 | tf_op jit(solution)/shard_map/ppermute | solution.py:337
  487.4 21.9 %collective-permute-done.10 = bf16[1024,512]{1,0:T(8,128)(2,1)} collective-permute-done((bf16[1024,512]{1,0:T(8,128)(2,1)S(1)}, bf16[1024,512]{1,0:T(8,128)(2,1)}, u32[]{:S(2)}, u32[]{:S(2)}) %collective-permute-start.10) | collective-permute-done | bytes 1048608 | tf_op jit(solution)/shard_map/ppermute | solution.py:337
  509.3 4.3 convolution_convert_fusion.2.part_ref
  513.6 21.5 %shard_map.233 = f32[1024,256]{1,0:T(8,128)S(1)} custom-call(bf16[1024,2048]{1,0:T(8,128)(2,1)S(1)} %convolution_convert_fusion.2.part_ref), custom_call_target="tpu_custom_call" | custom-call | tf_op jit(solution)/shard_map/pallas_call | solution.py:305
  536.1 3.3 multiply_reduce_fusion
  539.4 13.4 %convolution_convert_fusion.1.part_ref = bf16[1024,2048]{1,0:T(8,128)(2,1)} fusion(f32[1024,512]{1,0:T(8,128)} %copy-done.11, f32[1024,512]{1,0:T(8,128)} %copy-done.8, f32[1024,256]{1,0:T(8,128)} %copy-done.17, f32[1024,256]{1,0:T(8,128)} %copy-done.15, f32[1024]{0:T(1024)S(1)} %rsqrt_bitcast_fusion.1, bf16[1024,512]{1,0:T(8,128)(2,1)} %collective-permute-done.3, ...), kind=kOutput, calls=%fused_computation.10 | convolution fusion | flops 6502744064 | bytes 16781312 | tf_op jit(solution)/shard_map/tf,kf->tk/dot_general | solution.py:371
  552.8 2.2 copy-done.1
  555.0 22.2 %shard_map.237 = (f32[1024,256]{1,0:T(8,128)S(1)}, f32[8,128]{1,0:T(8,128)S(1)}) custom-call(bf16[1024,2048]{1,0:T(8,128)(2,1)S(1)} %copy-done.1, f32[8,128]{1,0:T(8,128)S(1)} %bitcast.79), custom_call_target="tpu_custom_call" | custom-call | tf_op jit(solution)/shard_map/pallas_call | solution.py:320
  577.3 1.6 multiply_reduce_fusion.4
  578.8 13.2 %all-reduce.2 = (f32[256]{0:T(256)}, f32[256]{0:T(256)}) all-reduce(f32[256]{0:T(256)S(1)} %get-tuple-element.93, f32[256]{0:T(256)S(1)} %get-tuple-element.92), channel_id=1, replica_groups=mesh['dp'=4,'row'=2,'col'=4] {'dp'}, use_global_device_ids=true, to_apply=%region_23.24 | all-reduce | flops 512 | bytes 4096 | tf_op jit(solution)/shard_map/psum | solution.py:552
  592.0 412.1 %all-reduce.6.cloned.1.call-done = (bf16[1024,256]{1,0:T(8,128)(2,1)}, bf16[1024,256]{1,0:T(8,128)(2,1)}, bf16[1024,256]{1,0:T(8,128)(2,1)}, bf16[1024,256]{1,0:...) async-done(((bf16[1024,256]{1,0:T(8,128)(2,1)}, ...) | async-done | bytes 14680080 | tf_op jit(solution)/shard_map/psum | solution.py:356
  1004.0 3.2 fusion.42
  1007.2 1.8 fusion.39
  1009.0 2.9 fusion.26
  1011.9 2.9 fusion.23
  1014.8 5.0 fusion.20
  1019.8 2.9 fusion.17
  1022.8 2.9 fusion.14
  1025.7 5.0 fusion.11
  (186 shorter events, 21.8 us)
Async XLA Ops:
  7.2 7.7 copy-start.22
  7.2 996.8 %all-reduce.6.cloned.1.call-start = ((), (), s32[]{:S(2)}) async-start(), calls=%async_computation | async-start | bytes 29360128 | tf_op jit(solution)/shard_map/psum | solution.py:356
  9.7 139.4 %collective-permute-start = (bf16[1024,256]{1,0:T(8,128)(2,1)}, bf16[1024,256]{1,0:T(8,128)(2,1)}, u32[]{:S(2)}, u32[]{:S(2)}) collective-permute-start(bf16[1024,256]{1,0:T(8,128)(2,1)} %get-tuple-element.162), channel_id=1, source_target_pairs={{0,4},{4,0},{1,5},{5,1},{2,6},{6,2},{3,7},{7,3},{8,12},{12,8},{9,1... | collective-permute-start | bytes 1572872 | tf_op jit(solution)/shard_map/ppermute | solution.py:337
  14.9 134.8 %collective-permute-start.1 = (bf16[1024,256]{1,0:T(8,128)(2,1)}, bf16[1024,256]{1,0:T(8,128)(2,1)}, u32[]{:S(2)}, u32[]{:S(2)}) collective-permute-start(bf16[1024,256]{1,0:T(8,128)(2,1)} %get-tuple-element.164), channel_id=1, source_target_pairs={{0,4},{4,0},{1,5},{5,1},{2,6},{6,2},{3,7},{7,3},{8,12},{12,8},{9,1... | collective-permute-start | bytes 1572872 | tf_op jit(solution)/shard_map/ppermute | solution.py:337
  14.9 3.3 copy-start.23
  16.1 135.6 %copy-start.34 = (bf16[1024,512]{1,0:T(8,128)(2,1)}, bf16[1024,512]{1,0:T(8,128)(2,1)S(1)}, u32[]{:S(2)}) copy-start(bf16[1024,512]{1,0:T(8,128)(2,1)S(1)} %get-tuple-element.146) | copy-start | bytes 3145732
  16.1 4.3 copy-start.24
  16.1 135.0 %collective-permute-start.2 = (bf16[1024,512]{1,0:T(8,128)(2,1)}, bf16[1024,512]{1,0:T(8,128)(2,1)}, u32[]{:S(2)}, u32[]{:S(2)}) collective-permute-start(bf16[1024,512]{1,0:T(8,128)(2,1)} %get-tuple-element.147), channel_id=1, source_target_pairs={{0,4},{4,0},{1,5},{5,1},{2,6},{6,2},{3,7},{7,3},{8,12},{12,8},{9,1... | collective-permute-start | bytes 3145736 | tf_op jit(solution)/shard_map/ppermute | solution.py:337
  19.7 3.5 copy-start.25
  19.7 132.0 %collective-permute-start.3 = (bf16[1024,512]{1,0:T(8,128)(2,1)}, bf16[1024,512]{1,0:T(8,128)(2,1)}, u32[]{:S(2)}, u32[]{:S(2)}) collective-permute-start(bf16[1024,512]{1,0:T(8,128)(2,1)} %get-tuple-element.149), channel_id=1, source_target_pairs={{0,4},{4,0},{1,5},{5,1},{2,6},{6,2},{3,7},{7,3},{8,12},{12,8},{9,1... | collective-permute-start | bytes 3145736 | tf_op jit(solution)/shard_map/ppermute | solution.py:337
  21.9 164.1 %collective-permute-start.4 = (bf16[512,1024]{1,0:T(8,128)(2,1)}, bf16[512,1024]{1,0:T(8,128)(2,1)}, u32[]{:S(2)}, u32[]{:S(2)}) collective-permute-start(bf16[512,1024]{1,0:T(8,128)(2,1)} %get-tuple-element.151), channel_id=1, source_target_pairs={{0,4},{4,0},{1,5},{5,1},{2,6},{6,2},{3,7},{7,3},{8,12},{12,8},{9,1... | collective-permute-start | bytes 3145736 | tf_op jit(solution)/shard_map/ppermute | solution.py:337
  29.0 122.7 %copy-start.35 = (bf16[1024,512]{1,0:T(8,128)(2,1)S(1)}, bf16[1024,512]{1,0:T(8,128)(2,1)}, u32[]{:S(2)}) copy-start(bf16[1024,512]{1,0:T(8,128)(2,1)} %get-tuple-element.148) | copy-start | bytes 3145732
  29.1 122.7 %copy-start.57 = (bf16[1024,256]{1,0:T(8,128)(2,1)S(1)}, bf16[1024,256]{1,0:T(8,128)(2,1)}, u32[]{:S(2)}) copy-start(bf16[1024,256]{1,0:T(8,128)(2,1)} %get-tuple-element.161) | copy-start | bytes 1572868
  147.1 30.2 %copy-start.4 = (f32[8,128]{1,0:T(8,128)}, f32[8,128]{1,0:T(8,128)S(1)}, u32[]{:S(2)}) copy-start(f32[8,128]{1,0:T(8,128)S(1)} %get-tuple-element.85) | copy-start | bytes 12292
  149.0 29.9 %copy-start.13 = (f32[1024,128]{1,0:T(8,128)}, f32[1024,128]{1,0:T(8,128)S(1)}, u32[]{:S(2)}) copy-start(f32[1024,128]{1,0:T(8,128)S(1)} %get-tuple-element.172) | copy-start | bytes 1572868
  149.1 109.0 %collective-permute-start.5 = (bf16[1024,512]{1,0:T(8,128)(2,1)}, bf16[1024,512]{1,0:T(8,128)(2,1)}, u32[]{:S(2)}, u32[]{:S(2)}) collective-permute-start(bf16[1024,512]{1,0:T(8,128)(2,1)} %get-tuple-element.143), channel_id=1, source_target_pairs={{0,4},{4,0},{1,5},{5,1},{2,6},{6,2},{3,7},{7,3},{8,12},{12,8},{9,1... | collective-permute-start | bytes 3145736 | tf_op jit(solution)/shard_map/ppermute | solution.py:337
  149.7 108.4 %collective-permute-start.6 = (bf16[1024,512]{1,0:T(8,128)(2,1)}, bf16[1024,512]{1,0:T(8,128)(2,1)}, u32[]{:S(2)}, u32[]{:S(2)}) collective-permute-start(bf16[1024,512]{1,0:T(8,128)(2,1)} %get-tuple-element.145), channel_id=1, source_target_pairs={{0,4},{4,0},{1,5},{5,1},{2,6},{6,2},{3,7},{7,3},{8,12},{12,8},{9,1... | collective-permute-start | bytes 3145736 | tf_op jit(solution)/shard_map/ppermute | solution.py:337
  151.2 113.1 %collective-permute-start.7 = (bf16[512,1024]{1,0:T(8,128)(2,1)}, bf16[512,1024]{1,0:T(8,128)(2,1)}, u32[]{:S(2)}, u32[]{:S(2)}) collective-permute-start(bf16[512,1024]{1,0:T(8,128)(2,1)} %get-tuple-element.141), channel_id=1, source_target_pairs={{0,4},{4,0},{1,5},{5,1},{2,6},{6,2},{3,7},{7,3},{8,12},{12,8},{9,1... | collective-permute-start | bytes 3145736 | tf_op jit(solution)/shard_map/ppermute | solution.py:337
  181.1 4.0 copy-start.32
  181.1 160.2 %copy-start.20 = (bf16[1024,256]{1,0:T(8,128)(2,1)}, bf16[1024,256]{1,0:T(8,128)(2,1)S(1)}, u32[]{:S(2)}) copy-start(bf16[1024,256]{1,0:T(8,128)(2,1)S(1)} %get-tuple-element.115) | copy-start | bytes 1572868
  181.5 3.5 copy-start.30
  185.0 6.0 copy-start.53
  191.1 45.8 %copy-start.62 = (f32[256]{0:T(256)S(1)}, f32[256]{0:T(256)}, u32[]{:S(2)}) copy-start(f32[256]{0:T(256)} %param.37) | copy-start | bytes 3076
  191.1 67.0 %copy-start.39 = (bf16[1024,512]{1,0:T(8,128)(2,1)S(1)}, bf16[1024,512]{1,0:T(8,128)(2,1)}, u32[]{:S(2)}) copy-start(bf16[1024,512]{1,0:T(8,128)(2,1)} %get-tuple-element.142) | copy-start | bytes 3145732
  191.1 67.0 %copy-start.40 = (bf16[1024,512]{1,0:T(8,128)(2,1)S(1)}, bf16[1024,512]{1,0:T(8,128)(2,1)}, u32[]{:S(2)}) copy-start(bf16[1024,512]{1,0:T(8,128)(2,1)} %get-tuple-element.144) | copy-start | bytes 3145732
  258.1 6.1 copy-start.36
  285.1 43.8 %slice-start = ((s8[6291456]{0:T(1024)(128)(4,1)}), s8[2097152]{0:T(1024)(128)(4,1)S(1)}, s32[]{:S(2)}) async-start(s8[6291456]{0:T(1024)(128)(4,1)} %bitcast.82), calls=%async_computation.1 | async-start | bytes 4194304
  307.4 21.6 %slice-start.1 = ((s8[6291456]{0:T(1024)(128)(4,1)}), s8[4194304]{0:T(1024)(128)(4,1)S(1)}, s32[]{:S(2)}) async-start(s8[6291456]{0:T(1024)(128)(4,1)} %bitcast.82), calls=%async_computation.2 | async-start | bytes 8388608
  329.0 4.1 copy-start.38
  339.4 15.9 %copy-start.11 = (f32[1024,512]{1,0:T(8,128)}, f32[1024,512]{1,0:T(8,128)S(1)}, u32[]{:S(2)}) copy-start(f32[1024,512]{1,0:T(8,128)S(1)} %get-tuple-element.113) | copy-start | bytes 6291460
  347.1 4.7 copy-start.21
  348.7 4.0 copy-start.54
  348.7 94.7 %collective-permute-start.15 = (bf16[512,1024]{1,0:T(8,128)(2,1)}, bf16[512,1024]{1,0:T(8,128)(2,1)}, u32[]{:S(2)}, u32[]{:S(2)}) collective-permute-start(bf16[512,1024]{1,0:T(8,128)(2,1)} %get-tuple-element.136), channel_id=1, source_target_pairs={{0,4},{4,0},{1,5},{5,1},{2,6},{6,2},{3,7},{7,3},{8,12},{12,8},{9,1... | collective-permute-start | bytes 3145736 | tf_op jit(solution)/shard_map/ppermute | solution.py:337
  349.8 94.6 %collective-permute-start.14 = (bf16[1024,512]{1,0:T(8,128)(2,1)}, bf16[1024,512]{1,0:T(8,128)(2,1)}, u32[]{:S(2)}, u32[]{:S(2)}) collective-permute-start(bf16[1024,512]{1,0:T(8,128)(2,1)} %get-tuple-element.130), channel_id=1, source_target_pairs={{0,4},{4,0},{1,5},{5,1},{2,6},{6,2},{3,7},{7,3},{8,12},{12,8},{9,1... | collective-permute-start | bytes 3145736 | tf_op jit(solution)/shard_map/ppermute | solution.py:337
  350.7 93.7 %collective-permute-start.13 = (bf16[1024,512]{1,0:T(8,128)(2,1)}, bf16[1024,512]{1,0:T(8,128)(2,1)}, u32[]{:S(2)}, u32[]{:S(2)}) collective-permute-start(bf16[1024,512]{1,0:T(8,128)(2,1)} %get-tuple-element.132), channel_id=1, source_target_pairs={{0,4},{4,0},{1,5},{5,1},{2,6},{6,2},{3,7},{7,3},{8,12},{12,8},{9,1... | collective-permute-start | bytes 3145736 | tf_op jit(solution)/shard_map/ppermute | solution.py:337
  354.9 2.9 copy-start.7
  355.3 11.1 %copy-start.15 = (f32[1024,256]{1,0:T(8,128)}, f32[1024,256]{1,0:T(8,128)S(1)}, u32[]{:S(2)}) copy-start(f32[1024,256]{1,0:T(8,128)S(1)} %get-tuple-element.155) | copy-start | bytes 3145732
  355.3 11.1 %copy-start.17 = (f32[1024,256]{1,0:T(8,128)}, f32[1024,256]{1,0:T(8,128)S(1)}, u32[]{:S(2)}) copy-start(f32[1024,256]{1,0:T(8,128)S(1)} %get-tuple-element.156) | copy-start | bytes 3145732
  366.4 3.2 copy-start.28
  367.5 63.6 %collective-permute-start.9 = (bf16[1024,256]{1,0:T(8,128)(2,1)S(1)}, bf16[1024,256]{1,0:T(8,128)(2,1)S(1)}, u32[]{:S(2)}, u32[]{:S(2)}) collective-permute-start(bf16[1024,256]{1,0:T(8,128)(2,1)S(1)} %get-tuple-element.120), channel_id=1, source_target_pairs={{0,4},{4,0},{1,5},{5,1},{2,6},{6,2},{3,7},{7,3},{8,12},{12,8},{9,1... | collective-permute-start | bytes 1572872 | tf_op jit(solution)/shard_map/ppermute | solution.py:337
  368.5 73.9 %collective-permute-start.8 = (bf16[1024,256]{1,0:T(8,128)(2,1)S(1)}, bf16[1024,256]{1,0:T(8,128)(2,1)S(1)}, u32[]{:S(2)}, u32[]{:S(2)}) collective-permute-start(bf16[1024,256]{1,0:T(8,128)(2,1)S(1)} %get-tuple-element.122), channel_id=1, source_target_pairs={{0,4},{4,0},{1,5},{5,1},{2,6},{6,2},{3,7},{7,3},{8,12},{12,8},{9,1... | collective-permute-start | bytes 1572872 | tf_op jit(solution)/shard_map/ppermute | solution.py:337
  431.1 78.2 %copy-start.55 = (bf16[1024,256]{1,0:T(8,128)(2,1)}, bf16[1024,256]{1,0:T(8,128)(2,1)S(1)}, u32[]{:S(2)}) copy-start(bf16[1024,256]{1,0:T(8,128)(2,1)S(1)} %collective-permute-done.9) | copy-start | bytes 1572868
  431.1 33.8 %collective-permute-start.12 = (bf16[512,1024]{1,0:T(8,128)(2,1)S(1)}, bf16[512,1024]{1,0:T(8,128)(2,1)}, u32[]{:S(2)}, u32[]{:S(2)}) collective-permute-start(bf16[512,1024]{1,0:T(8,128)(2,1)S(1)} %get-tuple-element.138), channel_id=1, source_target_pairs={{0,4},{4,0},{1,5},{5,1},{2,6},{6,2},{3,7},{7,3},{8,12},{12,8},{9,1... | collective-permute-start | bytes 3145736 | tf_op jit(solution)/shard_map/ppermute | solution.py:337
  442.3 67.0 %copy-start.56 = (bf16[1024,256]{1,0:T(8,128)(2,1)}, bf16[1024,256]{1,0:T(8,128)(2,1)S(1)}, u32[]{:S(2)}) copy-start(bf16[1024,256]{1,0:T(8,128)(2,1)S(1)} %collective-permute-done.8) | copy-start | bytes 1572868
  442.3 45.0 %collective-permute-start.11 = (bf16[1024,512]{1,0:T(8,128)(2,1)S(1)}, bf16[1024,512]{1,0:T(8,128)(2,1)}, u32[]{:S(2)}, u32[]{:S(2)}) collective-permute-start(bf16[1024,512]{1,0:T(8,128)(2,1)S(1)} %get-tuple-element.116), channel_id=1, source_target_pairs={{0,4},{4,0},{1,5},{5,1},{2,6},{6,2},{3,7},{7,3},{8,12},{12,8},{9,1... | collective-permute-start | bytes 3145736 | tf_op jit(solution)/shard_map/ppermute | solution.py:337
  443.4 65.9 %collective-permute-start.10 = (bf16[1024,512]{1,0:T(8,128)(2,1)S(1)}, bf16[1024,512]{1,0:T(8,128)(2,1)}, u32[]{:S(2)}, u32[]{:S(2)}) collective-permute-start(bf16[1024,512]{1,0:T(8,128)(2,1)S(1)} %get-tuple-element.118), channel_id=1, source_target_pairs={{0,4},{4,0},{1,5},{5,1},{2,6},{6,2},{3,7},{7,3},{8,12},{12,8},{9,1... | collective-permute-start | bytes 3145736 | tf_op jit(solution)/shard_map/ppermute | solution.py:337
  509.3 26.8 %copy-start.18 = (f32[1024,256]{1,0:T(8,128)S(1)}, f32[1024,256]{1,0:T(8,128)}, u32[]{:S(2)}) copy-start(f32[1024,256]{1,0:T(8,128)} %copy-done.17) | copy-start | bytes 3145732
  513.6 22.5 %copy-start.9 = (f32[1024,512]{1,0:T(8,128)S(1)}, f32[1024,512]{1,0:T(8,128)}, u32[]{:S(2)}) copy-start(f32[1024,512]{1,0:T(8,128)} %copy-done.8) | copy-start | bytes 6291460
  513.6 22.5 %copy-start.12 = (f32[1024,512]{1,0:T(8,128)S(1)}, f32[1024,512]{1,0:T(8,128)}, u32[]{:S(2)}) copy-start(f32[1024,512]{1,0:T(8,128)} %copy-done.11) | copy-start | bytes 6291460
  513.6 22.5 %copy-start.16 = (f32[1024,256]{1,0:T(8,128)S(1)}, f32[1024,256]{1,0:T(8,128)}, u32[]{:S(2)}) copy-start(f32[1024,256]{1,0:T(8,128)} %copy-done.15) | copy-start | bytes 3145732
  552.8 24.5 %copy-start.65 = (f32[256]{0:T(256)S(1)}, f32[256]{0:T(256)}, u32[]{:S(2)}) copy-start(f32[256]{0:T(256)} %param.36) | copy-start | bytes 3076
  555.0 22.2 %copy-start.5 = (f32[8,128]{1,0:T(8,128)S(1)}, f32[8,128]{1,0:T(8,128)}, u32[]{:S(2)}) copy-start(f32[8,128]{1,0:T(8,128)} %copy-done.4) | copy-start | bytes 12292
  555.0 22.3 %copy-start.3 = (f32[1024,256]{1,0:T(8,128)S(1)}, f32[1024,256]{1,0:T(8,128)}, u32[]{:S(2)}) copy-start(f32[1024,256]{1,0:T(8,128)} %copy-done.2) | copy-start | bytes 3145732
  1004.0 3.2 copy-start.58
  1004.0 3.2 copy-start.59
  1004.0 4.9 copy-start.51
  1004.0 4.9 copy-start.52
  1009.0 2.9 copy-start.50
  1011.9 2.9 copy-start.47
  1011.9 2.9 copy-start.48
  1014.8 5.0 copy-start.45
  1014.8 5.0 copy-start.46
  1019.8 2.9 copy-start.44
  1022.7 2.9 copy-start.42
  (22 other events, 43.7 us)
Sparse Core Ops, SparseCore 0:
  509.4 494.5 all-reduce.5

commit v2 on v1

--- a/solution.py
+++ b/solution.py
@@ -344,19 +344,453 @@
     return mine, theirs
 
 
-def whole_weight(values, axis, r):
-    mine, theirs = halves_of(values, axis, r)
-    return jnp.concatenate([mine, swap_rows(theirs)], axis=1 - axis)
-
-
-def sum_packs(grad, axis, r):
-    size = grad.shape[1 - axis] // 2
-    mine = lax.slice_in_dim(grad, 0, size, axis=1 - axis)
-    theirs = swap_rows(lax.slice_in_dim(grad, size, 2 * size, axis=1 - axis))
-    mine, theirs = lax.psum((mine, theirs), "dp")
+def swap_shared(values):
+    size = values.shape[0] // lax.axis_size("dp")
+    part = lax.dynamic_slice_in_dim(values, lax.axis_index("dp") * size, size, 0)
+    return lax.all_gather(swap_rows(part), "dp", axis=0, tiled=True)
+
+
+PIECE = 128
+GROUP = 8
+OUT_UNIT = 2
+UNITS = 6
+
+
+def last_kernel(
+    wide_one,
+    wide_two,
+    wide_att,
+    gated,
+    both_low,
+    weight,
+    all_low,
+    block_in,
+    inner_vec,
+    second_vec,
+    result,
+    back,
+    inner_out,
+    gains,
+    part,
+    from_edge,
+    from_inner,
+    big,
+    small,
+    stream,
+    rows_part,
+    rows_core,
+    rows_x,
+    rows_y,
+    total_got,
+    gain_own,
+    gain_got,
+    load_sem,
+    local_sem,
+    plane_send,
+    plane_recv,
+    gain_send,
+    gain_recv,
+    *line_sems,
+):
+    z, r, c = lax.axis_index("dp"), lax.axis_index("row"), lax.axis_index("col")
+    _, _, core, across = neighbours()
+    barrier = pltpu.get_barrier_semaphore()
+    peers = [{"dp": lax.rem(z + k, 4)} for k in (1, 2, 3)]
+    peers += [{"row": 1 - r}, {"col": core}, {"col": across}]
+    for target in peers:
+        pl.semaphore_signal(barrier, inc=1, device_id=target, device_id_type=MESH)
+    tokens, width = back.shape
+    half = tokens // 2
+
+    def load(slot, src, dst):
+        return pltpu.make_async_copy(src, dst, load_sem.at[slot])
+
+    hidden_cols = small.shape[2]
+    loads = [
+        load(0, wide_two, big.at[0]),
+        load(1, both_low.at[:, hidden_cols:], small.at[0]),
+        load(2, both_low.at[:, :hidden_cols], small.at[1]),
+        load(3, wide_att, big.at[1]),
+        load(4, gated, small.at[0]),
+        load(5, wide_one, big.at[0]),
+    ]
+    for i in range(4):
+        loads[i].start()
+
+    places = (4 + across, across, 4 + c, c)
+    other = core - c
+
+    def weight_load(i):
+        place = places[i % 4] + (other if i < 4 else 0)
+        rows = pl.ds(pl.multiple_of(place * width, width), width)
+        return load(6 + i % 2, weight.at[rows], stream.at[i % 2])
+
+    weight_load(0).start()
+    weight_load(1).start()
+    pl.semaphore_wait(barrier, len(peers))
+
+    is_edge = (z == 0) | (z == 3)
+    is_inner = (z == 1) | (z == 2)
+    near = jnp.where(z < 2, 1 - z, 5 - z)
+    far = 3 - z
+    flip = jnp.where((z == 0) | (z == 1), 1, 0)
+    steps = UNITS * GROUP // 2
+
+    def copy(stream_number, slot, src, dst, target):
+        send_sem, recv_sem = line_sems[2 * stream_number], line_sems[2 * stream_number + 1]
+        return pltpu.make_async_remote_copy(
+            src_ref=src,
+            dst_ref=dst,
+            send_sem=send_sem.at[slot],
+            recv_sem=recv_sem.at[slot],
+            device_id=target,
+            device_id_type=MESH,
+        )
+
+    def theirs_pair(q):
+        return 2 * q + flip
+
+    def mine_pair(q):
+        return 2 * q + 1 - flip
+
+    def final(pair, slot):
+        unit, place = pair // GROUP, lax.rem(pair, GROUP)
+        is_out = unit == OUT_UNIT
+        row = jnp.where(is_out, slot * 512 + (place // 2) * PIECE, place * PIECE)
+        col = jnp.where(is_out, lax.rem(place, 2) * 512, slot * 512)
+        return result.at[
+            unit,
+            pl.ds(pl.multiple_of(row, PIECE), PIECE),
+            pl.ds(pl.multiple_of(col, 512), 512),
+        ]
+
+    def edge_copy(pair):
+        return copy(0, pair, part.at[pair], from_edge.at[pair], {"dp": near})
+
+    def inner_copy(q):
+        return copy(1, q, part.at[theirs_pair(q)], from_inner.at[q], {"dp": far})
+
+    def row_copy(q):
+        pair = mine_pair(q)
+        return copy(2, q, part.at[pair, 1 - r], final(pair, r), {"row": 1 - r})
+
+    def row_arrival(q):
+        pair = mine_pair(q)
+        return copy(2, q, part.at[pair, 1 - r], final(pair, 1 - r), {"row": 1 - r})
+
+    def keep_copy(q):
+        pair = mine_pair(q)
+        return pltpu.make_async_copy(part.at[pair, r], final(pair, r), local_sem.at[q])
+
+    def own_copy(stream_number, q, pair, target):
+        return copy(stream_number, q, part.at[pair, r], final(pair, r), {"dp": target})
+
+    def got_copy(stream_number, q, pair, target):
+        return copy(stream_number, q, final(pair, 1 - r), final(pair, 1 - r), {"dp": target})
+
+    def pass_copy(slot, q, pair):
+        return copy(7 + slot, q, final(pair, slot), final(pair, slot), {"dp": near})
+
+    def compute(unit, x_ref, g_ref, shift=0):
+        def body(j, carry):
+            step, k = j // 2, lax.rem(j, 2)
+            k = k + flip - 2 * k * flip
+            place = 2 * step + k
+            pair = unit * GROUP + place
+            for slot in range(2):
+                if unit == OUT_UNIT:
+                    rows, cols = place // 2, lax.rem(place, 2) + 2 * slot
+                else:
+                    rows, cols = place + GROUP * slot, shift
+                x = x_ref[:, pl.ds(pl.multiple_of(rows * PIECE, PIECE), PIECE)]
+                g = g_ref[:, pl.ds(pl.multiple_of(cols * 512, 512), 512)]
+                value = lax.dot_general(
+                    x, g, (((0,), (0,)), ((), ())), preferred_element_type=F32
+                )
+                part[pair, r if slot == 0 else 1 - r] = value.astype(BF16)
+
+            @pl.when(is_edge)
+            def _():
+                edge_copy(pair).start()
+
+            return carry
+
+        lax.fori_loop(0, GROUP, body, 0)
+
+    def stage_far(q):
+        pair = theirs_pair(q)
+        edge_copy(pair).wait_recv()
+        part[pair] = (part[pair].astype(F32) + from_edge[pair].astype(F32)).astype(BF16)
+        inner_copy(q).start()
+
+    def stage_sum(q):
+        pair = mine_pair(q)
+        edge_copy(pair).wait_recv()
+        inner_copy(q).wait_recv()
+        total = part[pair].astype(F32) + from_edge[pair].astype(F32) + from_inner[q].astype(F32)
+        part[pair] = total.astype(BF16)
+        row_copy(q).start()
+        own_copy(3, q, pair, near).start()
+        own_copy(4, q, pair, far).start()
+        keep_copy(q).start()
+
+    def stage_out(q):
+        pair = mine_pair(q)
+        row_arrival(q).wait_recv()
+        got_copy(5, q, pair, near).start()
+        got_copy(6, q, pair, far).start()
+
+    def stage_pass(q):
+        pair = theirs_pair(q)
+        own_copy(4, q, pair, far).wait_recv()
+        got_copy(6, q, pair, far).wait_recv()
+        pass_copy(0, q, pair).start()
+        pass_copy(1, q, pair).start()
+
+    def step(q):
+        for lag, stage in enumerate((stage_far, stage_sum, stage_out, stage_pass)):
+
+            @pl.when((q >= lag) & (q < steps + lag))
+            def _():
+                stage(q - lag)
+
+    def run_steps(first, last):
+        @pl.when(is_inner)
+        def _():
+            lax.fori_loop(first, last, lambda q, carry: (step(q), carry)[1], 0)
+
+    send = Sender(plane_send, plane_recv)
+    to_core, to_x, to_y = {"col": core}, {"col": across}, {"row": 1 - r}
+    lo, hi = slice(0, half), slice(half, 2 * half)
+    state = {}
+
+    def product(i):
+        weight_load(i).wait()
+
+        def body(k, carry):
+            rows = pl.ds(pl.multiple_of(k * 256, 256), 256)
+            value = lax.dot_general(
+                all_low[rows],
+                stream[i % 2],
+                (((1,), (1,)), ((), ())),
+                preferred_element_type=F32,
+            )
+            rows_part[i, rows] = value.astype(BF16)
+            return carry
+
+        lax.fori_loop(0, tokens // 256, body, 0)
+        if i < 6:
+            weight_load(i + 2).start()
+
+    def summed(i, rows):
+        return rows_part[4 + i, rows].astype(F32) + rows_core[i, rows].astype(F32)
+
+    def phase_products():
+        state["side"] = total_side(inner_vec, inner_out, total_got)(send, to_core, to_x, to_y)
+        state["first"] = []
+        for i in range(4):
+            product(i)
+            state["first"].append(send(rows_part.at[i], rows_core.at[i], to_core))
+        next(state["side"])
+
+    def phase_first():
+        first = state["first"]
+        for i in range(4):
+            product(4 + i)
+        first[0].wait_recv()
+        rows_part[4, lo] = summed(0, lo).astype(BF16)
+        state["dx"] = send(rows_part.at[4, lo], rows_x.at[2], to_x)
+        rows_part[4, hi] = summed(0, hi).astype(BF16)
+        state["dy"] = send(rows_part.at[4, hi], rows_y.at[2], to_y)
+        first[1].wait_recv()
+        rows_part[5, lo] = summed(1, lo).astype(BF16)
+        state["x0"] = send(rows_part.at[5, lo], rows_x.at[0], to_x)
+        first[2].wait_recv()
+        rows_part[6, hi] = summed(2, hi).astype(BF16)
+        state["y1"] = send(rows_part.at[6, hi], rows_y.at[1], to_y)
+        next(state["side"])
+
+    def phase_second():
+        state["dy"].wait_recv()
+        rows_part[5, hi] = (summed(1, hi) + rows_y[2].astype(F32)).astype(BF16)
+        state["x1"] = send(rows_part.at[5, hi], rows_x.at[1], to_x)
+        state["dx"].wait_recv()
+        rows_part[6, lo] = (summed(2, lo) + rows_x[2].astype(F32)).astype(BF16)
+        state["y0"] = send(rows_part.at[6, lo], rows_y.at[0], to_y)
+        next(state["side"])
+
+    def phase_third():
+        state["first"][3].wait_recv()
+        state["x0"].wait_recv()
+        state["y1"].wait_recv()
+        state["x1"].wait_recv()
+        state["y0"].wait_recv()
+        back[lo] = summed(3, lo) + rows_x[0].astype(F32) + rows_y[0].astype(F32)
+        back[hi] = summed(3, hi) + rows_y[1].astype(F32) + rows_x[1].astype(F32)
+        first_gain = jnp.sum(back[...] * block_in[...].astype(F32), axis=0, keepdims=True)
+        gain_own[0:1] = first_gain
+        gain_own[1:2] = second_vec[...]
+        for each in gain_copies:
+            each.start()
+
+    gain_copies = [
+        pltpu.make_async_remote_copy(
+            src_ref=gain_own,
+            dst_ref=gain_got.at[k - 1],
+            send_sem=gain_send.at[k - 1],
+            recv_sem=gain_recv.at[k - 1],
+            device_id={"dp": lax.rem(z + k, 4)},
+            device_id_type=MESH,
+        )
+        for k in (1, 2, 3)
+    ]
+
+    loads[0].wait()
+    loads[1].wait()
+    compute(0, big.at[0], small.at[0])
+    loads[4].start()
+    phase_products()
+    run_steps(0, 1)
+    phase_first()
+    run_steps(1, 3)
+    loads[2].wait()
+    compute(1, big.at[0], small.at[1])
+    loads[5].start()
+    run_steps(3, 4)
+    phase_second()
+    run_steps(4, 7)
+    loads[3].wait()
+    loads[4].wait()
+    compute(2, small.at[0], big.at[1])
+    phase_third()
+    run_steps(7, 11)
+    loads[5].wait()
+    compute(3, big.at[0], all_low, 0)
+    run_steps(11, 15)
+    compute(4, big.at[0], all_low, 1)
+    run_steps(15, 19)
+    compute(5, big.at[0], all_low, 2)
+    run_steps(19, steps + 3)
+
+    total = gain_own[...]
+    for each in gain_copies:
+        each.wait_send()
+    for k in range(3):
+        gain_copies[k].wait_recv()
+        total = total + gain_got[k]
+    gains[...] = total
+    for each in send.started:
+        each.wait_send()
+
+    @pl.when(is_inner)
+    def _():
+        def body(q, carry):
+            pair = mine_pair(q)
+            inner_copy(q).wait_send()
+            row_copy(q).wait_send()
+            own_copy(3, q, pair, near).wait_send()
+            own_copy(4, q, pair, far).wait_send()
+            got_copy(5, q, pair, near).wait_send()
+            got_copy(6, q, pair, far).wait_send()
+            keep_copy(q).wait()
+            for slot in range(2):
+                pass_copy(slot, q, theirs_pair(q)).wait_send()
+            return carry
+
+        lax.fori_loop(0, steps, body, 0)
+
+    @pl.when(is_edge)
+    def _():
+        def body(q, carry):
+            edge_copy(theirs_pair(q)).wait_send()
+            edge_copy(mine_pair(q)).wait_send()
+            own_copy(3, q, mine_pair(q), near).wait_recv()
+            got_copy(5, q, mine_pair(q), near).wait_recv()
+            for slot in range(2):
+                pass_copy(slot, q, theirs_pair(q)).wait_recv()
+            return carry
+
+        lax.fori_loop(0, steps, body, 0)
+
+
+def last_scatter(wide_one, wide_two, wide_att, gated, both_low, weight, all_low, own, inner, second):
+    tokens, width = own.shape
+    small = (tokens // 128, 128)
+    pairs = UNITS * GROUP
+    steps = pairs // 2
+    shape = (pairs, 2, PIECE, 512)
+    half = tokens // 2
+    gain_shape = (8, width)
+    scratch = [
+        pltpu.VMEM(shape, BF16),
+        pltpu.VMEM(shape, BF16),
+        pltpu.VMEM((steps,) + shape[1:], BF16),
+        pltpu.VMEM((2,) + wide_one.shape, BF16),
+        pltpu.VMEM((2,) + gated.shape, BF16),
+        pltpu.VMEM((2, width, weight.shape[1]), BF16),
+        pltpu.VMEM((8, tokens, width), BF16),
+        pltpu.VMEM((4, tokens, width), BF16),
+        pltpu.VMEM((3, half, width), BF16),
+        pltpu.VMEM((3, half, width), BF16),
+        pltpu.VMEM((5,) + small, F32),
+        pltpu.VMEM(gain_shape, F32),
+        pltpu.VMEM((3,) + gain_shape, F32),
+        pltpu.SemaphoreType.DMA((8,)),
+        pltpu.SemaphoreType.DMA((steps,)),
+        pltpu.SemaphoreType.DMA((13,)),
+        pltpu.SemaphoreType.DMA((13,)),
+        pltpu.SemaphoreType.DMA((3,)),
+        pltpu.SemaphoreType.DMA((3,)),
+    ]
+    for size in (pairs,) + (steps,) * 8:
+        scratch += [pltpu.SemaphoreType.DMA((size,))] * 2
+    anywhere = pl.BlockSpec(memory_space=pl.ANY)
+    result, back, total, gains = pl.pallas_call(
+        last_kernel,
+        out_shape=(
+            jax.ShapeDtypeStruct((UNITS, 1024, 1024), BF16),
+            jax.ShapeDtypeStruct((tokens, width), F32),
+            jax.ShapeDtypeStruct(small, F32),
+            jax.ShapeDtypeStruct(gain_shape, F32),
+        ),
+        in_specs=[anywhere] * 6 + vmem(4),
+        out_specs=(anywhere,) + tuple(vmem(3)),
+        scratch_shapes=scratch,
+        compiler_params=pltpu.CompilerParams(
+            collective_id=4, has_side_effects=True, vmem_limit_bytes=62 << 20
+        ),
+        name="last_scatter",
+    )(
+        wide_one,
+        wide_two,
+        wide_att,
+        gated,
+        both_low,
+        weight,
+        all_low,
+        own,
+        inner.reshape(small),
+        second.reshape(1, width),
+    )
+    return result, back, total.reshape(tokens), gains[0], gains[1]
+
+
+def place_halves(mine, theirs, axis, r):
     both = jnp.concatenate([mine, theirs, mine], axis=axis)
     width = mine.shape[axis]
     return lax.dynamic_slice_in_dim(both, r * width, 2 * width, axis).astype(F32)
+
+
+def sum_packs(grads):
+    r = lax.axis_index("row")
+    totals = lax.psum(tuple(grad for grad, axis in grads), "dp")
+    placed = []
+    for total, (grad, axis) in zip(totals, grads):
+        size = total.shape[1 - axis] // 2
+        mine = lax.slice_in_dim(total, 0, size, axis=1 - axis)
+        theirs = swap_rows(lax.slice_in_dim(total, size, 2 * size, axis=1 - axis))
+        placed.append(place_halves(mine, theirs, axis, r))
+    return placed
 
 
 def matmul(left, right):
@@ -457,27 +891,36 @@
     log_decay = jnp.log(1.0 - 2.0 ** (-5.0 - head_index.astype(jnp.float32)))
     cosine_table, sine_table = rotary_tables(tokens, KD)
 
-    first_weight = jnp.concatenate(
-        [
-            whole_weight(query_weight, 1, r),
-            whole_weight(key_weight, 1, r),
-            whole_weight(value_weight, 1, r),
-            whole_weight(swish_weight, 1, r),
-        ],
+    heads = [halves_of(w, 1, r) for w in (query_weight, key_weight, value_weight, swish_weight)]
+    first_mine = jnp.concatenate([mine for mine, _ in heads], axis=1)
+    first_theirs = jnp.concatenate(
+        [swap_shared(jnp.concatenate([theirs for _, theirs in heads[:3]], axis=1)), swap_rows(heads[3][1])],
         axis=1,
     )
-    out_weight = whole_weight(output_weight, 0, r)
-    second_weight = jnp.concatenate(
-        [whole_weight(gelu_weight, 1, r), whole_weight(up_weight, 1, r)], axis=1
-    )
-    last_weight = whole_weight(down_weight, 0, r)
-    value_cols = out_weight.shape[0]
+    units = [halves_of(gelu_weight, 1, r), halves_of(up_weight, 1, r)]
+    ends = [halves_of(output_weight, 0, r), halves_of(down_weight, 0, r)]
+    value_cols = ends[0][0].shape[0]
+    hidden_cols = ends[1][0].shape[0]
+    rest = swap_shared(
+        jnp.concatenate(
+            [units[0][1], units[1][1], jnp.concatenate([ends[0][1], ends[1][1]], axis=0)], axis=1
+        )
+    )
+    second_mine = jnp.concatenate([units[0][0], units[1][0]], axis=1)
+    second_theirs = rest[:, : 2 * hidden_cols]
+    out_weight = jnp.concatenate([ends[0][0], rest[:value_cols, 2 * hidden_cols :]], axis=1)
+    last_weight = jnp.concatenate([ends[1][0], rest[value_cols:, 2 * hidden_cols :]], axis=1)
+    first_weight = jnp.concatenate([first_mine, first_theirs], axis=0)
+    second_weight = jnp.concatenate([second_mine, second_theirs], axis=0)
 
     wide_one, square_one = plane_gather_total(
         (hidden * first_gain).astype(BF16), jnp.sum(hidden * hidden, axis=1)
     )
     scale_one = lax.rsqrt(square_one / features + epsilon)[:, None]
-    sums_one = matmul(wide_one, first_weight) * scale_one
+    split = first_mine.shape[0]
+    sums_one = (
+        matmul(wide_one[:, :split], first_mine) + matmul(wide_one[:, split:], first_theirs)
+    ) * scale_one
     query_sum = sums_one[:, :KD]
     key_sum = sums_one[:, KD : 2 * KD]
     value_sum = sums_one[:, 2 * KD : 2 * KD + value_cols]
@@ -500,7 +943,6 @@
     )
     scale_two = lax.rsqrt(square_two / features + epsilon)[:, None]
     sums_two = matmul(wide_two, second_weight) * scale_two
-    hidden_cols = sums_two.shape[1] // 2
     gelu_sum, up_sum = sums_two[:, :hidden_cols], sums_two[:, hidden_cols:]
     product_full, gelu_pull = jax.vjp(gelu_gate, gelu_sum, up_sum)
     product = product_full.astype(jnp.bfloat16)
@@ -508,24 +950,20 @@
 
     upstream = block_cotangent[0].astype(jnp.float32)
     wide_feed_grad = plane_gather(block_cotangent[0])
-    grad_down = weight_grad(product, wide_feed_grad)
     product_grad = back_product(wide_feed_grad, last_weight)
     gelu_grad, up_grad = gelu_pull(product_grad)
     both_grad = jnp.concatenate([gelu_grad, up_grad], axis=1)
     inner_two = jnp.sum(both_grad * sums_two, axis=1)
     both_low = (both_grad * scale_two).astype(BF16)
-    grad_both = weight_grad(wide_two, both_low)
     normed_two_grad, inner_two = plane_scatter_total(
         back_product(both_low, second_weight).astype(BF16), inner_two
     )
-    grad_second = jnp.sum(normed_two_grad * middle, axis=0)
     middle_grad = (
         upstream
         + second_gain * normed_two_grad
         - middle * (scale_two**2 * inner_two[:, None] / features)
     )
     wide_attended_grad = plane_gather(middle_grad.astype(BF16))
-    grad_output = weight_grad(gated, wide_attended_grad)
     gated_grad = back_product(wide_attended_grad, out_weight)
     swish_grad, grouped_grad = swish_pull(gated_grad)
     (retained_grad,) = group_pull(grouped_grad)
@@ -538,29 +976,76 @@
     all_grad = jnp.concatenate([query_back, key_back, value_grad, swish_grad], axis=1)
     inner_one = jnp.sum(all_grad * sums_one, axis=1)
     all_low = (all_grad * scale_one).astype(BF16)
-    grad_all = weight_grad(wide_one, all_low)
-    normed_one_grad, inner_one = plane_scatter_total(
-        back_product(all_low, first_weight).astype(BF16), inner_one
-    )
-    grad_first = jnp.sum(normed_one_grad * hidden, axis=0)
+    own_second = jnp.sum(normed_two_grad * middle, axis=0)
+    if lax.axis_size("dp") == 4:
+        (grad_down,) = sum_packs(((weight_grad(product, wide_feed_grad), 0),))
+        result, normed_one_grad, inner_one, grad_first, grad_second = last_scatter(
+            wide_one,
+            wide_two,
+            wide_attended_grad,
+            gated,
+            both_low,
+            first_weight,
+            all_low,
+            block_in[0],
+            inner_one,
+            own_second,
+        )
+        grad_up, grad_gelu, grad_output = [result[i].astype(F32) for i in range(3)]
+        starts = (0, 2 * KD)
+        grad_query, grad_key = [
+            jnp.concatenate(
+                [result[3, :, side + shift : side + shift + KD] for side in starts], axis=1
+            ).astype(F32)
+            for shift in (0, KD)
+        ]
+        grad_value, grad_swish = result[4].astype(F32), result[5].astype(F32)
+    else:
+        normed_one_grad, inner_one = plane_scatter_total(
+            back_product(all_low, first_weight).astype(BF16), inner_one
+        )
+        grad_first, grad_second = lax.psum(
+            (jnp.sum(normed_one_grad * hidden, axis=0), own_second), "dp"
+        )
+        grad_all = weight_grad(wide_one, all_low)
+        (
+            grad_query,
+            grad_key,
+            grad_value,
+            grad_swish,
+            grad_output,
+            grad_gelu,
+            grad_up,
+            grad_down,
+        ) = sum_packs(
+            (
+                (grad_all[:, :KD], 1),
+                (grad_all[:, KD : 2 * KD], 1),
+                (grad_all[:, 2 * KD : 2 * KD + value_cols], 1),
+                (grad_all[:, 2 * KD + value_cols :], 1),
+                (weight_grad(gated, wide_attended_grad), 0),
+                (weight_grad(wide_two, both_low[:, :hidden_cols]), 1),
+                (weight_grad(wide_two, both_low[:, hidden_cols:]), 1),
+                (weight_grad(product, wide_feed_grad), 0),
+            )
+        )
     grad_input = (
         middle_grad
         + first_gain * normed_one_grad
         - hidden * (scale_one**2 * inner_one[:, None] / features)
     ).astype(BF16)
 
-    grad_first, grad_second = lax.psum((grad_first, grad_second), "dp")
     return (
         block_out[None],
         grad_input[None],
-        sum_packs(grad_all[:, :KD], 1, r),
-        sum_packs(grad_all[:, KD : 2 * KD], 1, r),
-        sum_packs(grad_all[:, 2 * KD : 2 * KD + value_cols], 1, r),
-        sum_packs(grad_all[:, 2 * KD + value_cols :], 1, r),
-        sum_packs(grad_output, 0, r),
-        sum_packs(grad_both[:, :hidden_cols], 1, r),
-        sum_packs(grad_both[:, hidden_cols:], 1, r),
-        sum_packs(grad_down, 0, r),
+        grad_query,
+        grad_key,
+        grad_value,
+        grad_swish,
+        grad_output,
+        grad_gelu,
+        grad_up,
+        grad_down,
         grad_first,
         grad_second,
     )

time: 1040 us -> 745 us (0.72)
  waiting for transfers between devices: 546 us -> 41.1 us
  Pallas kernels: 270 us -> 520 us
  matrix products: 99.7 us -> 57.9 us
  other arithmetic: 41.2 us -> 57.9 us
  blocking collectives: 13.2 us -> 0 us
  starting transfers between devices: 18 us -> 7.04 us
    psum x1, waiting for transfers between devices: 412 us -> 0.01 us  [sum_packs(): totals = lax.psum(tuple((grad for grad, axis in grads)), 'dp')]
    pallas_call x0 -> x1, Pallas kernels: none -> 349 us  [last_scatter(): pl.pallas_call(last_kernel, out_shape=(jax.ShapeDtypeStruct((UNITS, 1024,...]
    ppermute x16 -> x4, waiting for transfers between devices: 134 us -> 41.1 us  [swap_rows(): return lax.ppermute(values, 'row', [(0, 1), (1, 0)])]
    pallas_call x2, Pallas kernels: 114 us -> 59.9 us  [plane_gather(): pl.pallas_call(gather_kernel, out_shape=jax.ShapeDtypeStruct((rows, width...]
    concatenate x0 -> x3, other arithmetic: none -> 26 us  [the longest x1 23.6 us: shards(): first_weight = jnp.concatenate([first_mine, first_theirs], axis=0)]
    pallas_call x2, Pallas kernels: 67.2 us -> 44.1 us  [plane_scatter(): pl.pallas_call(scatter_kernel, out_shape=jax.ShapeDtypeStruct((rows, widt...]
    pallas_call x2 -> x1, Pallas kernels: 44.4 us -> 22.2 us  [plane_scatter_total(): pl.pallas_call(scatter_total_kernel, out_shape=(jax.ShapeDtypeStruct((row...]
    dot_general x4 -> x1, matrix products: 21.5 us -> 3.71 us  [weight_grad(): jnp.einsum('tk,tf->kf', inputs, grads, preferred_element_type=jnp.float32)]
  transfers between devices with their start and end apart: 17 -> 7, of which waited for: 6 -> 3; matrix products, arithmetic and copies ran while one was open for 9% -> 11% of each run, Pallas kernels for 22% -> 59%
where the time goes in v2:
time: 745 us; the launch traced here: 740 us
  Pallas kernels  520 us (70%)
  other arithmetic  57.9 us (8%)
  matrix products  57.9 us (8%)
  waiting for transfers between devices  41.1 us (6%)
  local copies, waits for them, and re-layouts  40.8 us (5%)
  between operations  15.3 us (2%)
    pallas_call x1, Pallas kernels, last_scatter(): pl.pallas_call(last_kernel, out_shape=(jax.ShapeDtypeStruct((UNITS, 1024,...  349 us
    pallas_call x2, Pallas kernels, plane_gather(): pl.pallas_call(gather_kernel, out_shape=jax.ShapeDtypeStruct((rows, width...  59.9 us
    pallas_call x2, Pallas kernels, plane_scatter(): pl.pallas_call(scatter_kernel, out_shape=jax.ShapeDtypeStruct((rows, widt...  44.1 us
    pallas_call x2, Pallas kernels, plane_gather_total(): pl.pallas_call(gather_total_kernel, out_shape=(jax.ShapeDtypeStruct((rows...  43.9 us
    ppermute x4, waiting for transfers between devices, swap_rows(): return lax.ppermute(values, 'row', [(0, 1), (1, 0)])  41.1 us
    dot_general x9, matrix products, matmul(): return jnp.dot(left, right, preferred_element_type=jnp.float32)  27.8 us
    concatenate x1, other arithmetic, shards(): first_weight = jnp.concatenate([first_mine, first_theirs], axis=0)  23.6 us
    pallas_call x1, Pallas kernels, plane_scatter_total(): pl.pallas_call(scatter_total_kernel, out_shape=(jax.ShapeDtypeStruct((row...  22.2 us
  transfers between devices with their start and end apart: 7, of which 3 were waited for; matrix products, arithmetic and copies ran while one was open for 11% of the time, Pallas kernels for 59%

profile of v2, /device:TPU:0, one launch (start us, length us, event | category | flops | bytes accessed | tf_op | source)
XLA Modules:
  0.0 739.6 jit_solution(3199182786709796405)
XLA Ops:
  7.3 2.8 constant_dynamic-slice_fusion.9
  10.1 0.9 constant_dynamic-slice_fusion.10
  11.1 3.1 collective-permute-start
  14.1 12.0 %collective-permute-done = bf16[256,1024]{1,0:T(8,128)(2,1)} collective-permute-done((bf16[256,1024]{1,0:T(8,128)(2,1)S(1)}, bf16[256,1024]{1,0:T(8,128)(2,1)}, u32[]{:S(2)}, u32[]{:S(2)}) %collective-permute-start) | collective-permute-done | bytes 524320 | tf_op jit(solution)/shard_map/ppermute | solution.py:337
  26.3 3.7 constant_dynamic-slice_fusion
  30.0 1.9 constant_dynamic-slice_fusion.1
  31.9 2.3 fusion.37
  34.3 1.8 collective-permute-start.2
  36.1 1.6 constant_dynamic-slice_fusion.8
  38.0 1.9 fusion.61
  40.2 20.3 %collective-permute-done.2 = bf16[256,2048]{1,0:T(8,128)(2,1)} collective-permute-done((bf16[256,2048]{1,0:T(8,128)(2,1)S(1)}, bf16[256,2048]{1,0:T(8,128)(2,1)}, u32[]{:S(2)}, u32[]{:S(2)}) %collective-permute-start.2) | collective-permute-done | bytes 1048608 | tf_op jit(solution)/shard_map/ppermute | solution.py:337
  60.9 38.9 %shard_map.234 = bf16[1024,2048]{1,0:T(8,128)(2,1)S(1)} custom-call(bf16[1024,256]{1,0:T(8,128)(2,1)S(1)} %bitcast.100), custom_call_target="tpu_custom_call" | custom-call | tf_op jit(solution)/shard_map/pallas_call | solution.py:180
  99.8 2.0 copy-done.3
  101.8 22.7 %shard_map.230 = (bf16[1024,2048]{1,0:T(8,128)(2,1)S(1)}, f32[8,128]{1,0:T(8,128)S(1)}) custom-call(bf16[1024,256]{1,0:T(8,128)(2,1)S(1)} %get-tuple-element.153.own_ref, f32[8,128]{1,0:T(8,128)S(1)} %bitcast.101), custom_call_target="tpu_custom_call" | custom-call | tf_op jit(solution)/shard_map/pallas_call | solution.py:197
  124.5 2.0 copy-done.7
  126.5 5.7 fusion
  132.2 1.9 constant_dynamic-update-slice_fusion.1
  134.2 1.3 constant_dynamic-update-slice_fusion
  135.5 5.5 fusion.94
  143.6 1.0 multiply_convert_fusion.5
  144.6 0.7 fusion.52
  145.6 0.7 copy-done.17
  146.3 0.7 multiply_convert_fusion.4.gated
  148.2 23.6 %pad_maximum_fusion.weight = bf16[2048,1536]{1,0:T(8,128)(2,1)} fusion(bf16[1024,1536]{1,0:T(8,128)(2,1)S(1)} %constant_dynamic-update-slice_fusion, bf16[1024,512]{1,0:T(8,128)(2,1)S(1)} %copy-done.28, bf16[1024,512]{1,0:T(8,128)(2,1)S(1)} %copy-done.26, bf16[1024,256]{1,0:T(8,128)(2,1)S(1)} %copy-done.41, bf16[1024,256]{1,0:T(8,128)(2,1)S(1)} %copy-done.43), kind=kLoop, calls=%fused_computation | loop fusion | flops 31457280 | bytes 12582912 | tf_op jit(solution)/shard_map/concatenate | solution.py:913
  171.7 2.8 fusion.90
  174.6 2.4 convolution_convert_fusion.1.part_ref
  177.0 22.1 %shard_map.231 = f32[1024,256]{1,0:T(8,128)S(1)} custom-call(bf16[1024,2048]{1,0:T(8,128)(2,1)S(1)} %convolution_convert_fusion.1.part_ref), custom_call_target="tpu_custom_call" | custom-call | tf_op jit(solution)/shard_map/pallas_call | solution.py:305
  199.3 21.2 %shard_map.232 = (bf16[1024,2048]{1,0:T(8,128)(2,1)S(1)}, f32[8,128]{1,0:T(8,128)S(1)}) custom-call(bf16[1024,256]{1,0:T(8,128)(2,1)S(1)} %get-tuple-element.141.own_ref, f32[8,128]{1,0:T(8,128)S(1)} %bitcast.103), custom_call_target="tpu_custom_call" | custom-call | tf_op jit(solution)/shard_map/pallas_call | solution.py:197
  220.9 1.8 copy-done.9
  222.7 1.0 copy-done.60
  223.7 4.5 convolution_multiply_fusion
  228.2 5.3 fusion.13
  233.5 1.1 copy-done.77
  234.6 3.7 convolution_convert_fusion.3
  238.3 6.4 convolution_convert_fusion.part_ref
  245.4 0.9 copy-done.46
  246.3 0.9 copy-done.59
  247.6 11.2 %convolution_convert_fusion.2.part_ref = bf16[1024,2048]{1,0:T(8,128)(2,1)S(1)} fusion(bf16[1024,1024]{1,0:T(8,128)(2,1)S(1)} %get-tuple-element.118.both_low, bf16[1024,1024]{1,0:T(8,128)(2,1)S(1)} %copy-done.46, bf16[1024,512]{1,0:T(8,128)(2,1)S(1)} %copy-done.59, bf16[1024,512]{1,0:T(8,128)(2,1)S(1)} %copy-done.61), kind=kOutput, calls=%fused_computation.15 | convolution fusion | flops 4309647360 | bytes 10485760 | tf_op jit(solution)/shard_map/tf,kf->tk/dot_general | solution.py:805
  258.8 22.2 %shard_map.235 = (f32[1024,256]{1,0:T(8,128)S(1)}, f32[8,128]{1,0:T(8,128)S(1)}) custom-call(bf16[1024,2048]{1,0:T(8,128)(2,1)S(1)} %convolution_convert_fusion.2.part_ref, f32[8,128]{1,0:T(8,128)S(1)} %bitcast.102), custom_call_target="tpu_custom_call" | custom-call | tf_op jit(solution)/shard_map/pallas_call | solution.py:320
  281.1 1.0 multiply_reduce_fusion.4
  282.1 21.1 %shard_map.236.wide_att = bf16[1024,2048]{1,0:T(8,128)(2,1)S(1)} custom-call(bf16[1024,256]{1,0:T(8,128)(2,1)S(1)} %get-tuple-element.123.own_ref), custom_call_target="tpu_custom_call" | custom-call | tf_op jit(solution)/shard_map/pallas_call | solution.py:180
  303.2 2.9 multiply_reduce_fusion.2
  306.1 3.0 fusion.14
  310.1 2.2 multiply_convert_fusion.2
  312.6 1.1 fusion.76
  313.8 1.9 fusion.95
  316.5 0.9 copy-done.22
  317.8 0.9 copy-done.34
  319.3 1.2 copy-done.2
  320.5 22.0 %shard_map.233 = f32[1024,256]{1,0:T(8,128)S(1)} custom-call(bf16[1024,2048]{1,0:T(8,128)(2,1)S(1)} %copy-done.2), custom_call_target="tpu_custom_call" | custom-call | tf_op jit(solution)/shard_map/pallas_call | solution.py:305
  342.6 0.7 pad_add_fusion
  343.5 1.0 copy-done.19
  344.6 3.1 multiply_reduce_fusion
  347.7 349.4 %last_scatter.1 = (bf16[6,1024,1024]{2,1,0:T(8,128)(2,1)}, f32[1024,256]{1,0:T(8,128)}, f32[8,128]{1,0:T(8,128)}, f32[8,256]{1,0:T(8,128)}) custom-call(bf16[1024,2048]{1,0:T(8,128)(2,1)} %copy-done.7, bf16[1024,2048]{1,0:T(8,128)(2,1)} %copy-done.9, bf16[1024,2048]{1,0:T(8,128)(2,1)} %copy-done, bf16[1024,512]{1,0:T(8,128)(2,1)} %copy-done.32, ...), custom_call_target="tpu_custom_call" | custom-call | tf_op jit(solution)/shard_map/last_scatter/pallas_call | solution.py:748
  697.1 1.8 slice_bitcast_fusion.1
  699.0 1.6 maximum_convert_fusion.1
  701.4 1.5 fusion.55
  702.9 1.7 fusion.91
  704.6 1.6 collective-permute-start.3
  706.2 1.6 maximum_convert_fusion
  707.8 1.3 fusion.92
  709.1 9.9 %bitcast_convert_fusion = (f32[1024,1024]{1,0:T(8,128)}, f32[1024,1024]{1,0:T(8,128)}, f32[1024,1024]{1,0:T(8,128)}, f32[1024,1024]{1,0:T(8,128)}, f32[1024,1024]{1,0:T(8,128)}) fusion(bf16[6,1024,1024]{2,1,0:T(8,128)(2,1)} %get-tuple-element.94), kind=kLoop, calls=%fused_computation.51 | loop fusion | flops 5242880 | bytes 31457280 | tf_op jit(solution)/shard_map/convert_element_type | solution.py:994
  719.0 8.7 %collective-permute-done.3 = bf16[512,1024]{1,0:T(8,128)(2,1)S(1)} collective-permute-done((bf16[512,1024]{1,0:T(8,128)(2,1)S(1)}, bf16[512,1024]{1,0:T(8,128)(2,1)S(1)}, u32[]{:S(2)}, u32[]{:S(2)}) %collective-permute-start.3) | collective-permute-done | bytes 1048608 | tf_op jit(solution)/shard_map/ppermute | solution.py:337
  727.7 5.0 fusion.19
  (191 shorter events, 10.7 us)
Async XLA Ops:
  7.2 125.0 %all-gather.3.cloned.1.call-start = ((), (), s32[]{:S(2)}) async-start(), calls=%async_computation | async-start | bytes 2621440 | tf_op jit(solution)/shard_map/all_gather | solution.py:350
  7.2 2.8 copy-start.54
  7.2 2.8 copy-start.55
  11.0 113.5 %copy-start.40 = (bf16[1024,256]{1,0:T(8,128)(2,1)}, bf16[1024,256]{1,0:T(8,128)(2,1)S(1)}, u32[]{:S(2)}) copy-start(bf16[1024,256]{1,0:T(8,128)(2,1)S(1)} %get-tuple-element.149) | copy-start | bytes 1572868
  11.0 15.2 %copy-start.37 = (bf16[1024,1024]{1,0:T(8,128)(2,1)S(1)}, bf16[1024,1024]{1,0:T(8,128)(2,1)}, u32[]{:S(2)}) copy-start(bf16[1024,1024]{1,0:T(8,128)(2,1)} %param.35) | copy-start | bytes 6291460
  11.1 15.1 %collective-permute-start = (bf16[256,1024]{1,0:T(8,128)(2,1)S(1)}, bf16[256,1024]{1,0:T(8,128)(2,1)}, u32[]{:S(2)}, u32[]{:S(2)}) collective-permute-start(bf16[256,1024]{1,0:T(8,128)(2,1)S(1)} %fusion.60), channel_id=1, source_target_pairs={{0,4},{4,0},{1,5},{5,1},{2,6},{6,2},{3,7},{7,3},{8,12},{12,8},{9,1... | collective-permute-start | bytes 1572872 | tf_op jit(solution)/shard_map/ppermute | solution.py:337
  26.2 145.6 %all-gather.5.cloned.1.call-start = ((), (), s32[]{:S(2)}) async-start(), calls=%async_computation.1 | async-start | bytes 5242880 | tf_op jit(solution)/shard_map/all_gather | solution.py:350
  26.2 3.8 copy-start.38
  26.2 3.7 copy-start.39
  31.9 4.2 copy-start.44
  34.2 3.7 copy-start.76
  34.3 5.6 copy-start.13
  34.3 5.6 copy-start.74
  34.3 26.2 %collective-permute-start.2 = (bf16[256,2048]{1,0:T(8,128)(2,1)S(1)}, bf16[256,2048]{1,0:T(8,128)(2,1)}, u32[]{:S(2)}, u32[]{:S(2)}) collective-permute-start(bf16[256,2048]{1,0:T(8,128)(2,1)S(1)} %fusion.37), channel_id=1, source_target_pairs={{0,4},{4,0},{1,5},{5,1},{2,6},{6,2},{3,7},{7,3},{8,12},{12,8},{9,1... | collective-permute-start | bytes 3145736 | tf_op jit(solution)/shard_map/ppermute | solution.py:337
  37.6 23.2 %copy-start.1 = (bf16[1,1024,256]{2,1,0:T(8,128)(2,1)S(1)}, bf16[1,1024,256]{2,1,0:T(8,128)(2,1)}, u32[]{:S(2)}) copy-start(bf16[1,1024,256]{2,1,0:T(8,128)(2,1)} %param.27) | copy-start | bytes 1572868
  37.6 96.5 %collective-permute-start.1 = (bf16[1024,512]{1,0:T(8,128)(2,1)}, bf16[1024,512]{1,0:T(8,128)(2,1)}, u32[]{:S(2)}, u32[]{:S(2)}) collective-permute-start(bf16[1024,512]{1,0:T(8,128)(2,1)} %get-tuple-element.134), channel_id=1, source_target_pairs={{0,4},{4,0},{1,5},{5,1},{2,6},{6,2},{3,7},{7,3},{8,12},{12,8},{9,1... | collective-permute-start | bytes 3145736 | tf_op jit(solution)/shard_map/ppermute | solution.py:337
  39.9 101.3 %copy-start.21 = (f32[1024,128]{1,0:T(8,128)}, f32[1024,128]{1,0:T(8,128)S(1)}, u32[]{:S(2)}) copy-start(f32[1024,128]{1,0:T(8,128)S(1)} %get-tuple-element.160) | copy-start | bytes 1572868
  39.9 101.3 %copy-start.23 = (f32[1024,128]{1,0:T(8,128)}, f32[1024,128]{1,0:T(8,128)S(1)}, u32[]{:S(2)}) copy-start(f32[1024,128]{1,0:T(8,128)S(1)} %get-tuple-element.161) | copy-start | bytes 1572868
  60.5 642.4 %all-reduce.4.cloned.1.call-start = ((), (), s32[]{:S(2)}) async-start(), calls=%async_computation.2 | async-start | bytes 4194304 | tf_op jit(solution)/shard_map/psum | solution.py:786
  60.9 65.6 %copy-start.25 = (bf16[1024,512]{1,0:T(8,128)(2,1)S(1)}, bf16[1024,512]{1,0:T(8,128)(2,1)}, u32[]{:S(2)}) copy-start(bf16[1024,512]{1,0:T(8,128)(2,1)} %get-tuple-element.137) | copy-start | bytes 3145732
  60.9 65.6 %copy-start.27 = (bf16[1024,512]{1,0:T(8,128)(2,1)S(1)}, bf16[1024,512]{1,0:T(8,128)(2,1)}, u32[]{:S(2)}) copy-start(bf16[1024,512]{1,0:T(8,128)(2,1)} %get-tuple-element.135) | copy-start | bytes 3145732
  60.9 65.6 %copy-start.42 = (bf16[1024,256]{1,0:T(8,128)(2,1)S(1)}, bf16[1024,256]{1,0:T(8,128)(2,1)}, u32[]{:S(2)}) copy-start(bf16[1024,256]{1,0:T(8,128)(2,1)} %get-tuple-element.170) | copy-start | bytes 1572868
  99.8 2.0 copy-start.3
  132.2 3.2 copy-start.8
  141.0 3.6 copy-start.71
  141.0 4.6 copy-start.12
  148.2 26.4 %copy-start.32 = (bf16[1024,512]{1,0:T(8,128)(2,1)}, bf16[1024,512]{1,0:T(8,128)(2,1)S(1)}, u32[]{:S(2)}) copy-start(bf16[1024,512]{1,0:T(8,128)(2,1)S(1)} %multiply_convert_fusion.4.gated) | copy-start | bytes 3145732
  171.7 2.8 copy-start.56
  174.5 2.4 copy-start.66
  176.9 22.1 %copy-start.14 = (bf16[1,1024,256]{2,1,0:T(8,128)(2,1)S(1)}, bf16[1,1024,256]{2,1,0:T(8,128)(2,1)}, u32[]{:S(2)}) copy-start(bf16[1,1024,256]{2,1,0:T(8,128)(2,1)} %param.25) | copy-start | bytes 1572868
  176.9 22.1 %copy-start.73 = (f32[256]{0:T(256)S(1)}, f32[256]{0:T(256)}, u32[]{:S(2)}) copy-start(f32[256]{0:T(256)} %param.37) | copy-start | bytes 3076
  177.0 43.6 %copy-start.29 = (bf16[1024,2048]{1,0:T(8,128)(2,1)S(1)}, bf16[1024,2048]{1,0:T(8,128)(2,1)}, u32[]{:S(2)}) copy-start(bf16[1024,2048]{1,0:T(8,128)(2,1)} %all-gather.5.cloned.1.call-done) | copy-start | bytes 12582916
  220.6 2.1 copy-start.9
  220.6 2.1 copy-start.58
  220.6 3.1 copy-start.60
  220.9 7.3 copy-start.45
  223.7 4.5 copy-start.4
  223.7 4.5 copy-start.62
  223.7 4.5 copy-start.68
  228.2 5.3 copy-start.30
  238.3 6.4 copy-start.31
  238.3 6.4 copy-start.47
  238.3 6.4 copy-start.48
  244.7 2.5 copy-start.59
  244.7 2.9 copy-start.61
  245.3 13.5 %copy-start.20 = (bf16[1024,1024]{1,0:T(8,128)(2,1)}, bf16[1024,1024]{1,0:T(8,128)(2,1)S(1)}, u32[]{:S(2)}) copy-start(bf16[1024,1024]{1,0:T(8,128)(2,1)S(1)} %get-tuple-element.118.both_low) | copy-start | bytes 6291460
  247.6 33.4 %copy-start.15 = (bf16[1,1024,256]{2,1,0:T(8,128)(2,1)S(1)}, bf16[1,1024,256]{2,1,0:T(8,128)(2,1)}, u32[]{:S(2)}) copy-start(bf16[1,1024,256]{2,1,0:T(8,128)(2,1)} %param.25) | copy-start | bytes 1572868
  258.8 44.4 %slice-start = ((s8[6291456]{0:T(1024)(128)(4,1)}), s8[4194304]{0:T(1024)(128)(4,1)S(1)}, s32[]{:S(2)}) async-start(s8[6291456]{0:T(1024)(128)(4,1)} %bitcast.104), calls=%async_computation.3 | async-start | bytes 8388608
  281.1 22.1 %slice-start.1 = ((s8[6291456]{0:T(1024)(128)(4,1)}), s8[2097152]{0:T(1024)(128)(4,1)S(1)}, s32[]{:S(2)}) async-start(s8[6291456]{0:T(1024)(128)(4,1)} %bitcast.104), calls=%async_computation.4 | async-start | bytes 4194304
  282.1 21.1 %copy-start.18 = (f32[512,512]{1,0:T(8,128)S(1)}, f32[512,512]{1,0:T(8,128)}, u32[]{:S(2)}) copy-start(f32[512,512]{1,0:T(8,128)} %copy-done.17) | copy-start | bytes 3145732
  282.1 21.1 %copy-start.57 = (bf16[512,1024]{1,0:T(8,128)(2,1)S(1)}, bf16[512,1024]{1,0:T(8,128)(2,1)}, u32[]{:S(2)}) copy-start(bf16[512,1024]{1,0:T(8,128)(2,1)} %get-tuple-element.167) | copy-start | bytes 3145732
  282.1 21.1 %copy-start.67 = (bf16[512,1024]{1,0:T(8,128)(2,1)S(1)}, bf16[512,1024]{1,0:T(8,128)(2,1)}, u32[]{:S(2)}) copy-start(bf16[512,1024]{1,0:T(8,128)(2,1)} %copy-done.66) | copy-start | bytes 3145732
  303.2 2.9 copy-start
  306.1 3.0 copy-start.72
  310.1 2.2 copy-start.36
  310.1 2.5 copy-start.52
  317.5 3.0 copy-start.2
  318.8 24.7 %slice-start.2 = ((s8[6291456]{0:T(1024)(128)(4,1)}), s8[4194304]{0:T(1024)(128)(4,1)S(1)}, s32[]{:S(2)}) async-start(s8[6291456]{0:T(1024)(128)(4,1)} %bitcast.106), calls=%async_computation.5 | async-start | bytes 8388608
  320.5 22.0 %copy-start.65 = (bf16[512,1024]{1,0:T(8,128)(2,1)S(1)}, bf16[512,1024]{1,0:T(8,128)(2,1)}, u32[]{:S(2)}) copy-start(bf16[512,1024]{1,0:T(8,128)(2,1)} %copy-done.64) | copy-start | bytes 3145732
  320.5 23.0 %slice-start.3 = ((s8[6291456]{0:T(1024)(128)(4,1)}), s8[2097152]{0:T(1024)(128)(4,1)S(1)}, s32[]{:S(2)}) async-start(s8[6291456]{0:T(1024)(128)(4,1)} %bitcast.106), calls=%async_computation.6 | async-start | bytes 4194304
  697.1 3.4 copy-start.69
  698.9 2.3 copy-start.11
  698.9 2.4 copy-start.16
  704.6 23.1 %collective-permute-start.3 = (bf16[512,1024]{1,0:T(8,128)(2,1)S(1)}, bf16[512,1024]{1,0:T(8,128)(2,1)S(1)}, u32[]{:S(2)}, u32[]{:S(2)}) collective-permute-start(bf16[512,1024]{1,0:T(8,128)(2,1)S(1)} %get-tuple-element.124), channel_id=1, source_target_pairs={{0,4},{4,0},{1,5},{5,1},{2,6},{6,2},{3,7},{7,3},{8,12},{12,8},{9,1... | collective-permute-start | bytes 3145736 | tf_op jit(solution)/shard_map/ppermute | solution.py:337
  (25 other events, 36.0 us)
Sparse Core Ops, SparseCore 0:
  26.3 47.1 all-gather.2
  75.1 79.4 all-gather.4
  313.9 117.8 all-reduce.3

commit v3 on v2

--- a/solution.py
+++ b/solution.py
@@ -52,21 +52,31 @@
     return r, c, core, across
 
 
-def enter():
+def plane_peers():
     r, c, core, across = neighbours()
+    return [{"col": core}, {"col": across}, {"row": 1 - r}]
+
+
+def line_peers():
+    z = lax.axis_index("dp")
+    return [{"dp": lax.rem(z + k, 4)} for k in (1, 2, 3)]
+
+
+def enter(peers):
     barrier = pltpu.get_barrier_semaphore()
-    for target in ({"col": core}, {"col": across}, {"row": 1 - r}):
+    for target in peers:
         pl.semaphore_signal(barrier, inc=1, device_id=target, device_id_type=MESH)
-    pl.semaphore_wait(barrier, 3)
+    pl.semaphore_wait(barrier, len(peers))
 
 
 class Sender:
     def __init__(self, send_sem, recv_sem):
-        self.send_sem, self.recv_sem, self.started = send_sem, recv_sem, []
-
-    def __call__(self, src, dst, target):
-        slot = len(self.started)
-        copy = pltpu.make_async_remote_copy(
+        self.send_sem, self.recv_sem, self.started, self.slots = send_sem, recv_sem, [], 0
+
+    def make(self, src, dst, target):
+        slot = self.slots
+        self.slots += 1
+        return pltpu.make_async_remote_copy(
             src_ref=src,
             dst_ref=dst,
             send_sem=self.send_sem.at[slot],
@@ -74,104 +84,565 @@
             device_id=target,
             device_id_type=MESH,
         )
+
+    def __call__(self, src, dst, target):
+        copy = self.make(src, dst, target)
         copy.start()
         self.started.append(copy)
         return copy
 
-
-def gather_body(own_ref, out_ref, send, local_sem, side):
+    def finish(self):
+        for copy in self.started:
+            copy.wait_send()
+        self.started = []
+
+
+def run(*generators):
+    waiting = list(generators)
+    while waiting:
+        waiting = [each for each in waiting if next(each, "end") != "end"]
+
+
+def gather_steps(own_ref, out_ref, send, local_sem):
     rows, width = own_ref.shape
     half = rows // 2
     r, c, core, across = neighbours()
-    to_core, to_x, to_y = {"col": core}, {"col": across}, {"row": 1 - r}
-
-    def view(ref, place, part):
+    to_core, to_x, to_y = plane_peers()
+
+    def view(place, part):
         cols = pl.ds(pl.multiple_of(place * width, width), width)
         if part is None:
-            return ref.at[:, cols]
-        return ref.at[part * half : (part + 1) * half, cols]
+            return out_ref.at[:, cols]
+        return out_ref.at[part * half : (part + 1) * half, cols]
 
     def own(part):
         return own_ref.at[part * half : (part + 1) * half]
 
-    side_start = side(send, to_core, to_x, to_y)
-    x0 = send(own(0), view(out_ref, c, 0), to_x)
-    y1 = send(own(1), view(out_ref, 4 + c, 1), to_y)
-    x1 = send(own(1), view(out_ref, c, 1), to_x)
-    y0 = send(own(0), view(out_ref, 4 + c, 0), to_y)
-    late = [send(own_ref, view(out_ref, c, None), to_core)]
-    keep = pltpu.make_async_copy(own_ref, view(out_ref, c, None), local_sem)
+    def forward(place, part, target, there):
+        return send(view(place, part), view(there, part), target)
+
+    y1 = send(own(1), view(4 + c, 1), to_y)
+    x0 = send(own(0), view(c, 0), to_x)
+    y0 = send(own(0), view(4 + c, 0), to_y)
+    x1 = send(own(1), view(c, 1), to_x)
+    late = [send(own_ref, view(c, None), to_core)]
+    keep = pltpu.make_async_copy(own_ref, view(c, None), local_sem)
     keep.start()
-    next(side_start)
+    yield
     x0.wait_recv()
-    fy = send(view(out_ref, across, 0), view(out_ref, 4 + across, 0), to_y)
-    late.append(send(view(out_ref, across, 0), view(out_ref, across, 0), to_core))
+    late.append(forward(across, 0, to_core, across))
+    diag0 = forward(across, 0, to_y, 4 + across)
+    yield
     y1.wait_recv()
-    fx = send(view(out_ref, 4 + c, 1), view(out_ref, 4 + c, 1), to_x)
-    late.append(send(view(out_ref, 4 + c, 1), view(out_ref, 4 + c, 1), to_core))
-    next(side_start)
+    diag1 = forward(4 + c, 1, to_x, 4 + c)
+    late.append(forward(4 + c, 1, to_core, 4 + c))
+    yield
     x1.wait_recv()
-    late.append(send(view(out_ref, across, 1), view(out_ref, across, 1), to_core))
+    late.append(forward(across, 1, to_core, across))
     y0.wait_recv()
-    late.append(send(view(out_ref, 4 + c, 0), view(out_ref, 4 + c, 0), to_core))
-    next(side_start)
-    fy.wait_recv()
-    late.append(send(view(out_ref, 4 + across, 0), view(out_ref, 4 + across, 0), to_core))
-    fx.wait_recv()
-    late.append(send(view(out_ref, 4 + across, 1), view(out_ref, 4 + across, 1), to_core))
+    late.append(forward(4 + c, 0, to_core, 4 + c))
+    yield
+    diag0.wait_recv()
+    late.append(forward(4 + across, 0, to_core, 4 + across))
+    yield
+    diag1.wait_recv()
+    late.append(forward(4 + across, 1, to_core, 4 + across))
     keep.wait()
     for copy in late:
         copy.wait_recv()
-    for copy in send.started:
-        copy.wait_send()
-
-
-def no_side(send, to_core, to_x, to_y):
-    while True:
+
+
+GATHERS = 13
+
+
+def gather_timed(own_ref, out_ref, send, local_sem, rounds, by_x):
+    rows, width = own_ref.shape
+    half = rows // 2
+    r, c, core, across = neighbours()
+    to_core, to_x, to_y = plane_peers()
+    now = 0
+
+    def view(place, part):
+        cols = pl.ds(pl.multiple_of(place * width, width), width)
+        if part is None:
+            return out_ref.at[:, cols]
+        return out_ref.at[part * half : (part + 1) * half, cols]
+
+    def forward(place, part, target, there):
+        return send(view(place, part), view(there, part), target)
+
+    keep = pltpu.make_async_copy(own_ref, view(c, None), local_sem)
+    late, diagonal = [], []
+    first = over = None
+    stages = sorted(rounds.items(), key=lambda item: item[1])
+    for name, at in stages:
+        while now < at:
+            now += 1
+            yield
+        if name == "x":
+            keep.start()
+            first = send(own_ref, view(c, None), to_x)
+            late.append(send(own_ref, view(c, None), to_core))
+        elif name == "y":
+            over = send(own_ref, view(4 + c, None), to_y)
+        elif name == "x_here":
+            first.wait_recv()
+            late.append(forward(across, None, to_core, across))
+            if not by_x:
+                diagonal.append(forward(across, 0, to_y, 4 + across))
+        elif name == "y_here":
+            over.wait_recv()
+            late.append(forward(4 + c, None, to_core, 4 + c))
+            if by_x:
+                diagonal.append(forward(4 + c, None, to_x, 4 + c))
+            else:
+                diagonal.append(forward(4 + c, 1, to_x, 4 + c))
+        elif name == "diagonal":
+            for copy in diagonal:
+                copy.wait_recv()
+            late.append(forward(4 + across, None, to_core, 4 + across))
+    keep.wait()
+    yield
+    for copy in late:
+        copy.wait_recv()
+
+
+def total_steps(vec_ref, total_ref, got, send):
+    to_core, to_x, to_y = plane_peers()
+    first = send(vec_ref, got.at[0], to_core)
+    yield
+    first.wait_recv()
+    got[3] = vec_ref[...] + got[0]
+    second = send(got.at[3], got.at[1], to_x)
+    yield
+    second.wait_recv()
+    got[4] = got[3] + got[1]
+    third = send(got.at[4], got.at[2], to_y)
+    yield
+    third.wait_recv()
+    total_ref[...] = got[4] + got[2]
+
+
+class Weight:
+    def __init__(self, source, target, kind, shift, part, parts):
+        self.source, self.target, self.kind, self.shift = source, target, kind, shift
+        self.part, self.parts, self.shape = part, parts, source.shape
+
+    def span(self, base, length, quarter):
+        if quarter is None:
+            size = length // self.parts
+            return pl.ds(pl.multiple_of(base + self.part * size, size), size)
+        size = length // (4 * self.parts)
+        return pl.ds(pl.multiple_of(base + (quarter * self.parts + self.part) * size, size), size)
+
+    def held(self, side, quarter):
+        rows, cols = self.shape
+        if self.kind == "in":
+            width = cols // 2
+            columns = pl.ds(pl.multiple_of(side * width, width), width)
+            return self.source.at[self.span(0, rows, quarter), columns]
+        return self.source.at[self.span(side * (rows // 2), rows // 2, quarter), :]
+
+    def whole(self, other, quarter):
+        rows, cols = self.shape
+        if self.kind == "in":
+            return self.target.at[
+                self.span(other * rows, rows, quarter), self.shift : self.shift + cols // 2
+            ]
+        return self.target.at[self.span(0, rows // 2, quarter), other * cols : (other + 1) * cols]
+
+
+def weight_steps(weights, bounce, local_sem, send):
+    z, r = lax.axis_index("dp"), lax.axis_index("row")
+    count = len(weights)
+    last = 3
+
+    def keep_in(i):
+        return pltpu.make_async_copy(weights[i].held(r, None), bounce[i], local_sem.at[i])
+
+    def keep_out(i):
+        return pltpu.make_async_copy(bounce[i], weights[i].whole(0, None), local_sem.at[i])
+
+    over = []
+
+    def start_over(i):
+        if i < count:
+            part = weights[i]
+            over.append(send(part.held(1 - r, z), part.whole(1, z), {"row": 1 - r}))
+
+    start_over(0)
+    start_over(1)
+    for i in range(count):
+        keep_in(i).start()
+
+    def hop(i, h, way):
+        quarter = z - way * (h - 1)
+        region = weights[i].whole(1, quarter)
+        return region, {"dp": z + way}
+
+    slots = {}
+    for i in range(count):
+        for h in (1, 2, 3):
+            for way in (1, -1):
+                slots[i, h, way] = send.slots
+                send.slots += 1
+
+    def copy(i, h, way):
+        region, target = hop(i, h, way)
+        slot = slots[i, h, way]
+        return pltpu.make_async_remote_copy(
+            src_ref=region,
+            dst_ref=region,
+            send_sem=send.send_sem.at[slot],
+            recv_sem=send.recv_sem.at[slot],
+            device_id=target,
+            device_id_type=MESH,
+        )
+
+    def sends(h, way):
+        if way > 0:
+            return (z >= h - 1) & (z < last)
+        return (z + h - 1 <= last) & (z > 0)
+
+    def receives(h, way):
+        return z >= h if way > 0 else z + h <= last
+
+    def pass_on(i, h):
+        for way in (1, -1):
+            if h > 1:
+
+                @pl.when(receives(h - 1, way))
+                def _():
+                    copy(i, h - 1, way).wait_recv()
+
+            if h <= last:
+
+                @pl.when(sends(h, way))
+                def _():
+                    copy(i, h, way).start()
+
+    yield
+    for i in range(count + 3):
+        if i < count:
+            over[i].wait_recv()
+            start_over(i + 2)
+            keep_in(i).wait()
+            keep_out(i).start()
+        for h in (1, 2, 3, 4):
+            if 0 <= i - h + 1 < count:
+                pass_on(i - h + 1, h)
         yield
-
-
-def total_side(vec_ref, total_ref, got):
-    def steps(send, to_core, to_x, to_y):
-        first = send(vec_ref, got.at[0], to_core)
-
-        def rest():
-            first.wait_recv()
-            got[3] = vec_ref[...] + got[0]
-            second = send(got.at[3], got.at[1], to_x)
-            yield
-            second.wait_recv()
-            got[4] = got[3] + got[1]
-            third = send(got.at[4], got.at[2], to_y)
-            yield
-            third.wait_recv()
-            total_ref[...] = got[4] + got[2]
-            yield
-
-        return rest()
-
-    return steps
+    for i in range(count):
+        keep_out(i).wait()
+        for h in (1, 2, 3):
+            for way in (1, -1):
+
+                @pl.when(sends(h, way))
+                def _():
+                    copy(i, h, way).wait_send()
+
+
+def scatter_steps(prepare, rows_part, rows_core, rows_x, rows_y, send, out_ref):
+    half = rows_part.shape[1] // 2
+    to_core, to_x, to_y = plane_peers()
+    lo, hi = slice(0, half), slice(half, 2 * half)
+
+    def summed(i, rows):
+        return rows_part[4 + i, rows].astype(F32) + rows_core[i, rows].astype(F32)
+
+    first = []
+    for i in range(4):
+        prepare(i)
+        first.append(send(rows_part.at[i], rows_core.at[i], to_core))
+    yield
+    for i in range(4):
+        prepare(4 + i)
+    first[0].wait_recv()
+    rows_part[4, lo] = summed(0, lo).astype(BF16)
+    dx = send(rows_part.at[4, lo], rows_x.at[2], to_x)
+    rows_part[4, hi] = summed(0, hi).astype(BF16)
+    dy = send(rows_part.at[4, hi], rows_y.at[2], to_y)
+    first[1].wait_recv()
+    rows_part[5, lo] = summed(1, lo).astype(BF16)
+    x0 = send(rows_part.at[5, lo], rows_x.at[0], to_x)
+    first[2].wait_recv()
+    rows_part[6, hi] = summed(2, hi).astype(BF16)
+    y1 = send(rows_part.at[6, hi], rows_y.at[1], to_y)
+    yield
+    dy.wait_recv()
+    rows_part[5, hi] = (summed(1, hi) + rows_y[2].astype(F32)).astype(BF16)
+    x1 = send(rows_part.at[5, hi], rows_x.at[1], to_x)
+    dx.wait_recv()
+    rows_part[6, lo] = (summed(2, lo) + rows_x[2].astype(F32)).astype(BF16)
+    y0 = send(rows_part.at[6, lo], rows_y.at[0], to_y)
+    yield
+    first[3].wait_recv()
+    x0.wait_recv()
+    y1.wait_recv()
+    out_ref[lo] = summed(3, lo) + rows_x[0].astype(F32)
+    out_ref[hi] = summed(3, hi) + rows_y[1].astype(F32)
+    yield
+    x1.wait_recv()
+    out_ref[hi] = out_ref[hi] + rows_x[1].astype(F32)
+    y0.wait_recv()
+    out_ref[lo] = out_ref[lo] + rows_y[0].astype(F32)
+
+
+SCATTERS = 10
+
+
+def block_places():
+    r, c, core, across = neighbours()
+    ours = (4 + across, across, 4 + c, c)
+    return [place + core - c for place in ours] + list(ours)
+
+
+def scatter_rows(rows, width):
+    half = rows // 2
+    return [
+        pltpu.VMEM((8, rows, width), BF16),
+        pltpu.VMEM((4, rows, width), BF16),
+        pltpu.VMEM((3, half, width), BF16),
+        pltpu.VMEM((3, half, width), BF16),
+    ]
+
+
+def block_loads(part_ref, rows_part, sems):
+    width = rows_part.shape[2]
+    loads = []
+    for i, place in enumerate(block_places()):
+        cols = pl.ds(pl.multiple_of(place * width, width), width)
+        loads.append(pltpu.make_async_copy(part_ref.at[:, cols], rows_part.at[i], sems.at[i]))
+        loads[-1].start()
+    return lambda i: loads[i].wait()
+
+
+def dma(*counts):
+    return [pltpu.SemaphoreType.DMA((count,)) for count in counts]
 
 
 def gather_kernel(own_ref, out_ref, send_sem, recv_sem, local_sem):
-    enter()
-    gather_body(own_ref, out_ref, Sender(send_sem, recv_sem), local_sem, no_side)
+    enter(plane_peers())
+    send = Sender(send_sem, recv_sem)
+    run(gather_steps(own_ref, out_ref, send, local_sem.at[0]))
+    send.finish()
 
 
 def gather_total_kernel(own_ref, vec_ref, out_ref, total_ref, got, send_sem, recv_sem, local_sem):
-    enter()
-    gather_body(
-        own_ref, out_ref, Sender(send_sem, recv_sem), local_sem, total_side(vec_ref, total_ref, got)
-    )
+    enter(plane_peers())
+    send = Sender(send_sem, recv_sem)
+    run(
+        total_steps(vec_ref, total_ref, got, send),
+        gather_steps(own_ref, out_ref, send, local_sem.at[0]),
+    )
+    send.finish()
+
+
+def scatter_kernel(part_ref, out_ref, *rest):
+    rows, (send_sem, recv_sem, load_sem) = rest[:4], rest[4:]
+    send = Sender(send_sem, recv_sem)
+    prepare = block_loads(part_ref, rows[0], load_sem)
+    enter(plane_peers())
+    run(scatter_steps(prepare, *rows, send, out_ref))
+    send.finish()
+
+
+def scatter_total_kernel(part_ref, vec_ref, out_ref, total_ref, got, *rest):
+    rows, (send_sem, recv_sem, load_sem) = rest[:4], rest[4:]
+    send = Sender(send_sem, recv_sem)
+    prepare = block_loads(part_ref, rows[0], load_sem)
+    enter(plane_peers())
+    run(
+        total_steps(vec_ref, total_ref, got, send),
+        scatter_steps(prepare, *rows, send, out_ref),
+    )
+    send.finish()
+
+
+def start_kernel(
+    own_ref,
+    vec_ref,
+    feed_ref,
+    query,
+    key,
+    value,
+    swish,
+    output,
+    wide,
+    wide_feed,
+    total,
+    first_weight,
+    out_weight,
+    got,
+    qk_bounce,
+    vs_bounce,
+    out_bounce,
+    send_sem,
+    recv_sem,
+    local_sem,
+):
+    enter(plane_peers() + line_peers())
+    send = Sender(send_sem, recv_sem)
+    head, value_cols = query.shape[1] // 2, value.shape[1] // 2
+    rows = query.shape[0]
+    weights, bounce = [], []
+    for i, (source, shift) in enumerate(((value, 2 * head), (swish, 2 * head + value_cols))):
+        for part in range(2):
+            weights.append(Weight(source, first_weight, "in", shift, part, 2))
+            bounce.append(vs_bounce.at[i, part * rows // 2 : (part + 1) * rows // 2])
+    for i, source in enumerate((query, key)):
+        weights.append(Weight(source, first_weight, "in", i * head, 0, 1))
+        bounce.append(qk_bounce.at[i])
+    for part in range(2):
+        weights.append(Weight(output, out_weight, "out", 0, part, 2))
+        size = output.shape[0] // 4
+        bounce.append(out_bounce.at[part * size : (part + 1) * size])
+    run(
+        weight_steps(weights, bounce, local_sem, send),
+        total_steps(vec_ref, total, got, send),
+        gather_timed(
+            own_ref,
+            wide,
+            send,
+            local_sem.at[8],
+            {"x": 0, "x_here": 2, "y": 3, "y_here": 5, "diagonal": 8},
+            True,
+        ),
+        gather_timed(
+            feed_ref,
+            wide_feed,
+            send,
+            local_sem.at[9],
+            {"x": 2, "x_here": 4, "y": 5, "y_here": 8, "diagonal": 10},
+            False,
+        ),
+    )
+    send.finish()
+
+
+def start(own, vector, feed, query, key, value, swish, output):
+    rows, width = own.shape
+    small = (rows // 128, 128)
+    features, head, value_cols = 2 * query.shape[0], query.shape[1] // 2, value.shape[1] // 2
+    wide = jax.ShapeDtypeStruct((rows, width * 8), BF16)
+    count = 3 + 8 * 7 + 2 * GATHERS
+    wide_one, wide_feed, total, first_weight, out_weight = pl.pallas_call(
+        start_kernel,
+        out_shape=(
+            wide,
+            wide,
+            jax.ShapeDtypeStruct(small, F32),
+            jax.ShapeDtypeStruct((features, 2 * head + 2 * value_cols), BF16),
+            jax.ShapeDtypeStruct((output.shape[0] // 2, 2 * output.shape[1]), BF16),
+        ),
+        in_specs=vmem(3) + [anywhere()] * 5,
+        out_specs=tuple(vmem(3) + [anywhere()] * 2),
+        scratch_shapes=[
+            pltpu.VMEM((5,) + small, F32),
+            pltpu.VMEM((2, features // 2, head), BF16),
+            pltpu.VMEM((2, features // 2, value_cols), BF16),
+            pltpu.VMEM((output.shape[0] // 2, output.shape[1]), BF16),
+        ]
+        + dma(count, count, 10),
+        compiler_params=params(5),
+        name="start",
+    )(own, vector.reshape(small), feed, query, key, value, swish, output)
+    return wide_one, total.reshape(rows), wide_feed, first_weight, out_weight
+
+
+def middle_scatter_kernel(part_ref, gelu, up, out_ref, second_weight, bounce, *rest):
+    rows, (send_sem, recv_sem, load_sem, local_sem) = rest[:4], rest[4:]
+    send = Sender(send_sem, recv_sem)
+    prepare = block_loads(part_ref, rows[0], load_sem)
+    enter(plane_peers() + line_peers())
+    hidden_cols = gelu.shape[1] // 2
+    weights, bounces = [], []
+    for i, source in enumerate((gelu, up)):
+        for part in range(2):
+            weights.append(Weight(source, second_weight, "in", i * hidden_cols, part, 2))
+            size = source.shape[0] // 2
+            bounces.append(bounce.at[i, part * size : (part + 1) * size])
+    run(
+        weight_steps(weights, bounces, local_sem, send),
+        scatter_steps(prepare, *rows, send, out_ref),
+    )
+    send.finish()
+
+
+def middle_scatter(part, gelu, up):
+    rows, wide = part.shape
+    width, hidden_cols = wide // 8, gelu.shape[1] // 2
+    count = SCATTERS + 4 * 7
+    return pl.pallas_call(
+        middle_scatter_kernel,
+        out_shape=(
+            jax.ShapeDtypeStruct((rows, width), F32),
+            jax.ShapeDtypeStruct((2 * gelu.shape[0], 2 * hidden_cols), BF16),
+        ),
+        in_specs=[anywhere()] * 3,
+        out_specs=tuple(vmem(1) + [anywhere()]),
+        scratch_shapes=[pltpu.VMEM((2, gelu.shape[0], hidden_cols), BF16)]
+        + scatter_rows(rows, width)
+        + dma(count, count, 8, 4),
+        compiler_params=params(6),
+        name="middle_scatter",
+    )(part, gelu, up)
+
+
+def middle_gather_kernel(
+    own_ref, vec_ref, down, out_ref, total_ref, last_weight, got, bounce, send_sem, recv_sem, local_sem
+):
+    enter(plane_peers() + line_peers())
+    send = Sender(send_sem, recv_sem)
+    size = down.shape[0] // 4
+    run(
+        weight_steps(
+            [Weight(down, last_weight, "out", 0, part, 2) for part in range(2)],
+            [bounce.at[part * size : (part + 1) * size] for part in range(2)],
+            local_sem,
+            send,
+        ),
+        total_steps(vec_ref, total_ref, got, send),
+        gather_steps(own_ref, out_ref, send, local_sem.at[2]),
+    )
+    send.finish()
+
+
+def middle_gather(own, vector, down):
+    rows, width = own.shape
+    small = (rows // 128, 128)
+    count = 3 + GATHERS + 2 * 7
+    wide, total, last_weight = pl.pallas_call(
+        middle_gather_kernel,
+        out_shape=(
+            jax.ShapeDtypeStruct((rows, width * 8), own.dtype),
+            jax.ShapeDtypeStruct(small, F32),
+            jax.ShapeDtypeStruct((down.shape[0] // 2, 2 * down.shape[1]), BF16),
+        ),
+        in_specs=vmem(2) + [anywhere()],
+        out_specs=tuple(vmem(2) + [anywhere()]),
+        scratch_shapes=[
+            pltpu.VMEM((5,) + small, F32),
+            pltpu.VMEM((down.shape[0] // 2, down.shape[1]), BF16),
+        ]
+        + dma(count, count, 3),
+        compiler_params=params(7),
+        name="middle_gather",
+    )(own, vector.reshape(small), down)
+    return wide, total.reshape(rows), last_weight
 
 
 def vmem(count):
     return [pl.BlockSpec(memory_space=VM)] * count
 
 
-def params(number):
+def anywhere():
+    return pl.BlockSpec(memory_space=pl.ANY)
+
+
+def params(number, limit=44):
     return pltpu.CompilerParams(
-        collective_id=number, has_side_effects=True, vmem_limit_bytes=40 << 20
+        collective_id=number, has_side_effects=True, vmem_limit_bytes=limit << 20
     )
 
 
@@ -182,12 +653,9 @@
         out_shape=jax.ShapeDtypeStruct((rows, width * 8), own.dtype),
         in_specs=vmem(1),
         out_specs=vmem(1)[0],
-        scratch_shapes=[
-            pltpu.SemaphoreType.DMA((13,)),
-            pltpu.SemaphoreType.DMA((13,)),
-            pltpu.SemaphoreType.DMA(()),
-        ],
+        scratch_shapes=dma(GATHERS, GATHERS, 1),
         compiler_params=params(0),
+        name="gather",
     )(own)
 
 
@@ -202,101 +670,10 @@
         ),
         in_specs=vmem(2),
         out_specs=tuple(vmem(2)),
-        scratch_shapes=[
-            pltpu.VMEM((5,) + small, F32),
-            pltpu.SemaphoreType.DMA((16,)),
-            pltpu.SemaphoreType.DMA((16,)),
-            pltpu.SemaphoreType.DMA(()),
-        ],
+        scratch_shapes=[pltpu.VMEM((5,) + small, F32)] + dma(3 + GATHERS, 3 + GATHERS, 1),
         compiler_params=params(1),
     )(own, vector.reshape(small))
     return wide, total.reshape(rows)
-
-
-def scatter_body(part_ref, out_ref, stage, from_core, from_x, from_y, send, side):
-    rows, width = out_ref.shape
-    half = rows // 2
-    r, c, core, across = neighbours()
-    to_core, to_x, to_y = {"col": core}, {"col": across}, {"row": 1 - r}
-    places = (4 + across, across, 4 + c, c)
-    other = core - c
-
-    def cols(place):
-        return pl.ds(pl.multiple_of(place * width, width), width)
-
-    side_start = side(send, to_core, to_x, to_y)
-    first = [
-        send(part_ref.at[:, cols(places[i] + other)], from_core.at[i], to_core) for i in range(4)
-    ]
-    lo, hi = slice(0, half), slice(half, 2 * half)
-
-    def summed(i, part):
-        return part_ref[part, cols(places[i])].astype(F32) + from_core[i, part].astype(F32)
-
-    first[0].wait_recv()
-    next(side_start)
-    stage[0, lo] = summed(0, lo).astype(BF16)
-    dx = send(stage.at[0, lo], from_x.at[2], to_x)
-    stage[0, hi] = summed(0, hi).astype(BF16)
-    dy = send(stage.at[0, hi], from_y.at[2], to_y)
-    first[1].wait_recv()
-    stage[1, lo] = summed(1, lo).astype(BF16)
-    x0 = send(stage.at[1, lo], from_x.at[0], to_x)
-    first[2].wait_recv()
-    stage[2, hi] = summed(2, hi).astype(BF16)
-    y1 = send(stage.at[2, hi], from_y.at[1], to_y)
-    next(side_start)
-    dy.wait_recv()
-    stage[1, hi] = (summed(1, hi) + from_y[2].astype(F32)).astype(BF16)
-    x1 = send(stage.at[1, hi], from_x.at[1], to_x)
-    dx.wait_recv()
-    stage[2, lo] = (summed(2, lo) + from_x[2].astype(F32)).astype(BF16)
-    y0 = send(stage.at[2, lo], from_y.at[0], to_y)
-    next(side_start)
-    first[3].wait_recv()
-    x0.wait_recv()
-    y1.wait_recv()
-    out_ref[lo] = summed(3, lo) + from_x[0].astype(F32)
-    out_ref[hi] = summed(3, hi) + from_y[1].astype(F32)
-    x1.wait_recv()
-    out_ref[hi] = out_ref[hi] + from_x[1].astype(F32)
-    y0.wait_recv()
-    out_ref[lo] = out_ref[lo] + from_y[0].astype(F32)
-    for copy in send.started:
-        copy.wait_send()
-
-
-def scatter_kernel(part_ref, out_ref, stage, from_core, from_x, from_y, send_sem, recv_sem):
-    enter()
-    scatter_body(
-        part_ref, out_ref, stage, from_core, from_x, from_y, Sender(send_sem, recv_sem), no_side
-    )
-
-
-def scatter_total_kernel(
-    part_ref, vec_ref, out_ref, total_ref, stage, from_core, from_x, from_y, got, send_sem, recv_sem
-):
-    enter()
-    scatter_body(
-        part_ref,
-        out_ref,
-        stage,
-        from_core,
-        from_x,
-        from_y,
-        Sender(send_sem, recv_sem),
-        total_side(vec_ref, total_ref, got),
-    )
-
-
-def scatter_scratch(rows, width):
-    half = rows // 2
-    return [
-        pltpu.VMEM((3, rows, width), BF16),
-        pltpu.VMEM((4, rows, width), BF16),
-        pltpu.VMEM((3, half, width), BF16),
-        pltpu.VMEM((3, half, width), BF16),
-    ]
 
 
 def plane_scatter(part):
@@ -305,10 +682,9 @@
     return pl.pallas_call(
         scatter_kernel,
         out_shape=jax.ShapeDtypeStruct((rows, width), F32),
-        in_specs=vmem(1),
+        in_specs=[anywhere()],
         out_specs=vmem(1)[0],
-        scratch_shapes=scatter_scratch(rows, width)
-        + [pltpu.SemaphoreType.DMA((10,)), pltpu.SemaphoreType.DMA((10,))],
+        scratch_shapes=scatter_rows(rows, width) + dma(SCATTERS, SCATTERS, 8),
         compiler_params=params(2),
     )(part)
 
@@ -320,15 +696,13 @@
     out, total = pl.pallas_call(
         scatter_total_kernel,
         out_shape=(jax.ShapeDtypeStruct((rows, width), F32), jax.ShapeDtypeStruct(small, F32)),
-        in_specs=vmem(2),
+        in_specs=[anywhere()] + vmem(1),
         out_specs=tuple(vmem(2)),
-        scratch_shapes=scatter_scratch(rows, width)
-        + [
-            pltpu.VMEM((5,) + small, F32),
-            pltpu.SemaphoreType.DMA((13,)),
-            pltpu.SemaphoreType.DMA((13,)),
-        ],
+        scratch_shapes=[pltpu.VMEM((5,) + small, F32)]
+        + scatter_rows(rows, width)
+        + dma(3 + SCATTERS, 3 + SCATTERS, 8),
         compiler_params=params(3),
+        name="scatter",
     )(part, vector.reshape(small))
     return out, total.reshape(rows)
 
@@ -344,31 +718,34 @@
     return mine, theirs
 
 
-def swap_shared(values):
-    size = values.shape[0] // lax.axis_size("dp")
-    part = lax.dynamic_slice_in_dim(values, lax.axis_index("dp") * size, size, 0)
-    return lax.all_gather(swap_rows(part), "dp", axis=0, tiled=True)
+def whole_weight(values, axis, r):
+    mine, theirs = halves_of(values, axis, r)
+    return jnp.concatenate([mine, swap_rows(theirs)], axis=1 - axis)
 
 
 PIECE = 128
 GROUP = 8
-OUT_UNIT = 2
-UNITS = 6
+OUT_UNITS = (0, 3)
+UNITS = 7
 
 
 def last_kernel(
     wide_one,
     wide_two,
     wide_att,
+    wide_feed,
     gated,
+    product,
     both_low,
     weight,
+    feed_part,
     all_low,
     block_in,
     inner_vec,
     second_vec,
     result,
     back,
+    feed,
     inner_out,
     gains,
     part,
@@ -386,6 +763,7 @@
     gain_got,
     load_sem,
     local_sem,
+    free_sem,
     plane_send,
     plane_recv,
     gain_send,
@@ -393,37 +771,35 @@
     *line_sems,
 ):
     z, r, c = lax.axis_index("dp"), lax.axis_index("row"), lax.axis_index("col")
-    _, _, core, across = neighbours()
     barrier = pltpu.get_barrier_semaphore()
-    peers = [{"dp": lax.rem(z + k, 4)} for k in (1, 2, 3)]
-    peers += [{"row": 1 - r}, {"col": core}, {"col": across}]
+    peers = plane_peers() + line_peers()
     for target in peers:
         pl.semaphore_signal(barrier, inc=1, device_id=target, device_id_type=MESH)
     tokens, width = back.shape
-    half = tokens // 2
 
     def load(slot, src, dst):
         return pltpu.make_async_copy(src, dst, load_sem.at[slot])
 
     hidden_cols = small.shape[2]
     loads = [
-        load(0, wide_two, big.at[0]),
-        load(1, both_low.at[:, hidden_cols:], small.at[0]),
-        load(2, both_low.at[:, :hidden_cols], small.at[1]),
-        load(3, wide_att, big.at[1]),
-        load(4, gated, small.at[0]),
-        load(5, wide_one, big.at[0]),
+        load(0, wide_feed, big.at[0]),
+        load(1, product, small.at[0]),
+        load(2, wide_two, big.at[1]),
+        load(3, both_low.at[:, hidden_cols:], small.at[1]),
+        load(4, both_low.at[:, :hidden_cols], small.at[0]),
+        load(5, wide_att, big.at[0]),
+        load(6, gated, small.at[1]),
+        load(7, wide_one, big.at[1]),
     ]
     for i in range(4):
         loads[i].start()
 
-    places = (4 + across, across, 4 + c, c)
-    other = core - c
+    places = block_places()
+    feed_ready = block_loads(feed_part, rows_part, load_sem.at[10:18])
 
     def weight_load(i):
-        place = places[i % 4] + (other if i < 4 else 0)
-        rows = pl.ds(pl.multiple_of(place * width, width), width)
-        return load(6 + i % 2, weight.at[rows], stream.at[i % 2])
+        rows = pl.ds(pl.multiple_of(places[i] * width, width), width)
+        return load(8 + i % 2, weight.at[rows], stream.at[i % 2])
 
     weight_load(0).start()
     weight_load(1).start()
@@ -455,7 +831,7 @@
 
     def final(pair, slot):
         unit, place = pair // GROUP, lax.rem(pair, GROUP)
-        is_out = unit == OUT_UNIT
+        is_out = (unit == OUT_UNITS[0]) | (unit == OUT_UNITS[1])
         row = jnp.where(is_out, slot * 512 + (place // 2) * PIECE, place * PIECE)
         col = jnp.where(is_out, lax.rem(place, 2) * 512, slot * 512)
         return result.at[
@@ -498,7 +874,7 @@
             place = 2 * step + k
             pair = unit * GROUP + place
             for slot in range(2):
-                if unit == OUT_UNIT:
+                if unit in OUT_UNITS:
                     rows, cols = place // 2, lax.rem(place, 2) + 2 * slot
                 else:
                     rows, cols = place + GROUP * slot, shift
@@ -560,11 +936,8 @@
             lax.fori_loop(first, last, lambda q, carry: (step(q), carry)[1], 0)
 
     send = Sender(plane_send, plane_recv)
-    to_core, to_x, to_y = {"col": core}, {"col": across}, {"row": 1 - r}
-    lo, hi = slice(0, half), slice(half, 2 * half)
-    state = {}
-
-    def product(i):
+
+    def product_ready(i):
         weight_load(i).wait()
 
         def body(k, carry):
@@ -582,56 +955,24 @@
         if i < 6:
             weight_load(i + 2).start()
 
-    def summed(i, rows):
-        return rows_part[4 + i, rows].astype(F32) + rows_core[i, rows].astype(F32)
-
-    def phase_products():
-        state["side"] = total_side(inner_vec, inner_out, total_got)(send, to_core, to_x, to_y)
-        state["first"] = []
-        for i in range(4):
-            product(i)
-            state["first"].append(send(rows_part.at[i], rows_core.at[i], to_core))
-        next(state["side"])
-
-    def phase_first():
-        first = state["first"]
-        for i in range(4):
-            product(4 + i)
-        first[0].wait_recv()
-        rows_part[4, lo] = summed(0, lo).astype(BF16)
-        state["dx"] = send(rows_part.at[4, lo], rows_x.at[2], to_x)
-        rows_part[4, hi] = summed(0, hi).astype(BF16)
-        state["dy"] = send(rows_part.at[4, hi], rows_y.at[2], to_y)
-        first[1].wait_recv()
-        rows_part[5, lo] = summed(1, lo).astype(BF16)
-        state["x0"] = send(rows_part.at[5, lo], rows_x.at[0], to_x)
-        first[2].wait_recv()
-        rows_part[6, hi] = summed(2, hi).astype(BF16)
-        state["y1"] = send(rows_part.at[6, hi], rows_y.at[1], to_y)
-        next(state["side"])
-
-    def phase_second():
-        state["dy"].wait_recv()
-        rows_part[5, hi] = (summed(1, hi) + rows_y[2].astype(F32)).astype(BF16)
-        state["x1"] = send(rows_part.at[5, hi], rows_x.at[1], to_x)
-        state["dx"].wait_recv()
-        rows_part[6, lo] = (summed(2, lo) + rows_x[2].astype(F32)).astype(BF16)
-        state["y0"] = send(rows_part.at[6, lo], rows_y.at[0], to_y)
-        next(state["side"])
-
-    def phase_third():
-        state["first"][3].wait_recv()
-        state["x0"].wait_recv()
-        state["y1"].wait_recv()
-        state["x1"].wait_recv()
-        state["y0"].wait_recv()
-        back[lo] = summed(3, lo) + rows_x[0].astype(F32) + rows_y[0].astype(F32)
-        back[hi] = summed(3, hi) + rows_y[1].astype(F32) + rows_x[1].astype(F32)
+    def plane_steps():
+        yield from scatter_steps(feed_ready, rows_part, rows_core, rows_x, rows_y, send, feed)
+        send.finish()
+        for target in plane_peers():
+            pl.semaphore_signal(free_sem, inc=1, device_id=target, device_id_type=MESH)
+        yield
+        pl.semaphore_wait(free_sem, 3)
+        beside = total_steps(inner_vec, inner_out, total_got, send)
+        for _ in scatter_steps(product_ready, rows_part, rows_core, rows_x, rows_y, send, back):
+            next(beside, None)
+            yield
         first_gain = jnp.sum(back[...] * block_in[...].astype(F32), axis=0, keepdims=True)
         gain_own[0:1] = first_gain
         gain_own[1:2] = second_vec[...]
         for each in gain_copies:
             each.start()
+        yield
+        send.finish()
 
     gain_copies = [
         pltpu.make_async_remote_copy(
@@ -647,30 +988,33 @@
 
     loads[0].wait()
     loads[1].wait()
-    compute(0, big.at[0], small.at[0])
+    compute(0, small.at[0], big.at[0])
     loads[4].start()
-    phase_products()
-    run_steps(0, 1)
-    phase_first()
-    run_steps(1, 3)
-    loads[2].wait()
-    compute(1, big.at[0], small.at[1])
     loads[5].start()
-    run_steps(3, 4)
-    phase_second()
-    run_steps(4, 7)
-    loads[3].wait()
-    loads[4].wait()
-    compute(2, small.at[0], big.at[1])
-    phase_third()
-    run_steps(7, 11)
-    loads[5].wait()
-    compute(3, big.at[0], all_low, 0)
-    run_steps(11, 15)
-    compute(4, big.at[0], all_low, 1)
-    run_steps(15, 19)
-    compute(5, big.at[0], all_low, 2)
-    run_steps(19, steps + 3)
+    plane = plane_steps()
+    done = 0
+    later = {
+        4: (1, (2, 3), lambda: (big.at[1], small.at[1]), (6,)),
+        8: (2, (4,), lambda: (big.at[1], small.at[0]), (7,)),
+        12: (3, (5, 6), lambda: (small.at[1], big.at[0]), ()),
+        16: (4, (7,), lambda: (big.at[1], all_low, 0), ()),
+        20: (5, (), lambda: (big.at[1], all_low, 1), ()),
+        24: (6, (), lambda: (big.at[1], all_low, 2), ()),
+    }
+    while done < 28:
+        next(plane, None)
+        run_steps(done, done + 1)
+        done += 1
+        if done + 1 in later:
+            unit, before, arguments, after = later[done + 1]
+            for i in before:
+                loads[i].wait()
+            compute(unit, *arguments())
+            for i in after:
+                loads[i].start()
+    for _ in plane:
+        pass
+    run_steps(done, steps + 3)
 
     total = gain_own[...]
     for each in gain_copies:
@@ -679,8 +1023,6 @@
         gain_copies[k].wait_recv()
         total = total + gain_got[k]
     gains[...] = total
-    for each in send.started:
-        each.wait_send()
 
     @pl.when(is_inner)
     def _():
@@ -713,13 +1055,26 @@
         lax.fori_loop(0, steps, body, 0)
 
 
-def last_scatter(wide_one, wide_two, wide_att, gated, both_low, weight, all_low, own, inner, second):
+def last_scatter(
+    wide_one,
+    wide_two,
+    wide_att,
+    wide_feed,
+    gated,
+    product,
+    both_low,
+    weight,
+    feed_part,
+    all_low,
+    own,
+    inner,
+    second,
+):
     tokens, width = own.shape
     small = (tokens // 128, 128)
     pairs = UNITS * GROUP
     steps = pairs // 2
     shape = (pairs, 2, PIECE, 512)
-    half = tokens // 2
     gain_shape = (8, width)
     scratch = [
         pltpu.VMEM(shape, BF16),
@@ -728,51 +1083,46 @@
         pltpu.VMEM((2,) + wide_one.shape, BF16),
         pltpu.VMEM((2,) + gated.shape, BF16),
         pltpu.VMEM((2, width, weight.shape[1]), BF16),
-        pltpu.VMEM((8, tokens, width), BF16),
-        pltpu.VMEM((4, tokens, width), BF16),
-        pltpu.VMEM((3, half, width), BF16),
-        pltpu.VMEM((3, half, width), BF16),
+        *scatter_rows(tokens, width),
         pltpu.VMEM((5,) + small, F32),
         pltpu.VMEM(gain_shape, F32),
         pltpu.VMEM((3,) + gain_shape, F32),
-        pltpu.SemaphoreType.DMA((8,)),
-        pltpu.SemaphoreType.DMA((steps,)),
-        pltpu.SemaphoreType.DMA((13,)),
-        pltpu.SemaphoreType.DMA((13,)),
-        pltpu.SemaphoreType.DMA((3,)),
-        pltpu.SemaphoreType.DMA((3,)),
+        *dma(18, steps),
+        pltpu.SemaphoreType.REGULAR,
+        *dma(2 * SCATTERS + 3, 2 * SCATTERS + 3, 3, 3),
     ]
     for size in (pairs,) + (steps,) * 8:
-        scratch += [pltpu.SemaphoreType.DMA((size,))] * 2
-    anywhere = pl.BlockSpec(memory_space=pl.ANY)
-    result, back, total, gains = pl.pallas_call(
+        scratch += dma(size, size)
+    result, back, feed, total, gains = pl.pallas_call(
         last_kernel,
         out_shape=(
             jax.ShapeDtypeStruct((UNITS, 1024, 1024), BF16),
             jax.ShapeDtypeStruct((tokens, width), F32),
+            jax.ShapeDtypeStruct((tokens, width), F32),
             jax.ShapeDtypeStruct(small, F32),
             jax.ShapeDtypeStruct(gain_shape, F32),
         ),
-        in_specs=[anywhere] * 6 + vmem(4),
-        out_specs=(anywhere,) + tuple(vmem(3)),
+        in_specs=[anywhere()] * 9 + vmem(4),
+        out_specs=tuple([anywhere()] + vmem(4)),
         scratch_shapes=scratch,
-        compiler_params=pltpu.CompilerParams(
-            collective_id=4, has_side_effects=True, vmem_limit_bytes=62 << 20
-        ),
+        compiler_params=params(4, 62),
         name="last_scatter",
     )(
         wide_one,
         wide_two,
         wide_att,
+        wide_feed,
         gated,
+        product,
         both_low,
         weight,
+        feed_part,
         all_low,
         own,
         inner.reshape(small),
         second.reshape(1, width),
     )
-    return result, back, total.reshape(tokens), gains[0], gains[1]
+    return result, back, feed, total.reshape(tokens), gains[0], gains[1]
 
 
 def place_halves(mine, theirs, axis, r):
@@ -891,36 +1241,40 @@
     log_decay = jnp.log(1.0 - 2.0 ** (-5.0 - head_index.astype(jnp.float32)))
     cosine_table, sine_table = rotary_tables(tokens, KD)
 
-    heads = [halves_of(w, 1, r) for w in (query_weight, key_weight, value_weight, swish_weight)]
-    first_mine = jnp.concatenate([mine for mine, _ in heads], axis=1)
-    first_theirs = jnp.concatenate(
-        [swap_shared(jnp.concatenate([theirs for _, theirs in heads[:3]], axis=1)), swap_rows(heads[3][1])],
-        axis=1,
-    )
-    units = [halves_of(gelu_weight, 1, r), halves_of(up_weight, 1, r)]
-    ends = [halves_of(output_weight, 0, r), halves_of(down_weight, 0, r)]
-    value_cols = ends[0][0].shape[0]
-    hidden_cols = ends[1][0].shape[0]
-    rest = swap_shared(
-        jnp.concatenate(
-            [units[0][1], units[1][1], jnp.concatenate([ends[0][1], ends[1][1]], axis=0)], axis=1
-        )
-    )
-    second_mine = jnp.concatenate([units[0][0], units[1][0]], axis=1)
-    second_theirs = rest[:, : 2 * hidden_cols]
-    out_weight = jnp.concatenate([ends[0][0], rest[:value_cols, 2 * hidden_cols :]], axis=1)
-    last_weight = jnp.concatenate([ends[1][0], rest[value_cols:, 2 * hidden_cols :]], axis=1)
-    first_weight = jnp.concatenate([first_mine, first_theirs], axis=0)
-    second_weight = jnp.concatenate([second_mine, second_theirs], axis=0)
-
-    wide_one, square_one = plane_gather_total(
-        (hidden * first_gain).astype(BF16), jnp.sum(hidden * hidden, axis=1)
-    )
+    value_cols = value_weight.shape[1] // 2
+    hidden_cols = gelu_weight.shape[1] // 2
+    line = lax.axis_size("dp") == 4
+    if not line:
+        first_weight = jnp.concatenate(
+            [
+                whole_weight(weight, 1, r)
+                for weight in (query_weight, key_weight, value_weight, swish_weight)
+            ],
+            axis=1,
+        )
+        out_weight = whole_weight(output_weight, 0, r)
+        second_weight = jnp.concatenate(
+            [whole_weight(gelu_weight, 1, r), whole_weight(up_weight, 1, r)], axis=1
+        )
+        last_weight = whole_weight(down_weight, 0, r)
+
+    own_one, own_square = (hidden * first_gain).astype(BF16), jnp.sum(hidden * hidden, axis=1)
+    if line:
+        wide_one, square_one, wide_feed_grad, first_weight, out_weight = start(
+            own_one,
+            own_square,
+            block_cotangent[0],
+            query_weight,
+            key_weight,
+            value_weight,
+            swish_weight,
+            output_weight,
+        )
+    else:
+        wide_one, square_one = plane_gather_total(own_one, own_square)
+        wide_feed_grad = plane_gather(block_cotangent[0])
     scale_one = lax.rsqrt(square_one / features + epsilon)[:, None]
-    split = first_mine.shape[0]
-    sums_one = (
-        matmul(wide_one[:, :split], first_mine) + matmul(wide_one[:, split:], first_theirs)
-    ) * scale_one
+    sums_one = matmul(wide_one, first_weight) * scale_one
     query_sum = sums_one[:, :KD]
     key_sum = sums_one[:, KD : 2 * KD]
     value_sum = sums_one[:, 2 * KD : 2 * KD + value_cols]
@@ -936,20 +1290,26 @@
     grouped, group_pull = jax.vjp(group_norm, retained)
     gated_full, swish_pull = jax.vjp(swish_gate, swish_sum, grouped)
     gated = gated_full.astype(jnp.bfloat16)
-    middle = hidden + plane_scatter(matmul(gated, out_weight).astype(BF16))
-
-    wide_two, square_two = plane_gather_total(
-        (middle * second_gain).astype(BF16), jnp.sum(middle * middle, axis=1)
-    )
+    attended = matmul(gated, out_weight).astype(BF16)
+    if line:
+        attended, second_weight = middle_scatter(attended, gelu_weight, up_weight)
+    else:
+        attended = plane_scatter(attended)
+    middle = hidden + attended
+
+    own_two, own_square = (middle * second_gain).astype(BF16), jnp.sum(middle * middle, axis=1)
+    if line:
+        wide_two, square_two, last_weight = middle_gather(own_two, own_square, down_weight)
+    else:
+        wide_two, square_two = plane_gather_total(own_two, own_square)
     scale_two = lax.rsqrt(square_two / features + epsilon)[:, None]
     sums_two = matmul(wide_two, second_weight) * scale_two
     gelu_sum, up_sum = sums_two[:, :hidden_cols], sums_two[:, hidden_cols:]
     product_full, gelu_pull = jax.vjp(gelu_gate, gelu_sum, up_sum)
     product = product_full.astype(jnp.bfloat16)
-    block_out = (middle + plane_scatter(matmul(product, last_weight).astype(BF16))).astype(BF16)
+    feed_part = matmul(product, last_weight).astype(BF16)
 
     upstream = block_cotangent[0].astype(jnp.float32)
-    wide_feed_grad = plane_gather(block_cotangent[0])
     product_grad = back_product(wide_feed_grad, last_weight)
     gelu_grad, up_grad = gelu_pull(product_grad)
     both_grad = jnp.concatenate([gelu_grad, up_grad], axis=1)
@@ -977,30 +1337,33 @@
     inner_one = jnp.sum(all_grad * sums_one, axis=1)
     all_low = (all_grad * scale_one).astype(BF16)
     own_second = jnp.sum(normed_two_grad * middle, axis=0)
-    if lax.axis_size("dp") == 4:
-        (grad_down,) = sum_packs(((weight_grad(product, wide_feed_grad), 0),))
-        result, normed_one_grad, inner_one, grad_first, grad_second = last_scatter(
+    if line:
+        result, normed_one_grad, feed, inner_one, grad_first, grad_second = last_scatter(
             wide_one,
             wide_two,
             wide_attended_grad,
+            wide_feed_grad,
             gated,
+            product,
             both_low,
             first_weight,
+            feed_part,
             all_low,
             block_in[0],
             inner_one,
             own_second,
         )
-        grad_up, grad_gelu, grad_output = [result[i].astype(F32) for i in range(3)]
+        grad_down, grad_up, grad_gelu, grad_output = [result[i].astype(F32) for i in range(4)]
         starts = (0, 2 * KD)
         grad_query, grad_key = [
             jnp.concatenate(
-                [result[3, :, side + shift : side + shift + KD] for side in starts], axis=1
+                [result[4, :, side + shift : side + shift + KD] for side in starts], axis=1
             ).astype(F32)
             for shift in (0, KD)
         ]
-        grad_value, grad_swish = result[4].astype(F32), result[5].astype(F32)
+        grad_value, grad_swish = result[5].astype(F32), result[6].astype(F32)
     else:
+        feed = plane_scatter(feed_part)
         normed_one_grad, inner_one = plane_scatter_total(
             back_product(all_low, first_weight).astype(BF16), inner_one
         )
@@ -1029,6 +1392,7 @@
                 (weight_grad(product, wide_feed_grad), 0),
             )
         )
+    block_out = (middle + feed).astype(BF16)
     grad_input = (
         middle_grad
         + first_gain * normed_one_grad

time: 745 us -> 667 us (0.90)
  Pallas kernels: 520 us -> 568 us
  waiting for transfers between devices: 41.1 us -> 0 us
  other arithmetic: 57.9 us -> 31.2 us
  local copies, waits for them, and re-layouts: 40.8 us -> 16.8 us
  between operations: 15.3 us -> 1.51 us
  matrix products: 57.9 us -> 46.7 us
    pallas_call x4 -> x3, Pallas kernels: 88 us -> 158 us  [the longest x1 84.8 us: start(): pl.pallas_call(start_kernel, out_shape=(wide, wide, jax.ShapeDtypeStruct(...]
    ppermute x4 -> x0, waiting for transfers between devices: 41.1 us -> none  [swap_rows(): return lax.ppermute(values, 'row', [(0, 1), (1, 0)])]
    pallas_call x2 -> x1, Pallas kernels: 59.9 us -> 21.7 us  [plane_gather(): pl.pallas_call(gather_kernel, out_shape=jax.ShapeDtypeStruct((rows, width...]
    concatenate x3 -> x0, other arithmetic: 26 us -> none  [the longest x1 23.6 us: shards(): first_weight = jnp.concatenate([first_mine, first_theirs], axis=0)]
    pallas_call x1, Pallas kernels: 349 us -> 363 us  [last_scatter(): pl.pallas_call(last_kernel, out_shape=(jax.ShapeDtypeStruct((UNITS, 1024,...]
    dynamic_slice x5 -> x0, local copies, waits for them, and re-layouts: 10.9 us -> none  [the longest x2 5.64 us: halves_of(): mine = lax.dynamic_slice_in_dim(values, r * size, size, axis)]
    unnamed x165 -> x72, local copies, waits for them, and re-layouts: 20.7 us -> 12.2 us
    convert_element_type x4 -> x3, other arithmetic: 18 us -> 11.8 us  [the longest x1 8.63 us: shards(): result[i].astype(F32)]
  transfers between devices with their start and end apart: 7 -> 0, of which waited for: 3 -> 0; matrix products, arithmetic and copies ran while one was open for 11% -> 0% of each run, Pallas kernels for 59% -> 0%
where the time goes in v3:
time: 667 us; the launch traced here: 664 us
  Pallas kernels  568 us (85%)
  matrix products  46.7 us (7%)
  other arithmetic  31.2 us (5%)
  local copies, waits for them, and re-layouts  16.8 us (3%)
    pallas_call x1, Pallas kernels, last_scatter(): pl.pallas_call(last_kernel, out_shape=(jax.ShapeDtypeStruct((UNITS, 1024,...  363 us
    pallas_call x1, Pallas kernels, start(): pl.pallas_call(start_kernel, out_shape=(wide, wide, jax.ShapeDtypeStruct(...  84.8 us
    pallas_call x1, Pallas kernels, middle_scatter(): pl.pallas_call(middle_scatter_kernel, out_shape=(jax.ShapeDtypeStruct((ro...  44.7 us
    pallas_call x1, Pallas kernels, middle_gather(): pl.pallas_call(middle_gather_kernel, out_shape=(jax.ShapeDtypeStruct((row...  28.5 us
    dot_general x8, matrix products, matmul(): return jnp.dot(left, right, preferred_element_type=jnp.float32)  25.1 us
    pallas_call x1, Pallas kernels, plane_scatter_total(): pl.pallas_call(scatter_total_kernel, out_shape=(jax.ShapeDtypeStruct((row...  24.7 us
    pallas_call x1, Pallas kernels, plane_gather(): pl.pallas_call(gather_kernel, out_shape=jax.ShapeDtypeStruct((rows, width...  21.7 us
    dot_general x3, matrix products, back_product(): jnp.einsum('tf,kf->tk', grads, weights, preferred_element_type=jnp.float32)  16.3 us

profile of v3, /device:TPU:0, one launch (start us, length us, event | category | flops | bytes accessed | tf_op | source)
XLA Modules:
  0.0 663.7 jit_solution(12461478590431975966)
XLA Ops:
  0.8 0.8 fusion.65
  1.6 1.3 fusion.18
  2.8 1.9 fusion.42
  4.8 1.8 copy-done.5
  6.6 1.6 copy-done.6
  8.2 1.2 copy-done.10
  9.4 84.8 %start.1 = (bf16[1024,2048]{1,0:T(8,128)(2,1)}, bf16[1024,2048]{1,0:T(8,128)(2,1)}, f32[8,128]{1,0:T(8,128)S(1)}, bf16[2048,1536]{1,0:T(8,128)(2,1)}, bf16[512,2048]{1,0:T(8,128)(2,1)S(1)}) custom-call(bf16[1024,256]{1,0:T(8,128)(2,1)S(1)} %get-tuple-element.148.own_ref, f32[8,128]{1,0:T(8,128)S(1)} %bitcast.104, bf16[1024,256]{1,0:T(8,128)(2,1)S(1)} %bitcast.103, ...), custom_call_target="tpu_custom_call" | custom-call | tf_op jit(solution)/shard_map/start/pallas_call | solution.py:529
  94.3 10.0 %fusion.66 = (bf16[1024,1536]{1,0:T(8,128)(2,1)S(1)}, f32[1024,1536]{1,0:T(8,128)S(1)}) fusion(f32[1024]{0:T(1024)S(1)} %rsqrt_bitcast_fusion.1, bf16[1024,2048]{1,0:T(8,128)(2,1)} %get-tuple-element.93.wide_one, bf16[2048,1536]{1,0:T(8,128)(2,1)} %get-tuple-element.94.weight), kind=kOutput, calls=%fused_computation.143 | convolution fusion | flops 6445596672 | bytes 19927040 | tf_op jit(solution)/shard_map/dot_general | solution.py:1147
  104.3 0.1 slice_negate_fusion.2
  104.5 0.5 fusion.25
  105.0 0.0 copy-start.33
  105.0 0.4 fusion.13
  105.5 0.0 copy-start.22
  105.5 0.4 fusion.50
  105.9 0.3 copy-done.20
  106.3 0.2 copy-done.24
  106.5 1.0 multiply_convert_fusion.5
  107.5 0.0 copy-start.27
  107.5 1.3 copy-done.27
  108.8 0.7 fusion.34
  109.5 0.2 multiply_reduce_fusion.3
  109.8 0.7 multiply_convert_fusion.4.gated
  110.5 1.0 copy-done.18
  111.5 4.4 convolution_convert_fusion.1.part_ref
  115.8 44.7 %middle_scatter.1 = (f32[1024,256]{1,0:T(8,128)S(1)}, bf16[2048,1024]{1,0:T(8,128)(2,1)S(1)}) custom-call(bf16[1024,2048]{1,0:T(8,128)(2,1)} %convolution_convert_fusion.1.part_ref, bf16[1024,1024]{1,0:T(8,128)(2,1)S(1)} %copy-done.7, bf16[1024,1024]{1,0:T(8,128)(2,1)S(1)} %copy-done.8), custom_call_target="tpu_custom_call" | custom-call | tf_op jit(solution)/shard_map/middle_scatter/pallas_call | solution.py:576
  160.5 0.3 multiply_reduce_fusion.5
  160.8 1.3 copy-done.4
  162.1 28.5 %middle_gather.1 = (bf16[1024,2048]{1,0:T(8,128)(2,1)S(1)}, f32[8,128]{1,0:T(8,128)S(1)}, bf16[512,2048]{1,0:T(8,128)(2,1)S(1)}) custom-call(bf16[1024,256]{1,0:T(8,128)(2,1)S(1)} %get-tuple-element.140.own_ref, f32[8,128]{1,0:T(8,128)S(1)} %bitcast.106, bf16[1024,1024]{1,0:T(8,128)(2,1)S(1)} %copy-done.4), custom_call_target="tpu_custom_call" | custom-call | tf_op jit(solution)/shard_map/middle_gather/pallas_call | solution.py:615
  190.7 4.5 convolution_multiply_fusion.1
  195.3 5.4 fusion.5
  200.7 3.5 multiply_reduce_fusion.1
  204.2 1.3 copy-done.14
  205.6 4.8 convolution_convert_fusion.2.part_ref
  210.3 24.7 %scatter.1 = (f32[1024,256]{1,0:T(8,128)S(1)}, f32[8,128]{1,0:T(8,128)S(1)}) custom-call(bf16[1024,2048]{1,0:T(8,128)(2,1)S(1)} %convolution_convert_fusion.2.part_ref, f32[8,128]{1,0:T(8,128)S(1)} %bitcast.105), custom_call_target="tpu_custom_call" | custom-call | tf_op jit(solution)/shard_map/scatter/pallas_call | solution.py:696
  235.1 0.9 multiply_reduce_fusion.4
  236.0 0.0 copy-done.2
  236.0 0.6 copy-done.26
  236.7 4.4 convolution_convert_fusion.feed_part
  241.0 21.7 %gather.1.wide_att = bf16[1024,2048]{1,0:T(8,128)(2,1)S(1)} custom-call(bf16[1024,256]{1,0:T(8,128)(2,1)S(1)} %get-tuple-element.136.own_ref), custom_call_target="tpu_custom_call" | custom-call | tf_op jit(solution)/shard_map/gather/pallas_call | solution.py:651
  262.8 6.1 multiply_reduce_fusion.2
  268.9 1.9 fusion.6
  270.8 0.6 fusion.14
  271.4 1.2 multiply_convert_fusion.2
  272.7 0.4 fusion.67
  273.1 0.3 fusion.54
  273.4 0.3 copy-done.25
  273.7 0.3 fusion.57
  274.1 0.5 fusion.12
  274.5 0.2 copy-done.23
  274.7 0.5 fusion.46
  275.2 0.1 copy-done.28
  275.3 0.7 pad_add_fusion
  276.1 0.1 fusion.40
  276.2 0.9 copy-done.16
  277.1 0.4 fusion.16
  277.5 3.0 multiply_reduce_fusion
  280.5 363.1 %last_scatter.1 = (bf16[7,1024,1024]{2,1,0:T(8,128)(2,1)}, f32[1024,256]{1,0:T(8,128)}, f32[1024,256]{1,0:T(8,128)}, f32[8,128]{1,0:T(8,128)}, f32[8,256]{1,0:T(8,128)}) custom-call(bf16[1024,2048]{1,0:T(8,128)(2,1)} %get-tuple-element.93.wide_one, bf16[1024,2048]{1,0:T(8,128)(2,1)} %copy-done.3, bf16[1024,2048]{1,0:T(8,128)(2,1)} %copy-done, ...), custom_call_target="tpu_custom_call" | custom-call | tf_op jit(solution)/shard_map/last_scatter/pallas_call | solution.py:1096
  643.6 0.7 fusion.60
  644.3 3.7 fusion.38
  648.0 2.0 fusion.64
  650.0 1.7 slice_bitcast_fusion.1
  651.7 1.6 maximum_convert_fusion.1
  653.3 1.6 maximum_convert_fusion
  654.9 8.6 %bitcast_convert_fusion = (f32[1024,1024]{1,0:T(8,128)}, f32[1024,1024]{1,0:T(8,128)}, f32[1024,1024]{1,0:T(8,128)}, f32[1024,1024]{1,0:T(8,128)}, f32[1024,1024]{1,0:T(8,128)}, /*index=5*/f32[1024,1024]{1,0:T(8,128)}) fusion(bf16[7,1024,1024]{2,1,0:T(8,128)(2,1)S(1)} %copy-done.12), kind=kLoop, calls=%fused_computation.25 | loop fusion | flops 6291456 | bytes 37748736 | tf_op jit(solution)/shard_map/convert_element_type | solution.py:1356
  (62 shorter events, 0.2 us)
Async XLA Ops:
  0.6 4.2 copy-start.1
  0.7 4.2 copy-start.9
  4.8 99.7 %copy-start.15 = (f32[1024,128]{1,0:T(8,128)}, f32[1024,128]{1,0:T(8,128)S(1)}, u32[]{:S(2)}) copy-start(f32[1024,128]{1,0:T(8,128)S(1)} %get-tuple-element.156) | copy-start | bytes 1572868
  4.8 1.8 copy-start.5
  6.6 1.6 copy-start.6
  8.2 1.2 copy-start.10
  104.3 3.2 copy-start.29
  104.3 5.5 copy-start.11
  105.0 1.3 copy-start.20
  105.0 1.5 copy-start.24
  105.0 1.5 copy-start.33
  105.5 2.1 copy-start.22
  107.5 1.3 copy-start.27
  110.5 1.0 copy-start.18
  111.5 4.4 copy-start.7
  111.5 4.4 copy-start.8
  115.8 44.7 %copy-start.13 = (bf16[1,1024,256]{2,1,0:T(8,128)(2,1)S(1)}, bf16[1,1024,256]{2,1,0:T(8,128)(2,1)}, u32[]{:S(2)}) copy-start(bf16[1,1024,256]{2,1,0:T(8,128)(2,1)} %param.25) | copy-start | bytes 1572868
  115.8 44.7 %copy-start.31 = (f32[256]{0:T(256)S(1)}, f32[256]{0:T(256)}, u32[]{:S(2)}) copy-start(f32[256]{0:T(256)} %param.37) | copy-start | bytes 3076
  160.5 1.6 copy-start.4
  190.7 4.6 copy-start.3
  190.7 4.6 copy-start.19
  195.3 5.5 copy-start.17
  204.2 1.3 copy-start.14
  235.0 1.0 copy-start.2
  235.1 1.6 copy-start.26
  241.0 27.9 %slice-start = ((s8[6291456]{0:T(1024)(128)(4,1)}), s8[2097152]{0:T(1024)(128)(4,1)S(1)}, s32[]{:S(2)}) async-start(s8[6291456]{0:T(1024)(128)(4,1)} %bitcast.107), calls=%async_computation | async-start | bytes 4194304
  262.7 6.1 copy-start
  262.8 6.1 slice-start.1
  268.9 1.9 copy-start.30
  271.4 1.2 copy-start.21
  272.7 1.0 copy-start.25
  273.7 1.0 copy-start.23
  274.0 1.3 copy-start.28
  276.0 1.0 copy-start.16
  280.5 363.8 %copy-start.32 = (f32[256]{0:T(256)S(1)}, f32[256]{0:T(256)}, u32[]{:S(2)}) copy-start(f32[256]{0:T(256)} %param.36) | copy-start | bytes 3076
  644.3 10.6 %copy-start.12 = (bf16[7,1024,1024]{2,1,0:T(8,128)(2,1)S(1)}, bf16[7,1024,1024]{2,1,0:T(8,128)(2,1)}, u32[]{:S(2)}) copy-start(bf16[7,1024,1024]{2,1,0:T(8,128)(2,1)} %get-tuple-element.108) | copy-start | bytes 44040196
